TPU v7x, 32 devices: a whole 2x2x4 slice. The times are simulated.
32 devices in a mesh: layer: 4 (over x, core), tok: 8 (over z, y).
Axes of the slice: x: 2, y: 2, z: 4, core: 2. Of those that a mesh axis runs over, the one named last changes fastest.
Arguments:
- kv_cache: bfloat16 [4, 2, 2, 1, 1024, 1024], P('layer', None, None, None, 'tok'), may hold values from -6 to 6
- keep_mask: int32 [4, 1, 1024], P('layer', None, 'tok'), may hold values 0 or 1
- lengths: int32 [1], replicated, may hold values from 256 to 1024
Outputs:
- decode_cache: bfloat16 [1, 8, 8, 2, 1024, 128], P(None, 'layer', None, None, 'tok')
Inputs may be any that keep to these rules, and one draw needn't show every extreme that they name: `keep_mask`: 1 keeps the token of both layers of the pair unmerged. `lengths`: positions at or past a sequence's length are padding.
All inputs are finite; a program needn't handle non-finite values. No bound on the sum of `keep_mask` on one device may be relied on, other than what follows from the above.
Results may differ from a plain program's by a relative error of at most 0.001.
Values may be sent and summed in bfloat16 or wider, within the bound.
No kernel may reach another device: no remote copies, remote signals or barrier semaphores. Data moves between devices by JAX's collectives and lax.ppermute only.
A program may use at most 64 MiB of HBM per device.

v0:
```python
import functools

import jax
import jax.numpy as jnp
from jax import lax
from jax.experimental import pallas as pl
from jax.experimental.pallas import tpu as pltpu
from jax.sharding import PartitionSpec as P


KVH = 8
HD = 128
PAGE = 16


epsilon = 1e-06

VMEM_GRANT = 16 * 2**20


def merge(lower, upper, retained, live):
    lower_square = jnp.mean(lower * lower, axis=-1, keepdims=True) + epsilon
    upper_square = jnp.mean(upper * upper, axis=-1, keepdims=True) + epsilon
    lower_inverse = lax.rsqrt(lower_square)
    upper_inverse = lax.rsqrt(upper_square)
    summed = lower * lower_inverse + upper * upper_inverse
    summed_inverse = lax.rsqrt(jnp.mean(summed * summed, axis=-1, keepdims=True) + epsilon)
    direction = summed * (summed_inverse * live)
    lower_out = jnp.where(retained, lower, (lower_square * lower_inverse) * direction)
    upper_out = jnp.where(retained, upper, (upper_square * upper_inverse) * direction)
    return lower_out.astype(jnp.bfloat16), upper_out.astype(jnp.bfloat16)


def merge_kernel(length_ref, keep_ref, values_ref, *rest, plan, groups, tok_count, rounds):
    outs, (loaded, mask, columns, sems, mask_sem) = rest[: len(plan)], rest[len(plan) :]
    layer, tok = lax.axis_index("layer"), lax.axis_index("tok")
    rows_dev = values_ref.shape[2]
    head_group = KVH // groups
    width = head_group * HD
    offsets = sorted({k for entry in plan for _, k in entry})
    run = rounds * PAGE

    def copies(j):
        lanes = pl.ds(pl.multiple_of((layer ^ j) * width, width), width)
        for n, k in enumerate(offsets):
            for r in range(rounds):
                source = pl.ds(pl.multiple_of((r * tok_count + (tok ^ k)) * PAGE, PAGE), PAGE)
                target = pl.ds(n * run + r * PAGE, PAGE)
                yield pltpu.make_async_copy(
                    values_ref.at[:, :, source, lanes], loaded.at[j, :, :, target, :], sems.at[j, n, r]
                )

    mask_copy = pltpu.make_async_copy(keep_ref, mask, mask_sem)
    mask_copy.start()
    for j in range(groups):
        for copy in copies(j):
            copy.start()
    mask_copy.wait()
    for block in range(0, rows_dev, HD):
        keep = (mask[:, block : block + HD] > 0).astype(jnp.float32)
        columns[block : block + HD, :] = jnp.broadcast_to(keep, (HD, HD)).T
    row = lax.broadcasted_iota(jnp.int32, (PAGE, HD), 0)
    retained, live = [], []
    for k in offsets:
        for r in range(rounds):
            start = pl.multiple_of((r * tok_count + (tok ^ k)) * PAGE, PAGE)
            inside = (row + (tok * rows_dev + start)) < length_ref[0]
            live.append(inside.astype(jnp.float32))
            kept = columns[pl.ds(start, PAGE), :]
            retained.append(kept * live[-1])
    retained = jnp.concatenate(retained, axis=0) > 0.0
    live = jnp.concatenate(live, axis=0)
    where = {}
    for o, entry in enumerate(plan):
        for n, piece in enumerate(entry):
            where[piece] = (o, n)
    for j in range(groups):
        for copy in copies(j):
            copy.wait()
        for c in range(2):
            for member in range(head_group):
                lanes = slice(member * HD, (member + 1) * HD)
                both = merge(
                    loaded[j, 0, c, :, lanes].astype(jnp.float32),
                    loaded[j, 1, c, :, lanes].astype(jnp.float32),
                    retained,
                    live,
                )
                for side in range(2):
                    for n, k in enumerate(offsets):
                        o, slot = where[(j, k)]
                        outs[o][slot, :, member, side, c] = both[side][n * run : (n + 1) * run].reshape(rounds, PAGE, HD)


def merged(values, keep, lengths, plan, groups, tok_count):
    rows_dev = values.shape[2]
    rounds = rows_dev // (PAGE * tok_count)
    head_group = KVH // groups
    count = len({k for entry in plan for _, k in entry})
    return pl.pallas_call(
        functools.partial(merge_kernel, plan=plan, groups=groups, tok_count=tok_count, rounds=rounds),
        in_specs=[
            pl.BlockSpec(memory_space=pltpu.SMEM),
            pl.BlockSpec(memory_space=pltpu.HBM),
            pl.BlockSpec(memory_space=pltpu.HBM),
        ],
        out_specs=[pl.BlockSpec(memory_space=pltpu.VMEM) for _ in plan],
        out_shape=[
            jax.ShapeDtypeStruct((len(entry), rounds, head_group, 2, 2, PAGE, HD), jnp.bfloat16)
            for entry in plan
        ],
        scratch_shapes=[
            pltpu.VMEM((groups, 2, 2, count * rounds * PAGE, head_group * HD), jnp.bfloat16),
            pltpu.VMEM((1, rows_dev), jnp.int32),
            pltpu.VMEM((rows_dev, HD), jnp.float32),
            pltpu.SemaphoreType.DMA((groups, count, rounds)),
            pltpu.SemaphoreType.DMA(()),
        ],
        compiler_params=pltpu.CompilerParams(vmem_limit_bytes=VMEM_GRANT),
    )(lengths, *[pltpu.with_memory_space_constraint(array, pltpu.HBM) for array in (keep, values)])


def place_kernel(*rest, plan, rounds, chained):
    pieces = rest[: len(plan)]
    out_ref, sems = rest[len(plan) + chained :]
    layer, tok = lax.axis_index("layer"), lax.axis_index("tok")

    def copies():
        n = 0
        for piece_ref, entry in zip(pieces, plan):
            for slot, (j, k) in enumerate(entry):
                for r in range(rounds):
                    pair = pl.ds((layer ^ j) * 2, 2)
                    rows = pl.ds(pl.multiple_of(((tok ^ k) * rounds + r) * PAGE, PAGE), PAGE)
                    yield pltpu.make_async_copy(
                        piece_ref.at[slot, r], out_ref.at[:, pair, :, rows, :], sems.at[n]
                    )
                    n += 1

    for copy in copies():
        copy.start()
    for copy in copies():
        copy.wait()


def placed(pieces, groups, rows_dev, before=None):
    arrays, plan = [array for array, _ in pieces], [entry for _, entry in pieces]
    rounds, head_group = arrays[0].shape[1], arrays[0].shape[2]
    count = sum(len(entry) for entry in plan) * rounds
    chained = before is not None
    return pl.pallas_call(
        functools.partial(place_kernel, plan=plan, rounds=rounds, chained=int(chained)),
        in_specs=[pl.BlockSpec(memory_space=pltpu.VMEM) for _ in arrays]
        + [pl.BlockSpec(memory_space=pltpu.HBM)] * chained,
        out_specs=pl.BlockSpec(memory_space=pltpu.HBM),
        out_shape=jax.ShapeDtypeStruct((head_group, 2 * groups, 2, rows_dev, HD), jnp.bfloat16),
        scratch_shapes=[pltpu.SemaphoreType.DMA((count,))],
        input_output_aliases={len(arrays): 0} if chained else {},
        compiler_params=pltpu.CompilerParams(vmem_limit_bytes=VMEM_GRANT),
    )(*arrays, *([before] if chained else []))


def offsets_of(groups, tok_count):
    half, quarter = tok_count // 2, tok_count // 4
    early = list(range(half, half + quarter))
    late = list(range(half + quarter, tok_count))
    near = list(range(half))
    return [j for j in range(groups - 1, 0, -1)], early, late, near


def one_sequence(values, keep, lengths, groups, tok_count):
    rows_dev = values.shape[2]
    _, early, late, near = offsets_of(groups, tok_count)
    layers = range(groups)

    def over_layer(array, j):
        return lax.ppermute(array, "layer", [(i, i ^ j) for i in range(groups)])

    def over_tok(array, k):
        return lax.ppermute(array, "tok", [(i, i ^ k) for i in range(tok_count)])

    def joined(arrays, n):
        return jnp.concatenate([array[n : n + 1] for array in arrays])

    def merge_into(plan):
        return merged(values, keep, lengths, plan, groups, tok_count)

    first = merge_into([[(j, early[0]) for j in layers]])
    second = merge_into(
        [[(j, k) for k in late] for j in layers] + [[(j, k) for j in layers] for k in early[1:]],
    )
    third = merge_into([[(j, k) for k in near] for j in layers])
    early_in = [over_tok(array, k) for array, k in zip([*first, *second[groups:]], early)]
    late_mine = [second[0]] + [over_layer(second[j], j) for j in layers if j]
    near_mine = [third[0]] + [over_layer(third[j], j) for j in layers if j]
    late_in = [over_tok(joined(late_mine, n), k) for n, k in enumerate(late)]
    near_in = [over_tok(joined(near_mine, n), k) for n, k in enumerate(near) if k]
    early_mine = [over_layer(joined(early_in, j), j) for j in layers if j]
    out = placed(
        [(array[:1], [(0, k)]) for array, k in zip(early_in, early)]
        + [(array[:1], [(j, 0)]) for array, j in zip(near_mine, layers)]
        + [(array, [(j, k) for j in layers]) for array, k in zip(near_in, near[1:])],
        groups, rows_dev,
    )
    return placed(
        [(array, [(j, k) for k in early]) for array, j in zip(early_mine, layers[1:])]
        + [(array, [(j, k) for j in layers]) for array, k in zip(late_in, late)],
        groups, rows_dev, before=out,
    )


def shards(kv_cache, keep_mask, lengths):
    groups = lax.axis_size("layer")
    tok_count = lax.axis_size("tok")
    seq_count = kv_cache.shape[3]
    return jnp.stack(
        [
            one_sequence(kv_cache[0, :, :, s], keep_mask[0, s : s + 1], lengths[s : s + 1], groups, tok_count)
            for s in range(seq_count)
        ]
    )


def solution(mesh):
    in_specs = (P("layer", None, None, None, "tok", None), P("layer", None, "tok"), P())
    out_specs = P(None, "layer", None, None, "tok", None)
    return jax.shard_map(shards, mesh=mesh, in_specs=in_specs, out_specs=out_specs, check_vma=False)
```

profile of v0, /device:TPU:0, one launch (start us, length us, event | category | flops | bytes accessed | tf_op | source)
XLA Modules:
  0.0 38.5 jit_solution(2377675084540677973)
XLA Ops:
  0.7 1.6 %shard_map.37 = bf16[4,1,2,2,2,16,128]{6,5,4,3,2,1,0:T(8,128)(2,1)S(1)} custom-call(s32[1]{0:T(128)S(6)} %copy.6.length_ref, s32[1,128]{1,0:T(1,128)} %bitcast.6, bf16[2,2,128,1024]{3,2,1,0:T(8,128)(2,1)} %bitcast.3), custom_call_target="tpu_custom_call" | custom-call | tf_op jit(solution)/shard_map/pallas_call | solution.py:100
  2.3 4.1 %collective-permute-start = (bf16[4,1,2,2,2,16,128]{6,5,4,3,2,1,0:T(8,128)(2,1)S(1)}, bf16[4,1,2,2,2,16,128]{6,5,4,3,2,1,0:T(8,128)(2,1)S(1)}, u32[]{:S(2)}, u32[]{:S(2)}) collective-permute-start(bf16[4,1,2,2,2,16,128]{6,5,4,3,2,1,0:T(8,128)(2,1)S(1)} %shard_map.37), channel_id=1, source_target_pairs={{0,4},{1,5},{2,6},{3,7},{4,0},{5,1},{6,2},{7,3},{8,12},{9,13},{10,... | collective-permute-start | bytes 393224 | tf_op jit(solution)/shard_map/ppermute | solution.py:180
  6.4 1.8 %shard_map.38 = (bf16[2,1,2,2,2,16,128]{6,5,4,3,2,1,0:T(8,128)(2,1)S(1)}, bf16[2,1,2,2,2,16,128]{6,5,4,3,2,1,0:T(8,128)(2,1)S(1)}, bf16[2,1,2,2,2,16,128]{6,5,4,...) custom-call(s32[1]{0:T(128)S(6)} %copy.6.length_ref, ...), custom_call_target="tpu_custom_call" | custom-call | tf_op jit(solution)/shard_map/pallas_call | solution.py:100
  8.2 0.1 collective-permute-start.5
  8.3 1.6 %collective-permute-start.6 = (bf16[2,1,2,2,2,16,128]{6,5,4,3,2,1,0:T(8,128)(2,1)S(1)}, bf16[2,1,2,2,2,16,128]{6,5,4,3,2,1,0:T(8,128)(2,1)S(1)}, u32[]{:S(2)}, u32[]{:S(2)}) collective-permute-start(bf16[2,1,2,2,2,16,128]{6,5,4,3,2,1,0:T(8,128)(2,1)S(1)} %get-tuple-element.17), channel_id=1, source_target_pairs={{0,16},{8,24},{16,0},{24,8},{1,17},{9,25},{17,1},{25,9},{2,18},{10... | collective-permute-start | bytes 196616 | tf_op jit(solution)/shard_map/ppermute | solution.py:177
  9.9 0.3 collective-permute-start.7
  10.2 1.3 %collective-permute-start.1 = (bf16[4,1,2,2,2,16,128]{6,5,4,3,2,1,0:T(8,128)(2,1)S(1)}, bf16[4,1,2,2,2,16,128]{6,5,4,3,2,1,0:T(8,128)(2,1)S(1)}, u32[]{:S(2)}, u32[]{:S(2)}) collective-permute-start(bf16[4,1,2,2,2,16,128]{6,5,4,3,2,1,0:T(8,128)(2,1)S(1)} %get-tuple-element.14), channel_id=1, source_target_pairs={{0,5},{1,4},{2,7},{3,6},{4,1},{5,0},{6,3},{7,2},{8,13},{9,12},{10,... | collective-permute-start | bytes 393224 | tf_op jit(solution)/shard_map/ppermute | solution.py:180
  11.4 2.0 %shard_map.39 = (bf16[4,1,2,2,2,16,128]{6,5,4,3,2,1,0:T(8,128)(2,1)S(1)}, bf16[4,1,2,2,2,16,128]{6,5,4,3,2,1,0:T(8,128)(2,1)S(1)}, bf16[4,1,2,2,2,16,128]{6,5,4,...) custom-call(s32[1]{0:T(128)S(6)} %copy.6.length_ref, s32[1,128]{1,0:T(1,128)} %bitcast.8, ...), custom_call_target="tpu_custom_call" | custom-call | tf_op jit(solution)/shard_map/pallas_call | solution.py:100
  13.5 0.0 collective-permute-done.5
  13.5 0.1 collective-permute-start.10
  13.6 0.0 collective-permute-done.6
  13.6 1.6 %collective-permute-start.11 = (bf16[4,1,2,2,2,16,128]{6,5,4,3,2,1,0:T(8,128)(2,1)S(1)}, bf16[4,1,2,2,2,16,128]{6,5,4,3,2,1,0:T(8,128)(2,1)S(1)}, u32[]{:S(2)}, u32[]{:S(2)}) collective-permute-start(bf16[4,1,2,2,2,16,128]{6,5,4,3,2,1,0:T(8,128)(2,1)S(1)} %get-tuple-element.21), channel_id=1, source_target_pairs={{0,16},{8,24},{16,0},{24,8},{1,17},{9,25},{17,1},{25,9},{2,18},{10... | collective-permute-start | bytes 393224 | tf_op jit(solution)/shard_map/ppermute | solution.py:177
  15.2 0.0 collective-permute-done.7
  15.2 0.4 collective-permute-start.12
  15.6 3.7 %collective-permute-start.8 = (bf16[4,1,2,2,2,16,128]{6,5,4,3,2,1,0:T(8,128)(2,1)S(1)}, bf16[4,1,2,2,2,16,128]{6,5,4,3,2,1,0:T(8,128)(2,1)S(1)}, u32[]{:S(2)}, u32[]{:S(2)}) collective-permute-start(bf16[4,1,2,2,2,16,128]{6,5,4,3,2,1,0:T(8,128)(2,1)S(1)} %pad_maximum_fusion), channel_id=1, source_target_pairs={{0,6},{1,7},{2,4},{3,5},{4,2},{5,3},{6,0},{7,1},{8,14},{9,15},{10,... | collective-permute-start | bytes 393224 | tf_op jit(solution)/shard_map/ppermute | solution.py:180
  19.3 0.8 %collective-permute-done.11 = bf16[4,1,2,2,2,16,128]{6,5,4,3,2,1,0:T(8,128)(2,1)S(1)} collective-permute-done((bf16[4,1,2,2,2,16,128]{6,5,4,3,2,1,0:T(8,128)(2,1)S(1)}, bf16[4,1,2,2,2,16,128]{6,5,4,3,2,1,0:T(8,128)(2,1)S(1)}, u32[]{:S(2)}, u32[]{:S(2)}) %collective-permute-start.11) | collective-permute-done | bytes 131104 | tf_op jit(solution)/shard_map/ppermute | solution.py:177
  20.1 3.5 %collective-permute-start.9 = (bf16[4,1,2,2,2,16,128]{6,5,4,3,2,1,0:T(8,128)(2,1)S(1)}, bf16[4,1,2,2,2,16,128]{6,5,4,3,2,1,0:T(8,128)(2,1)S(1)}, u32[]{:S(2)}, u32[]{:S(2)}) collective-permute-start(bf16[4,1,2,2,2,16,128]{6,5,4,3,2,1,0:T(8,128)(2,1)S(1)} %pad_maximum_fusion.1), channel_id=1, source_target_pairs={{0,7},{1,6},{2,5},{3,4},{4,3},{5,2},{6,1},{7,0},{8,15},{9,14},{10,... | collective-permute-start | bytes 393224 | tf_op jit(solution)/shard_map/ppermute | solution.py:180
  23.6 0.0 collective-permute-done.12
  23.7 1.6 %collective-permute-start.13 = (bf16[4,1,2,2,2,16,128]{6,5,4,3,2,1,0:T(8,128)(2,1)S(1)}, bf16[4,1,2,2,2,16,128]{6,5,4,3,2,1,0:T(8,128)(2,1)S(1)}, u32[]{:S(2)}, u32[]{:S(2)}) collective-permute-start(bf16[4,1,2,2,2,16,128]{6,5,4,3,2,1,0:T(8,128)(2,1)S(1)} %pad_maximum_fusion.2), channel_id=1, source_target_pairs={{0,1},{1,0},{2,3},{3,2},{4,5},{5,4},{6,7},{7,6},{8,9},{9,8},{10,11... | collective-permute-start | bytes 393224 | tf_op jit(solution)/shard_map/ppermute | solution.py:180
  25.3 0.1 collective-permute-start.14
  25.4 0.0 collective-permute-done.1
  25.4 2.0 %collective-permute-start.15 = (bf16[4,1,2,2,2,16,128]{6,5,4,3,2,1,0:T(8,128)(2,1)S(1)}, bf16[4,1,2,2,2,16,128]{6,5,4,3,2,1,0:T(8,128)(2,1)S(1)}, u32[]{:S(2)}, u32[]{:S(2)}) collective-permute-start(bf16[4,1,2,2,2,16,128]{6,5,4,3,2,1,0:T(8,128)(2,1)S(1)} %pad_maximum_fusion.4), channel_id=1, source_target_pairs={{0,3},{1,2},{2,1},{3,0},{4,7},{5,6},{6,5},{7,4},{8,11},{9,10},{10,... | collective-permute-start | bytes 393224 | tf_op jit(solution)/shard_map/ppermute | solution.py:180
  27.5 4.0 %collective-permute-done.13.rest_6_ = bf16[4,1,2,2,2,16,128]{6,5,4,3,2,1,0:T(8,128)(2,1)S(1)} collective-permute-done((bf16[4,1,2,2,2,16,128]{6,5,4,3,2,1,0:T(8,128)(2,1)S(1)}, bf16[4,1,2,2,2,16,128]{6,5,4,3,2,1,0:T(8,128)(2,1)S(1)}, u32[]{:S(2)}, u32[]{:S(2)}) %collective-permute-start.13) | collective-permute-done | bytes 131104 | tf_op jit(solution)/shard_map/ppermute | solution.py:180
  31.5 1.7 %collective-permute-start.3 = (bf16[2,1,2,2,2,16,128]{6,5,4,3,2,1,0:T(8,128)(2,1)S(1)}, bf16[2,1,2,2,2,16,128]{6,5,4,3,2,1,0:T(8,128)(2,1)S(1)}, u32[]{:S(2)}, u32[]{:S(2)}) collective-permute-start(bf16[2,1,2,2,2,16,128]{6,5,4,3,2,1,0:T(8,128)(2,1)S(1)} %pad_maximum_fusion.6), channel_id=1, source_target_pairs={{0,16},{8,24},{16,0},{24,8},{1,17},{9,25},{17,1},{25,9},{2,18},{10... | collective-permute-start | bytes 196616 | tf_op jit(solution)/shard_map/ppermute | solution.py:177
  33.2 0.1 collective-permute-done.15.rest_8_
  33.3 0.1 collective-permute-start.4
  33.4 1.0 %shard_map.40.rest_5_ = bf16[2,8,2,128,128]{4,3,2,1,0:T(8,128)(2,1)} custom-call(bf16[1,1,2,2,2,16,128]{6,5,4,3,2,1,0:T(8,128)(2,1)S(1)} %get-tuple-element.43.rest_0_, bf16[1,1,2,2,2,16,128]{6,5,4,3,2,1,0:T(8,128)(2,1)S(1)} %get-tuple-element.39.rest_1_, bf16[1,1,2,2,2,16,128]{6,5,4,3,2,1,0:T(8,128)(2,1)S(1)} %get-tuple-element.26.rest_2_, ...), custom_call_target="tpu_custom_call" | custom-call | tf_op jit(solution)/shard_map/pallas_call | solution.py:151
  34.4 0.0 collective-permute-done.8.rest_3_
  34.4 0.0 collective-permute-done.2.rest_0_
  34.4 1.6 %collective-permute-done.3.rest_1_ = bf16[2,1,2,2,2,16,128]{6,5,4,3,2,1,0:T(8,128)(2,1)S(1)} collective-permute-done((bf16[2,1,2,2,2,16,128]{6,5,4,3,2,1,0:T(8,128)(2,1)S(1)}, bf16[2,1,2,2,2,16,128]{6,5,4,3,2,1,0:T(8,128)(2,1)S(1)}, u32[]{:S(2)}, u32[]{:S(2)}) %collective-permute-start.3) | collective-permute-done | bytes 65568 | tf_op jit(solution)/shard_map/ppermute | solution.py:177
  36.0 1.6 %collective-permute-done.4.rest_2_ = bf16[2,1,2,2,2,16,128]{6,5,4,3,2,1,0:T(8,128)(2,1)S(1)} collective-permute-done((bf16[2,1,2,2,2,16,128]{6,5,4,3,2,1,0:T(8,128)(2,1)S(1)}, bf16[2,1,2,2,2,16,128]{6,5,4,3,2,1,0:T(8,128)(2,1)S(1)}, u32[]{:S(2)}, u32[]{:S(2)}) %collective-permute-start.4) | collective-permute-done | bytes 65568 | tf_op jit(solution)/shard_map/ppermute | solution.py:177
  37.7 0.9 %shard_map.41 = bf16[2,8,2,128,128]{4,3,2,1,0:T(8,128)(2,1)} custom-call(bf16[2,1,2,2,2,16,128]{6,5,4,3,2,1,0:T(8,128)(2,1)S(1)} %collective-permute-done.2.rest_0_, bf16[2,1,2,2,2,16,128]{6,5,4,3,2,1,0:T(8,128)(2,1)S(1)} %collective-permute-done.3.rest_1_, ...), custom_call_target="tpu_custom_call", output_to_operand_aliasing={{}: (5, {})} | custom-call | tf_op jit(solution)/shard_map/pallas_call | solution.py:151
  (23 shorter events, 0.2 us)
Async XLA Ops:
  2.3 23.0 %collective-permute-start = (bf16[4,1,2,2,2,16,128]{6,5,4,3,2,1,0:T(8,128)(2,1)S(1)}, bf16[4,1,2,2,2,16,128]{6,5,4,3,2,1,0:T(8,128)(2,1)S(1)}, u32[]{:S(2)}, u32[]{:S(2)}) collective-permute-start(bf16[4,1,2,2,2,16,128]{6,5,4,3,2,1,0:T(8,128)(2,1)S(1)} %shard_map.37), channel_id=1, source_target_pairs={{0,4},{1,5},{2,6},{3,7},{4,0},{5,1},{6,2},{7,3},{8,12},{9,13},{10,... | collective-permute-start | bytes 393224 | tf_op jit(solution)/shard_map/ppermute | solution.py:180
  8.2 5.2 %collective-permute-start.5 = (bf16[2,1,2,2,2,16,128]{6,5,4,3,2,1,0:T(8,128)(2,1)S(1)}, bf16[2,1,2,2,2,16,128]{6,5,4,3,2,1,0:T(8,128)(2,1)S(1)}, u32[]{:S(2)}, u32[]{:S(2)}) collective-permute-start(bf16[2,1,2,2,2,16,128]{6,5,4,3,2,1,0:T(8,128)(2,1)S(1)} %get-tuple-element.16), channel_id=1, source_target_pairs={{0,8},{8,0},{16,24},{24,16},{1,9},{9,1},{17,25},{25,17},{2,10},{10... | collective-permute-start | bytes 196616 | tf_op jit(solution)/shard_map/ppermute | solution.py:177
  8.3 5.3 %collective-permute-start.6 = (bf16[2,1,2,2,2,16,128]{6,5,4,3,2,1,0:T(8,128)(2,1)S(1)}, bf16[2,1,2,2,2,16,128]{6,5,4,3,2,1,0:T(8,128)(2,1)S(1)}, u32[]{:S(2)}, u32[]{:S(2)}) collective-permute-start(bf16[2,1,2,2,2,16,128]{6,5,4,3,2,1,0:T(8,128)(2,1)S(1)} %get-tuple-element.17), channel_id=1, source_target_pairs={{0,16},{8,24},{16,0},{24,8},{1,17},{9,25},{17,1},{25,9},{2,18},{10... | collective-permute-start | bytes 196616 | tf_op jit(solution)/shard_map/ppermute | solution.py:177
  9.9 5.3 %collective-permute-start.7 = (bf16[2,1,2,2,2,16,128]{6,5,4,3,2,1,0:T(8,128)(2,1)S(1)}, bf16[2,1,2,2,2,16,128]{6,5,4,3,2,1,0:T(8,128)(2,1)S(1)}, u32[]{:S(2)}, u32[]{:S(2)}) collective-permute-start(bf16[2,1,2,2,2,16,128]{6,5,4,3,2,1,0:T(8,128)(2,1)S(1)} %get-tuple-element.18), channel_id=1, source_target_pairs={{0,24},{8,16},{16,8},{24,0},{1,25},{9,17},{17,9},{25,1},{2,26},{10... | collective-permute-start | bytes 196616 | tf_op jit(solution)/shard_map/ppermute | solution.py:177
  10.2 15.3 %collective-permute-start.1 = (bf16[4,1,2,2,2,16,128]{6,5,4,3,2,1,0:T(8,128)(2,1)S(1)}, bf16[4,1,2,2,2,16,128]{6,5,4,3,2,1,0:T(8,128)(2,1)S(1)}, u32[]{:S(2)}, u32[]{:S(2)}) collective-permute-start(bf16[4,1,2,2,2,16,128]{6,5,4,3,2,1,0:T(8,128)(2,1)S(1)} %get-tuple-element.14), channel_id=1, source_target_pairs={{0,5},{1,4},{2,7},{3,6},{4,1},{5,0},{6,3},{7,2},{8,13},{9,12},{10,... | collective-permute-start | bytes 393224 | tf_op jit(solution)/shard_map/ppermute | solution.py:180
  13.5 2.1 %collective-permute-start.10 = (bf16[4,1,2,2,2,16,128]{6,5,4,3,2,1,0:T(8,128)(2,1)S(1)}, bf16[4,1,2,2,2,16,128]{6,5,4,3,2,1,0:T(8,128)(2,1)S(1)}, u32[]{:S(2)}, u32[]{:S(2)}) collective-permute-start(bf16[4,1,2,2,2,16,128]{6,5,4,3,2,1,0:T(8,128)(2,1)S(1)} %get-tuple-element.20), channel_id=1, source_target_pairs={{0,8},{8,0},{16,24},{24,16},{1,9},{9,1},{17,25},{25,17},{2,10},{10... | collective-permute-start | bytes 393224 | tf_op jit(solution)/shard_map/ppermute | solution.py:177
  13.6 6.4 %collective-permute-start.11 = (bf16[4,1,2,2,2,16,128]{6,5,4,3,2,1,0:T(8,128)(2,1)S(1)}, bf16[4,1,2,2,2,16,128]{6,5,4,3,2,1,0:T(8,128)(2,1)S(1)}, u32[]{:S(2)}, u32[]{:S(2)}) collective-permute-start(bf16[4,1,2,2,2,16,128]{6,5,4,3,2,1,0:T(8,128)(2,1)S(1)} %get-tuple-element.21), channel_id=1, source_target_pairs={{0,16},{8,24},{16,0},{24,8},{1,17},{9,25},{17,1},{25,9},{2,18},{10... | collective-permute-start | bytes 393224 | tf_op jit(solution)/shard_map/ppermute | solution.py:177
  15.2 8.4 %collective-permute-start.12 = (bf16[4,1,2,2,2,16,128]{6,5,4,3,2,1,0:T(8,128)(2,1)S(1)}, bf16[4,1,2,2,2,16,128]{6,5,4,3,2,1,0:T(8,128)(2,1)S(1)}, u32[]{:S(2)}, u32[]{:S(2)}) collective-permute-start(bf16[4,1,2,2,2,16,128]{6,5,4,3,2,1,0:T(8,128)(2,1)S(1)} %get-tuple-element.22), channel_id=1, source_target_pairs={{0,24},{8,16},{16,8},{24,0},{1,25},{9,17},{17,9},{25,1},{2,26},{10... | collective-permute-start | bytes 393224 | tf_op jit(solution)/shard_map/ppermute | solution.py:177
  15.6 18.8 %collective-permute-start.8 = (bf16[4,1,2,2,2,16,128]{6,5,4,3,2,1,0:T(8,128)(2,1)S(1)}, bf16[4,1,2,2,2,16,128]{6,5,4,3,2,1,0:T(8,128)(2,1)S(1)}, u32[]{:S(2)}, u32[]{:S(2)}) collective-permute-start(bf16[4,1,2,2,2,16,128]{6,5,4,3,2,1,0:T(8,128)(2,1)S(1)} %pad_maximum_fusion), channel_id=1, source_target_pairs={{0,6},{1,7},{2,4},{3,5},{4,2},{5,3},{6,0},{7,1},{8,14},{9,15},{10,... | collective-permute-start | bytes 393224 | tf_op jit(solution)/shard_map/ppermute | solution.py:180
  20.1 14.3 %collective-permute-start.9 = (bf16[4,1,2,2,2,16,128]{6,5,4,3,2,1,0:T(8,128)(2,1)S(1)}, bf16[4,1,2,2,2,16,128]{6,5,4,3,2,1,0:T(8,128)(2,1)S(1)}, u32[]{:S(2)}, u32[]{:S(2)}) collective-permute-start(bf16[4,1,2,2,2,16,128]{6,5,4,3,2,1,0:T(8,128)(2,1)S(1)} %pad_maximum_fusion.1), channel_id=1, source_target_pairs={{0,7},{1,6},{2,5},{3,4},{4,3},{5,2},{6,1},{7,0},{8,15},{9,14},{10,... | collective-permute-start | bytes 393224 | tf_op jit(solution)/shard_map/ppermute | solution.py:180
  23.7 7.8 %collective-permute-start.13 = (bf16[4,1,2,2,2,16,128]{6,5,4,3,2,1,0:T(8,128)(2,1)S(1)}, bf16[4,1,2,2,2,16,128]{6,5,4,3,2,1,0:T(8,128)(2,1)S(1)}, u32[]{:S(2)}, u32[]{:S(2)}) collective-permute-start(bf16[4,1,2,2,2,16,128]{6,5,4,3,2,1,0:T(8,128)(2,1)S(1)} %pad_maximum_fusion.2), channel_id=1, source_target_pairs={{0,1},{1,0},{2,3},{3,2},{4,5},{5,4},{6,7},{7,6},{8,9},{9,8},{10,11... | collective-permute-start | bytes 393224 | tf_op jit(solution)/shard_map/ppermute | solution.py:180
  25.3 6.2 %collective-permute-start.14 = (bf16[4,1,2,2,2,16,128]{6,5,4,3,2,1,0:T(8,128)(2,1)S(1)}, bf16[4,1,2,2,2,16,128]{6,5,4,3,2,1,0:T(8,128)(2,1)S(1)}, u32[]{:S(2)}, u32[]{:S(2)}) collective-permute-start(bf16[4,1,2,2,2,16,128]{6,5,4,3,2,1,0:T(8,128)(2,1)S(1)} %pad_maximum_fusion.3), channel_id=1, source_target_pairs={{0,2},{1,3},{2,0},{3,1},{4,6},{5,7},{6,4},{7,5},{8,10},{9,11},{10,... | collective-permute-start | bytes 393224 | tf_op jit(solution)/shard_map/ppermute | solution.py:180
  25.4 7.9 %collective-permute-start.15 = (bf16[4,1,2,2,2,16,128]{6,5,4,3,2,1,0:T(8,128)(2,1)S(1)}, bf16[4,1,2,2,2,16,128]{6,5,4,3,2,1,0:T(8,128)(2,1)S(1)}, u32[]{:S(2)}, u32[]{:S(2)}) collective-permute-start(bf16[4,1,2,2,2,16,128]{6,5,4,3,2,1,0:T(8,128)(2,1)S(1)} %pad_maximum_fusion.4), channel_id=1, source_target_pairs={{0,3},{1,2},{2,1},{3,0},{4,7},{5,6},{6,5},{7,4},{8,11},{9,10},{10,... | collective-permute-start | bytes 393224 | tf_op jit(solution)/shard_map/ppermute | solution.py:180
  31.5 2.9 %collective-permute-start.2 = (bf16[2,1,2,2,2,16,128]{6,5,4,3,2,1,0:T(8,128)(2,1)S(1)}, bf16[2,1,2,2,2,16,128]{6,5,4,3,2,1,0:T(8,128)(2,1)S(1)}, u32[]{:S(2)}, u32[]{:S(2)}) collective-permute-start(bf16[2,1,2,2,2,16,128]{6,5,4,3,2,1,0:T(8,128)(2,1)S(1)} %pad_maximum_fusion.5), channel_id=1, source_target_pairs={{0,8},{8,0},{16,24},{24,16},{1,9},{9,1},{17,25},{25,17},{2,10},{10... | collective-permute-start | bytes 196616 | tf_op jit(solution)/shard_map/ppermute | solution.py:177
  31.5 4.5 %collective-permute-start.3 = (bf16[2,1,2,2,2,16,128]{6,5,4,3,2,1,0:T(8,128)(2,1)S(1)}, bf16[2,1,2,2,2,16,128]{6,5,4,3,2,1,0:T(8,128)(2,1)S(1)}, u32[]{:S(2)}, u32[]{:S(2)}) collective-permute-start(bf16[2,1,2,2,2,16,128]{6,5,4,3,2,1,0:T(8,128)(2,1)S(1)} %pad_maximum_fusion.6), channel_id=1, source_target_pairs={{0,16},{8,24},{16,0},{24,8},{1,17},{9,25},{17,1},{25,9},{2,18},{10... | collective-permute-start | bytes 196616 | tf_op jit(solution)/shard_map/ppermute | solution.py:177
  33.3 4.3 %collective-permute-start.4 = (bf16[2,1,2,2,2,16,128]{6,5,4,3,2,1,0:T(8,128)(2,1)S(1)}, bf16[2,1,2,2,2,16,128]{6,5,4,3,2,1,0:T(8,128)(2,1)S(1)}, u32[]{:S(2)}, u32[]{:S(2)}) collective-permute-start(bf16[2,1,2,2,2,16,128]{6,5,4,3,2,1,0:T(8,128)(2,1)S(1)} %pad_maximum_fusion.7), channel_id=1, source_target_pairs={{0,24},{8,16},{16,8},{24,0},{1,25},{9,17},{17,9},{25,1},{2,26},{10... | collective-permute-start | bytes 196616 | tf_op jit(solution)/shard_map/ppermute | solution.py:177
where the time goes:
time: 39.2 us; the launch traced here: 38.5 us
  starting transfers between devices  22 us (56%)
  waiting for transfers between devices  8.18 us (21%)
  Pallas kernels  7.22 us (18%)
  between operations  0.88 us (2%)
    ppermute x7, starting transfers between devices, over_tok(): return lax.ppermute(array, 'tok', [(i, i ^ k) for i in range(tok_count)])  16.3 us
    ppermute x9, starting transfers between devices, over_layer(): return lax.ppermute(array, 'layer', [(i, i ^ j) for i in range(groups)])  5.74 us
    pallas_call x3, Pallas kernels, merged(): pl.pallas_call(functools.partial(merge_kernel, plan=plan, groups=groups,...  5.39 us
    ppermute x7, waiting for transfers between devices, over_tok(): return lax.ppermute(array, 'tok', [(i, i ^ k) for i in range(tok_count)])  4.15 us
    ppermute x9, waiting for transfers between devices, over_layer(): return lax.ppermute(array, 'layer', [(i, i ^ j) for i in range(groups)])  4.03 us
    pallas_call x2, Pallas kernels, placed(): pl.pallas_call(functools.partial(place_kernel, plan=plan, rounds=rounds,...  1.83 us
  transfers between devices with their start and end apart: 16, of which 5 were waited for; matrix products, arithmetic and copies ran while one was open for 1% of the time, Pallas kernels for 12%

commit v1 on v0

--- a/solution.py
+++ b/solution.py
@@ -25,13 +25,14 @@
     upper_inverse = lax.rsqrt(upper_square)
     summed = lower * lower_inverse + upper * upper_inverse
     summed_inverse = lax.rsqrt(jnp.mean(summed * summed, axis=-1, keepdims=True) + epsilon)
-    direction = summed * (summed_inverse * live)
+    direction = summed * (summed_inverse if live is None else summed_inverse * live)
     lower_out = jnp.where(retained, lower, (lower_square * lower_inverse) * direction)
     upper_out = jnp.where(retained, upper, (upper_square * upper_inverse) * direction)
     return lower_out.astype(jnp.bfloat16), upper_out.astype(jnp.bfloat16)
 
 
-def merge_kernel(length_ref, keep_ref, values_ref, *rest, plan, groups, tok_count, rounds):
+def merge_kernel(*refs, plan, groups, tok_count, rounds, limited):
+    keep_ref, values_ref, *rest = refs[limited:]
     outs, (loaded, mask, columns, sems, mask_sem) = rest[: len(plan)], rest[len(plan) :]
     layer, tok = lax.axis_index("layer"), lax.axis_index("tok")
     rows_dev = values_ref.shape[2]
@@ -64,12 +65,13 @@
     for k in offsets:
         for r in range(rounds):
             start = pl.multiple_of((r * tok_count + (tok ^ k)) * PAGE, PAGE)
-            inside = (row + (tok * rows_dev + start)) < length_ref[0]
-            live.append(inside.astype(jnp.float32))
-            kept = columns[pl.ds(start, PAGE), :]
-            retained.append(kept * live[-1])
+            retained.append(columns[pl.ds(start, PAGE), :])
+            if limited:
+                inside = (row + (tok * rows_dev + start)) < refs[0][0]
+                live.append(inside.astype(jnp.float32))
+                retained[-1] *= live[-1]
     retained = jnp.concatenate(retained, axis=0) > 0.0
-    live = jnp.concatenate(live, axis=0)
+    live = jnp.concatenate(live, axis=0) if limited else None
     where = {}
     for o, entry in enumerate(plan):
         for n, piece in enumerate(entry):
@@ -98,9 +100,9 @@
     head_group = KVH // groups
     count = len({k for entry in plan for _, k in entry})
     return pl.pallas_call(
-        functools.partial(merge_kernel, plan=plan, groups=groups, tok_count=tok_count, rounds=rounds),
+        functools.partial(merge_kernel, plan=plan, groups=groups, tok_count=tok_count, rounds=rounds, limited=len(lengths)),
         in_specs=[
-            pl.BlockSpec(memory_space=pltpu.SMEM),
+            *[pl.BlockSpec(memory_space=pltpu.SMEM) for _ in lengths],
             pl.BlockSpec(memory_space=pltpu.HBM),
             pl.BlockSpec(memory_space=pltpu.HBM),
         ],
@@ -117,7 +119,7 @@
             pltpu.SemaphoreType.DMA(()),
         ],
         compiler_params=pltpu.CompilerParams(vmem_limit_bytes=VMEM_GRANT),
-    )(lengths, *[pltpu.with_memory_space_constraint(array, pltpu.HBM) for array in (keep, values)])
+    )(*lengths, *[pltpu.with_memory_space_constraint(array, pltpu.HBM) for array in (keep, values)])
 
 
 def place_kernel(*rest, plan, rounds, chained):
@@ -162,15 +164,16 @@
 
 def offsets_of(groups, tok_count):
     half, quarter = tok_count // 2, tok_count // 4
+    small = list(range(quarter))
+    middle = list(range(quarter, half))
     early = list(range(half, half + quarter))
     late = list(range(half + quarter, tok_count))
-    near = list(range(half))
-    return [j for j in range(groups - 1, 0, -1)], early, late, near
+    return list(range(groups - 1, 0, -1)), small, middle, early, late
 
 
 def one_sequence(values, keep, lengths, groups, tok_count):
     rows_dev = values.shape[2]
-    _, early, late, near = offsets_of(groups, tok_count)
+    _, small, middle, early, late = offsets_of(groups, tok_count)
     layers = range(groups)
 
     def over_layer(array, j):
@@ -182,29 +185,42 @@
     def joined(arrays, n):
         return jnp.concatenate([array[n : n + 1] for array in arrays])
 
-    def merge_into(plan):
-        return merged(values, keep, lengths, plan, groups, tok_count)
-
-    first = merge_into([[(j, early[0]) for j in layers]])
-    second = merge_into(
-        [[(j, k) for k in late] for j in layers] + [[(j, k) for j in layers] for k in early[1:]],
-    )
-    third = merge_into([[(j, k) for k in near] for j in layers])
-    early_in = [over_tok(array, k) for array, k in zip([*first, *second[groups:]], early)]
+    def merge_into(plan, limits):
+        return merged(values, keep, limits, plan, groups, tok_count)
+
+    def without_padding(array, k):
+        rounds = array.shape[1]
+        tok = lax.axis_index("tok")
+        first = (tok ^ k) * rows_dev + tok * PAGE
+        shape = (1, rounds, 1, 1, 1, PAGE, HD)
+        position = first + lax.broadcasted_iota(jnp.int32, shape, 5)
+        position += lax.broadcasted_iota(jnp.int32, shape, 1) * (PAGE * tok_count)
+        return jnp.where(position < lengths[0], array, jnp.zeros_like(array))
+
+    first = merge_into([[(j, k) for j in layers] for k in early], [])
+    lengths, first = lax.optimization_barrier((lengths, first))
+    second = merge_into([[(j, k) for k in late] for j in layers], [lengths])
+    third = merge_into(
+        [[(j, k) for j in layers] for k in middle] + [[(j, k) for k in small] for j in layers], [lengths]
+    )
+    early_in = [without_padding(over_tok(array, k), k) for array, k in zip(first, early)]
     late_mine = [second[0]] + [over_layer(second[j], j) for j in layers if j]
-    near_mine = [third[0]] + [over_layer(third[j], j) for j in layers if j]
+    middle_in = [over_tok(array, k) for array, k in zip(third, middle)]
+    small_mine = third[len(middle) :]
+    small_mine = [small_mine[0]] + [over_layer(small_mine[j], j) for j in layers if j]
     late_in = [over_tok(joined(late_mine, n), k) for n, k in enumerate(late)]
-    near_in = [over_tok(joined(near_mine, n), k) for n, k in enumerate(near) if k]
-    early_mine = [over_layer(joined(early_in, j), j) for j in layers if j]
+    small_in = [over_tok(joined(small_mine, n), k) for n, k in enumerate(small) if k]
+    relayed = middle + early
+    relayed_mine = [over_layer(joined(middle_in + early_in, j), j) for j in layers if j]
     out = placed(
-        [(array[:1], [(0, k)]) for array, k in zip(early_in, early)]
-        + [(array[:1], [(j, 0)]) for array, j in zip(near_mine, layers)]
-        + [(array, [(j, k) for j in layers]) for array, k in zip(near_in, near[1:])],
+        [(array[:1], [(0, k)]) for array, k in zip(middle_in + early_in, relayed)]
+        + [(array[:1], [(j, 0)]) for array, j in zip(small_mine, layers)]
+        + [(array, [(j, k) for j in layers]) for array, k in zip(small_in, small[1:])]
+        + [(array, [(j, k) for k in relayed]) for array, j in zip(relayed_mine, layers[1:])],
         groups, rows_dev,
     )
     return placed(
-        [(array, [(j, k) for k in early]) for array, j in zip(early_mine, layers[1:])]
-        + [(array, [(j, k) for j in layers]) for array, k in zip(late_in, late)],
+        [(array, [(j, k) for j in layers]) for array, k in zip(late_in, late)],
         groups, rows_dev, before=out,
     )
 

time: 39.2 us -> 43.1 us (1.099)
  waiting for transfers between devices: 8.18 us -> 11.3 us
  starting transfers between devices: 22 us -> 23 us
    ppermute x7, waiting for transfers between devices: 4.15 us -> 8.39 us  [over_tok(): return lax.ppermute(array, 'tok', [(i, i ^ k) for i in range(tok_count)])]
    ppermute x9, starting transfers between devices: 5.74 us -> 7.23 us  [over_layer(): return lax.ppermute(array, 'layer', [(i, i ^ j) for i in range(groups)])]
    ppermute x9, waiting for transfers between devices: 4.03 us -> 2.91 us  [over_layer(): return lax.ppermute(array, 'layer', [(i, i ^ j) for i in range(groups)])]
    ppermute x7, starting transfers between devices: 16.3 us -> 15.8 us  [over_tok(): return lax.ppermute(array, 'tok', [(i, i ^ k) for i in range(tok_count)])]
  transfers between devices with their start and end apart: 16 -> 16, of which waited for: 5 -> 6; matrix products, arithmetic and copies ran while one was open for 1% -> 1% of each run, Pallas kernels for 12% -> 11%
where the time goes in v1:
time: 43.1 us; the launch traced here: 42.8 us
  starting transfers between devices  23 us (53%)
  waiting for transfers between devices  11.3 us (26%)
  Pallas kernels  7.22 us (17%)
  between operations  0.88 us (2%)
    ppermute x7, starting transfers between devices, over_tok(): return lax.ppermute(array, 'tok', [(i, i ^ k) for i in range(tok_count)])  15.8 us
    ppermute x7, waiting for transfers between devices, over_tok(): return lax.ppermute(array, 'tok', [(i, i ^ k) for i in range(tok_count)])  8.39 us
    ppermute x9, starting transfers between devices, over_layer(): return lax.ppermute(array, 'layer', [(i, i ^ j) for i in range(groups)])  7.23 us
    pallas_call x3, Pallas kernels, merged(): pl.pallas_call(functools.partial(merge_kernel, plan=plan, groups=groups,...  5.39 us
    ppermute x9, waiting for transfers between devices, over_layer(): return lax.ppermute(array, 'layer', [(i, i ^ j) for i in range(groups)])  2.91 us
    pallas_call x2, Pallas kernels, placed(): pl.pallas_call(functools.partial(place_kernel, plan=plan, rounds=rounds,...  1.83 us
  transfers between devices with their start and end apart: 16, of which 6 were waited for; matrix products, arithmetic and copies ran while one was open for 1% of the time, Pallas kernels for 11%

profile of v1, /device:TPU:0, one launch (start us, length us, event | category | flops | bytes accessed | tf_op | source)
XLA Modules:
  0.0 42.8 jit_solution(11537183736135691211)
XLA Ops:
  0.7 1.7 %shard_map.38 = (bf16[2,1,2,2,2,16,128]{6,5,4,3,2,1,0:T(8,128)(2,1)S(1)}, bf16[2,1,2,2,2,16,128]{6,5,4,3,2,1,0:T(8,128)(2,1)S(1)}, bf16[2,1,2,2,2,16,128]{6,5,4,...) custom-call(s32[1]{0:T(128)} %copy.6.refs_0_, s32[1,128]{1,0:T(1,128)} %bitcast.9, bf16[2,2,128,1024]{3,2,1,0:T(8,128)(2,1)} %bitcast.6), custom_call_target="tpu_custom_call" | custom-call | tf_op jit(solution)/shard_map/pallas_call | solution.py:102
  2.4 0.6 %collective-permute-start = (bf16[2,1,2,2,2,16,128]{6,5,4,3,2,1,0:T(8,128)(2,1)S(1)}, bf16[2,1,2,2,2,16,128]{6,5,4,3,2,1,0:T(8,128)(2,1)S(1)}, u32[]{:S(2)}, u32[]{:S(2)}) collective-permute-start(bf16[2,1,2,2,2,16,128]{6,5,4,3,2,1,0:T(8,128)(2,1)S(1)} %get-tuple-element.24), channel_id=1, source_target_pairs={{0,8},{8,0},{16,24},{24,16},{1,9},{9,1},{17,25},{25,17},{2,10},{10... | collective-permute-start | bytes 196616 | tf_op jit(solution)/shard_map/ppermute | solution.py:180
  2.9 2.6 %collective-permute-start.1 = (bf16[2,1,2,2,2,16,128]{6,5,4,3,2,1,0:T(8,128)(2,1)S(1)}, bf16[2,1,2,2,2,16,128]{6,5,4,3,2,1,0:T(8,128)(2,1)S(1)}, u32[]{:S(2)}, u32[]{:S(2)}) collective-permute-start(bf16[2,1,2,2,2,16,128]{6,5,4,3,2,1,0:T(8,128)(2,1)S(1)} %get-tuple-element.25), channel_id=1, source_target_pairs={{0,16},{8,24},{16,0},{24,8},{1,17},{9,25},{17,1},{25,9},{2,18},{10... | collective-permute-start | bytes 196616 | tf_op jit(solution)/shard_map/ppermute | solution.py:180
  5.5 0.0 collective-permute-start.2
  5.5 1.7 %shard_map.37 = (bf16[4,1,2,2,2,16,128]{6,5,4,3,2,1,0:T(8,128)(2,1)S(1)}, bf16[4,1,2,2,2,16,128]{6,5,4,3,2,1,0:T(8,128)(2,1)S(1)}) custom-call(s32[1,128]{1,0:T(1,128)} %bitcast.10, bf16[2,2,128,1024]{3,2,1,0:T(8,128)(2,1)} %bitcast.7), custom_call_target="tpu_custom_call" | custom-call | tf_op jit(solution)/shard_map/pallas_call | solution.py:102
  7.3 2.9 %collective-permute-start.7 = (bf16[4,1,2,2,2,16,128]{6,5,4,3,2,1,0:T(8,128)(2,1)S(1)}, bf16[4,1,2,2,2,16,128]{6,5,4,3,2,1,0:T(8,128)(2,1)S(1)}, u32[]{:S(2)}, u32[]{:S(2)}) collective-permute-start(bf16[4,1,2,2,2,16,128]{6,5,4,3,2,1,0:T(8,128)(2,1)S(1)} %get-tuple-element.29), channel_id=1, source_target_pairs={{0,4},{1,5},{2,6},{3,7},{4,0},{5,1},{6,2},{7,3},{8,12},{9,13},{10,... | collective-permute-start | bytes 393224 | tf_op jit(solution)/shard_map/ppermute | solution.py:183
  10.2 1.3 %collective-permute-start.8 = (bf16[4,1,2,2,2,16,128]{6,5,4,3,2,1,0:T(8,128)(2,1)S(1)}, bf16[4,1,2,2,2,16,128]{6,5,4,3,2,1,0:T(8,128)(2,1)S(1)}, u32[]{:S(2)}, u32[]{:S(2)}) collective-permute-start(bf16[4,1,2,2,2,16,128]{6,5,4,3,2,1,0:T(8,128)(2,1)S(1)} %get-tuple-element.30), channel_id=1, source_target_pairs={{0,5},{1,4},{2,7},{3,6},{4,1},{5,0},{6,3},{7,2},{8,13},{9,12},{10,... | collective-permute-start | bytes 393224 | tf_op jit(solution)/shard_map/ppermute | solution.py:183
  11.5 2.0 %shard_map.39 = (bf16[4,1,2,2,2,16,128]{6,5,4,3,2,1,0:T(8,128)(2,1)S(1)}, bf16[4,1,2,2,2,16,128]{6,5,4,3,2,1,0:T(8,128)(2,1)S(1)}, bf16[2,1,2,2,2,16,128]{6,5,4,...) custom-call(s32[1]{0:T(128)} %copy.6.refs_0_, ...), custom_call_target="tpu_custom_call" | custom-call | tf_op jit(solution)/shard_map/pallas_call | solution.py:102
  13.5 0.0 collective-permute-done
  13.5 0.1 collective-permute-start.9
  13.6 1.6 %collective-permute-start.10 = (bf16[2,1,2,2,2,16,128]{6,5,4,3,2,1,0:T(8,128)(2,1)S(1)}, bf16[2,1,2,2,2,16,128]{6,5,4,3,2,1,0:T(8,128)(2,1)S(1)}, u32[]{:S(2)}, u32[]{:S(2)}) collective-permute-start(bf16[2,1,2,2,2,16,128]{6,5,4,3,2,1,0:T(8,128)(2,1)S(1)} %get-tuple-element.33), channel_id=1, source_target_pairs={{0,16},{8,24},{16,0},{24,8},{1,17},{9,25},{17,1},{25,9},{2,18},{10... | collective-permute-start | bytes 196616 | tf_op jit(solution)/shard_map/ppermute | solution.py:180
  15.2 0.4 collective-permute-start.11
  15.6 1.6 %collective-permute-start.5 = (bf16[4,1,2,2,2,16,128]{6,5,4,3,2,1,0:T(8,128)(2,1)S(1)}, bf16[4,1,2,2,2,16,128]{6,5,4,3,2,1,0:T(8,128)(2,1)S(1)}, u32[]{:S(2)}, u32[]{:S(2)}) collective-permute-start(bf16[4,1,2,2,2,16,128]{6,5,4,3,2,1,0:T(8,128)(2,1)S(1)} %get-tuple-element.27), channel_id=1, source_target_pairs={{0,2},{1,3},{2,0},{3,1},{4,6},{5,7},{6,4},{7,5},{8,10},{9,11},{10,... | collective-permute-start | bytes 393224 | tf_op jit(solution)/shard_map/ppermute | solution.py:183
  17.2 0.9 %collective-permute-done.10 = bf16[2,1,2,2,2,16,128]{6,5,4,3,2,1,0:T(8,128)(2,1)S(1)} collective-permute-done((bf16[2,1,2,2,2,16,128]{6,5,4,3,2,1,0:T(8,128)(2,1)S(1)}, bf16[2,1,2,2,2,16,128]{6,5,4,3,2,1,0:T(8,128)(2,1)S(1)}, u32[]{:S(2)}, u32[]{:S(2)}) %collective-permute-start.10) | collective-permute-done | bytes 65568 | tf_op jit(solution)/shard_map/ppermute | solution.py:180
  18.1 1.5 %collective-permute-start.6 = (bf16[4,1,2,2,2,16,128]{6,5,4,3,2,1,0:T(8,128)(2,1)S(1)}, bf16[4,1,2,2,2,16,128]{6,5,4,3,2,1,0:T(8,128)(2,1)S(1)}, u32[]{:S(2)}, u32[]{:S(2)}) collective-permute-start(bf16[4,1,2,2,2,16,128]{6,5,4,3,2,1,0:T(8,128)(2,1)S(1)} %get-tuple-element.28), channel_id=1, source_target_pairs={{0,3},{1,2},{2,1},{3,0},{4,7},{5,6},{6,5},{7,4},{8,11},{9,10},{10,... | collective-permute-start | bytes 393224 | tf_op jit(solution)/shard_map/ppermute | solution.py:183
  19.7 0.0 collective-permute-done.11
  19.7 3.1 %collective-permute-start.3 = (bf16[4,1,2,2,2,16,128]{6,5,4,3,2,1,0:T(8,128)(2,1)S(1)}, bf16[4,1,2,2,2,16,128]{6,5,4,3,2,1,0:T(8,128)(2,1)S(1)}, u32[]{:S(2)}, u32[]{:S(2)}) collective-permute-start(bf16[4,1,2,2,2,16,128]{6,5,4,3,2,1,0:T(8,128)(2,1)S(1)} %pad_maximum_fusion), channel_id=1, source_target_pairs={{0,6},{1,7},{2,4},{3,5},{4,2},{5,3},{6,0},{7,1},{8,14},{9,15},{10,... | collective-permute-start | bytes 393224 | tf_op jit(solution)/shard_map/ppermute | solution.py:183
  22.9 0.0 collective-permute-done.7
  22.9 1.0 %collective-permute-start.12 = (bf16[4,1,2,2,2,16,128]{6,5,4,3,2,1,0:T(8,128)(2,1)S(1)}, bf16[4,1,2,2,2,16,128]{6,5,4,3,2,1,0:T(8,128)(2,1)S(1)}, u32[]{:S(2)}, u32[]{:S(2)}) collective-permute-start(bf16[4,1,2,2,2,16,128]{6,5,4,3,2,1,0:T(8,128)(2,1)S(1)} %pad_maximum_fusion.2), channel_id=1, source_target_pairs={{0,1},{1,0},{2,3},{3,2},{4,5},{5,4},{6,7},{7,6},{8,9},{9,8},{10,11... | collective-permute-start | bytes 393224 | tf_op jit(solution)/shard_map/ppermute | solution.py:183
  23.9 0.1 broadcast_select_fusion.1
  24.0 0.1 broadcast_select_fusion
  24.1 1.4 %collective-permute-done.5 = bf16[4,1,2,2,2,16,128]{6,5,4,3,2,1,0:T(8,128)(2,1)S(1)} collective-permute-done((bf16[4,1,2,2,2,16,128]{6,5,4,3,2,1,0:T(8,128)(2,1)S(1)}, bf16[4,1,2,2,2,16,128]{6,5,4,3,2,1,0:T(8,128)(2,1)S(1)}, u32[]{:S(2)}, u32[]{:S(2)}) %collective-permute-start.5) | collective-permute-done | bytes 131104 | tf_op jit(solution)/shard_map/ppermute | solution.py:183
  25.5 5.8 %collective-permute-done.6 = bf16[4,1,2,2,2,16,128]{6,5,4,3,2,1,0:T(8,128)(2,1)S(1)} collective-permute-done((bf16[4,1,2,2,2,16,128]{6,5,4,3,2,1,0:T(8,128)(2,1)S(1)}, bf16[4,1,2,2,2,16,128]{6,5,4,3,2,1,0:T(8,128)(2,1)S(1)}, u32[]{:S(2)}, u32[]{:S(2)}) %collective-permute-start.6) | collective-permute-done | bytes 131104 | tf_op jit(solution)/shard_map/ppermute | solution.py:183
  31.3 0.1 collective-permute-start.13
  31.4 1.7 %collective-permute-start.14 = (bf16[4,1,2,2,2,16,128]{6,5,4,3,2,1,0:T(8,128)(2,1)S(1)}, bf16[4,1,2,2,2,16,128]{6,5,4,3,2,1,0:T(8,128)(2,1)S(1)}, u32[]{:S(2)}, u32[]{:S(2)}) collective-permute-start(bf16[4,1,2,2,2,16,128]{6,5,4,3,2,1,0:T(8,128)(2,1)S(1)} %pad_maximum_fusion.4), channel_id=1, source_target_pairs={{0,16},{8,24},{16,0},{24,8},{1,17},{9,25},{17,1},{25,9},{2,18},{10... | collective-permute-start | bytes 393224 | tf_op jit(solution)/shard_map/ppermute | solution.py:180
  33.2 0.3 collective-permute-start.15
  33.4 4.3 %collective-permute-start.4 = (bf16[4,1,2,2,2,16,128]{6,5,4,3,2,1,0:T(8,128)(2,1)S(1)}, bf16[4,1,2,2,2,16,128]{6,5,4,3,2,1,0:T(8,128)(2,1)S(1)}, u32[]{:S(2)}, u32[]{:S(2)}) collective-permute-start(bf16[4,1,2,2,2,16,128]{6,5,4,3,2,1,0:T(8,128)(2,1)S(1)} %pad_maximum_fusion.1), channel_id=1, source_target_pairs={{0,7},{1,6},{2,5},{3,4},{4,3},{5,2},{6,1},{7,0},{8,15},{9,14},{10,... | collective-permute-start | bytes 393224 | tf_op jit(solution)/shard_map/ppermute | solution.py:183
  37.7 0.1 collective-permute-done.14.rest_10_
  37.8 1.8 %collective-permute-done.15.rest_11_ = bf16[4,1,2,2,2,16,128]{6,5,4,3,2,1,0:T(8,128)(2,1)S(1)} collective-permute-done((bf16[4,1,2,2,2,16,128]{6,5,4,3,2,1,0:T(8,128)(2,1)S(1)}, bf16[4,1,2,2,2,16,128]{6,5,4,3,2,1,0:T(8,128)(2,1)S(1)}, u32[]{:S(2)}, u32[]{:S(2)}) %collective-permute-start.15) | collective-permute-done | bytes 131104 | tf_op jit(solution)/shard_map/ppermute | solution.py:180
  39.7 1.1 %shard_map.40.rest_2_ = bf16[2,8,2,128,128]{4,3,2,1,0:T(8,128)(2,1)} custom-call(bf16[1,1,2,2,2,16,128]{6,5,4,3,2,1,0:T(8,128)(2,1)S(1)} %get-tuple-element.38.rest_0_, bf16[1,1,2,2,2,16,128]{6,5,4,3,2,1,0:T(8,128)(2,1)S(1)} %get-tuple-element.42.rest_1_, bf16[1,1,2,2,2,16,128]{6,5,4,3,2,1,0:T(8,128)(2,1)S(1)} %get-tuple-element.46.rest_2_, ...), custom_call_target="tpu_custom_call" | custom-call | tf_op jit(solution)/shard_map/pallas_call | solution.py:153
  40.8 1.2 %collective-permute-done.4.rest_1_ = bf16[4,1,2,2,2,16,128]{6,5,4,3,2,1,0:T(8,128)(2,1)S(1)} collective-permute-done((bf16[4,1,2,2,2,16,128]{6,5,4,3,2,1,0:T(8,128)(2,1)S(1)}, bf16[4,1,2,2,2,16,128]{6,5,4,3,2,1,0:T(8,128)(2,1)S(1)}, u32[]{:S(2)}, u32[]{:S(2)}) %collective-permute-start.4) | collective-permute-done | bytes 131104 | tf_op jit(solution)/shard_map/ppermute | solution.py:183
  42.0 0.8 %shard_map.41 = bf16[2,8,2,128,128]{4,3,2,1,0:T(8,128)(2,1)} custom-call(bf16[4,1,2,2,2,16,128]{6,5,4,3,2,1,0:T(8,128)(2,1)S(1)} %collective-permute-done.3.rest_0_, bf16[4,1,2,2,2,16,128]{6,5,4,3,2,1,0:T(8,128)(2,1)S(1)} %collective-permute-done.4.rest_1_, bf16[2,8,2,128,128]{4,3,2,1,0:T(8,128)(2,1)} %shard_map.40.rest_2_), custom_call_target="tpu_custom_call", output_to_operand_aliasing={{}: (2, {})} | custom-call | tf_op jit(solution)/shard_map/pallas_call | solution.py:153
  (27 shorter events, 0.2 us)
Async XLA Ops:
  2.4 11.1 %collective-permute-start = (bf16[2,1,2,2,2,16,128]{6,5,4,3,2,1,0:T(8,128)(2,1)S(1)}, bf16[2,1,2,2,2,16,128]{6,5,4,3,2,1,0:T(8,128)(2,1)S(1)}, u32[]{:S(2)}, u32[]{:S(2)}) collective-permute-start(bf16[2,1,2,2,2,16,128]{6,5,4,3,2,1,0:T(8,128)(2,1)S(1)} %get-tuple-element.24), channel_id=1, source_target_pairs={{0,8},{8,0},{16,24},{24,16},{1,9},{9,1},{17,25},{25,17},{2,10},{10... | collective-permute-start | bytes 196616 | tf_op jit(solution)/shard_map/ppermute | solution.py:180
  2.9 10.7 %collective-permute-start.1 = (bf16[2,1,2,2,2,16,128]{6,5,4,3,2,1,0:T(8,128)(2,1)S(1)}, bf16[2,1,2,2,2,16,128]{6,5,4,3,2,1,0:T(8,128)(2,1)S(1)}, u32[]{:S(2)}, u32[]{:S(2)}) collective-permute-start(bf16[2,1,2,2,2,16,128]{6,5,4,3,2,1,0:T(8,128)(2,1)S(1)} %get-tuple-element.25), channel_id=1, source_target_pairs={{0,16},{8,24},{16,0},{24,8},{1,17},{9,25},{17,1},{25,9},{2,18},{10... | collective-permute-start | bytes 196616 | tf_op jit(solution)/shard_map/ppermute | solution.py:180
  5.5 9.7 %collective-permute-start.2 = (bf16[2,1,2,2,2,16,128]{6,5,4,3,2,1,0:T(8,128)(2,1)S(1)}, bf16[2,1,2,2,2,16,128]{6,5,4,3,2,1,0:T(8,128)(2,1)S(1)}, u32[]{:S(2)}, u32[]{:S(2)}) collective-permute-start(bf16[2,1,2,2,2,16,128]{6,5,4,3,2,1,0:T(8,128)(2,1)S(1)} %get-tuple-element.26), channel_id=1, source_target_pairs={{0,24},{8,16},{16,8},{24,0},{1,25},{9,17},{17,9},{25,1},{2,26},{10... | collective-permute-start | bytes 196616 | tf_op jit(solution)/shard_map/ppermute | solution.py:180
  7.3 15.6 %collective-permute-start.7 = (bf16[4,1,2,2,2,16,128]{6,5,4,3,2,1,0:T(8,128)(2,1)S(1)}, bf16[4,1,2,2,2,16,128]{6,5,4,3,2,1,0:T(8,128)(2,1)S(1)}, u32[]{:S(2)}, u32[]{:S(2)}) collective-permute-start(bf16[4,1,2,2,2,16,128]{6,5,4,3,2,1,0:T(8,128)(2,1)S(1)} %get-tuple-element.29), channel_id=1, source_target_pairs={{0,4},{1,5},{2,6},{3,7},{4,0},{5,1},{6,2},{7,3},{8,12},{9,13},{10,... | collective-permute-start | bytes 393224 | tf_op jit(solution)/shard_map/ppermute | solution.py:183
  10.2 13.8 %collective-permute-start.8 = (bf16[4,1,2,2,2,16,128]{6,5,4,3,2,1,0:T(8,128)(2,1)S(1)}, bf16[4,1,2,2,2,16,128]{6,5,4,3,2,1,0:T(8,128)(2,1)S(1)}, u32[]{:S(2)}, u32[]{:S(2)}) collective-permute-start(bf16[4,1,2,2,2,16,128]{6,5,4,3,2,1,0:T(8,128)(2,1)S(1)} %get-tuple-element.30), channel_id=1, source_target_pairs={{0,5},{1,4},{2,7},{3,6},{4,1},{5,0},{6,3},{7,2},{8,13},{9,12},{10,... | collective-permute-start | bytes 393224 | tf_op jit(solution)/shard_map/ppermute | solution.py:183
  13.5 2.1 %collective-permute-start.9 = (bf16[2,1,2,2,2,16,128]{6,5,4,3,2,1,0:T(8,128)(2,1)S(1)}, bf16[2,1,2,2,2,16,128]{6,5,4,3,2,1,0:T(8,128)(2,1)S(1)}, u32[]{:S(2)}, u32[]{:S(2)}) collective-permute-start(bf16[2,1,2,2,2,16,128]{6,5,4,3,2,1,0:T(8,128)(2,1)S(1)} %get-tuple-element.32), channel_id=1, source_target_pairs={{0,8},{8,0},{16,24},{24,16},{1,9},{9,1},{17,25},{25,17},{2,10},{10... | collective-permute-start | bytes 196616 | tf_op jit(solution)/shard_map/ppermute | solution.py:180
  13.6 4.5 %collective-permute-start.10 = (bf16[2,1,2,2,2,16,128]{6,5,4,3,2,1,0:T(8,128)(2,1)S(1)}, bf16[2,1,2,2,2,16,128]{6,5,4,3,2,1,0:T(8,128)(2,1)S(1)}, u32[]{:S(2)}, u32[]{:S(2)}) collective-permute-start(bf16[2,1,2,2,2,16,128]{6,5,4,3,2,1,0:T(8,128)(2,1)S(1)} %get-tuple-element.33), channel_id=1, source_target_pairs={{0,16},{8,24},{16,0},{24,8},{1,17},{9,25},{17,1},{25,9},{2,18},{10... | collective-permute-start | bytes 196616 | tf_op jit(solution)/shard_map/ppermute | solution.py:180
  15.2 4.5 %collective-permute-start.11 = (bf16[2,1,2,2,2,16,128]{6,5,4,3,2,1,0:T(8,128)(2,1)S(1)}, bf16[2,1,2,2,2,16,128]{6,5,4,3,2,1,0:T(8,128)(2,1)S(1)}, u32[]{:S(2)}, u32[]{:S(2)}) collective-permute-start(bf16[2,1,2,2,2,16,128]{6,5,4,3,2,1,0:T(8,128)(2,1)S(1)} %get-tuple-element.34), channel_id=1, source_target_pairs={{0,24},{8,16},{16,8},{24,0},{1,25},{9,17},{17,9},{25,1},{2,26},{10... | collective-permute-start | bytes 196616 | tf_op jit(solution)/shard_map/ppermute | solution.py:180
  15.6 9.9 %collective-permute-start.5 = (bf16[4,1,2,2,2,16,128]{6,5,4,3,2,1,0:T(8,128)(2,1)S(1)}, bf16[4,1,2,2,2,16,128]{6,5,4,3,2,1,0:T(8,128)(2,1)S(1)}, u32[]{:S(2)}, u32[]{:S(2)}) collective-permute-start(bf16[4,1,2,2,2,16,128]{6,5,4,3,2,1,0:T(8,128)(2,1)S(1)} %get-tuple-element.27), channel_id=1, source_target_pairs={{0,2},{1,3},{2,0},{3,1},{4,6},{5,7},{6,4},{7,5},{8,10},{9,11},{10,... | collective-permute-start | bytes 393224 | tf_op jit(solution)/shard_map/ppermute | solution.py:183
  18.1 13.1 %collective-permute-start.6 = (bf16[4,1,2,2,2,16,128]{6,5,4,3,2,1,0:T(8,128)(2,1)S(1)}, bf16[4,1,2,2,2,16,128]{6,5,4,3,2,1,0:T(8,128)(2,1)S(1)}, u32[]{:S(2)}, u32[]{:S(2)}) collective-permute-start(bf16[4,1,2,2,2,16,128]{6,5,4,3,2,1,0:T(8,128)(2,1)S(1)} %get-tuple-element.28), channel_id=1, source_target_pairs={{0,3},{1,2},{2,1},{3,0},{4,7},{5,6},{6,5},{7,4},{8,11},{9,10},{10,... | collective-permute-start | bytes 393224 | tf_op jit(solution)/shard_map/ppermute | solution.py:183
  19.7 21.1 %collective-permute-start.3 = (bf16[4,1,2,2,2,16,128]{6,5,4,3,2,1,0:T(8,128)(2,1)S(1)}, bf16[4,1,2,2,2,16,128]{6,5,4,3,2,1,0:T(8,128)(2,1)S(1)}, u32[]{:S(2)}, u32[]{:S(2)}) collective-permute-start(bf16[4,1,2,2,2,16,128]{6,5,4,3,2,1,0:T(8,128)(2,1)S(1)} %pad_maximum_fusion), channel_id=1, source_target_pairs={{0,6},{1,7},{2,4},{3,5},{4,2},{5,3},{6,0},{7,1},{8,14},{9,15},{10,... | collective-permute-start | bytes 393224 | tf_op jit(solution)/shard_map/ppermute | solution.py:183
  22.9 10.6 %collective-permute-start.12 = (bf16[4,1,2,2,2,16,128]{6,5,4,3,2,1,0:T(8,128)(2,1)S(1)}, bf16[4,1,2,2,2,16,128]{6,5,4,3,2,1,0:T(8,128)(2,1)S(1)}, u32[]{:S(2)}, u32[]{:S(2)}) collective-permute-start(bf16[4,1,2,2,2,16,128]{6,5,4,3,2,1,0:T(8,128)(2,1)S(1)} %pad_maximum_fusion.2), channel_id=1, source_target_pairs={{0,1},{1,0},{2,3},{3,2},{4,5},{5,4},{6,7},{7,6},{8,9},{9,8},{10,11... | collective-permute-start | bytes 393224 | tf_op jit(solution)/shard_map/ppermute | solution.py:183
  31.3 6.4 %collective-permute-start.13 = (bf16[4,1,2,2,2,16,128]{6,5,4,3,2,1,0:T(8,128)(2,1)S(1)}, bf16[4,1,2,2,2,16,128]{6,5,4,3,2,1,0:T(8,128)(2,1)S(1)}, u32[]{:S(2)}, u32[]{:S(2)}) collective-permute-start(bf16[4,1,2,2,2,16,128]{6,5,4,3,2,1,0:T(8,128)(2,1)S(1)} %pad_maximum_fusion.3), channel_id=1, source_target_pairs={{0,8},{8,0},{16,24},{24,16},{1,9},{9,1},{17,25},{25,17},{2,10},{10... | collective-permute-start | bytes 393224 | tf_op jit(solution)/shard_map/ppermute | solution.py:180
  31.4 6.4 %collective-permute-start.14 = (bf16[4,1,2,2,2,16,128]{6,5,4,3,2,1,0:T(8,128)(2,1)S(1)}, bf16[4,1,2,2,2,16,128]{6,5,4,3,2,1,0:T(8,128)(2,1)S(1)}, u32[]{:S(2)}, u32[]{:S(2)}) collective-permute-start(bf16[4,1,2,2,2,16,128]{6,5,4,3,2,1,0:T(8,128)(2,1)S(1)} %pad_maximum_fusion.4), channel_id=1, source_target_pairs={{0,16},{8,24},{16,0},{24,8},{1,17},{9,25},{17,1},{25,9},{2,18},{10... | collective-permute-start | bytes 393224 | tf_op jit(solution)/shard_map/ppermute | solution.py:180
  33.2 6.5 %collective-permute-start.15 = (bf16[4,1,2,2,2,16,128]{6,5,4,3,2,1,0:T(8,128)(2,1)S(1)}, bf16[4,1,2,2,2,16,128]{6,5,4,3,2,1,0:T(8,128)(2,1)S(1)}, u32[]{:S(2)}, u32[]{:S(2)}) collective-permute-start(bf16[4,1,2,2,2,16,128]{6,5,4,3,2,1,0:T(8,128)(2,1)S(1)} %pad_maximum_fusion.5), channel_id=1, source_target_pairs={{0,24},{8,16},{16,8},{24,0},{1,25},{9,17},{17,9},{25,1},{2,26},{10... | collective-permute-start | bytes 393224 | tf_op jit(solution)/shard_map/ppermute | solution.py:180
  33.4 8.6 %collective-permute-start.4 = (bf16[4,1,2,2,2,16,128]{6,5,4,3,2,1,0:T(8,128)(2,1)S(1)}, bf16[4,1,2,2,2,16,128]{6,5,4,3,2,1,0:T(8,128)(2,1)S(1)}, u32[]{:S(2)}, u32[]{:S(2)}) collective-permute-start(bf16[4,1,2,2,2,16,128]{6,5,4,3,2,1,0:T(8,128)(2,1)S(1)} %pad_maximum_fusion.1), channel_id=1, source_target_pairs={{0,7},{1,6},{2,5},{3,4},{4,3},{5,2},{6,1},{7,0},{8,15},{9,14},{10,... | collective-permute-start | bytes 393224 | tf_op jit(solution)/shard_map/ppermute | solution.py:183

commit v2 on v1

--- a/solution.py
+++ b/solution.py
@@ -130,7 +130,10 @@
     def copies():
         n = 0
         for piece_ref, entry in zip(pieces, plan):
-            for slot, (j, k) in enumerate(entry):
+            for slot, offset in enumerate(entry):
+                if offset is None:
+                    continue
+                j, k = offset
                 for r in range(rounds):
                     pair = pl.ds((layer ^ j) * 2, 2)
                     rows = pl.ds(pl.multiple_of(((tok ^ k) * rounds + r) * PAGE, PAGE), PAGE)
@@ -164,16 +167,15 @@
 
 def offsets_of(groups, tok_count):
     half, quarter = tok_count // 2, tok_count // 4
-    small = list(range(quarter))
-    middle = list(range(quarter, half))
+    near = list(range(half))
     early = list(range(half, half + quarter))
     late = list(range(half + quarter, tok_count))
-    return list(range(groups - 1, 0, -1)), small, middle, early, late
+    return list(range(groups - 1, 0, -1)), near, early, late
 
 
 def one_sequence(values, keep, lengths, groups, tok_count):
     rows_dev = values.shape[2]
-    _, small, middle, early, late = offsets_of(groups, tok_count)
+    _, near, early, late = offsets_of(groups, tok_count)
     layers = range(groups)
 
     def over_layer(array, j):
@@ -188,39 +190,34 @@
     def merge_into(plan, limits):
         return merged(values, keep, limits, plan, groups, tok_count)
 
-    def without_padding(array, k):
+    def without_padding(array, k, source):
         rounds = array.shape[1]
-        tok = lax.axis_index("tok")
-        first = (tok ^ k) * rows_dev + tok * PAGE
+        first = source * rows_dev + (source ^ k) * PAGE
         shape = (1, rounds, 1, 1, 1, PAGE, HD)
         position = first + lax.broadcasted_iota(jnp.int32, shape, 5)
         position += lax.broadcasted_iota(jnp.int32, shape, 1) * (PAGE * tok_count)
         return jnp.where(position < lengths[0], array, jnp.zeros_like(array))
 
-    first = merge_into([[(j, k) for j in layers] for k in early], [])
+    tok = lax.axis_index("tok")
+    first = merge_into([[(j, k) for j in layers] for k in early] + [[(j, k) for k in late] for j in layers], [])
     lengths, first = lax.optimization_barrier((lengths, first))
-    second = merge_into([[(j, k) for k in late] for j in layers], [lengths])
-    third = merge_into(
-        [[(j, k) for j in layers] for k in middle] + [[(j, k) for k in small] for j in layers], [lengths]
-    )
-    early_in = [without_padding(over_tok(array, k), k) for array, k in zip(first, early)]
-    late_mine = [second[0]] + [over_layer(second[j], j) for j in layers if j]
-    middle_in = [over_tok(array, k) for array, k in zip(third, middle)]
-    small_mine = third[len(middle) :]
-    small_mine = [small_mine[0]] + [over_layer(small_mine[j], j) for j in layers if j]
-    late_in = [over_tok(joined(late_mine, n), k) for n, k in enumerate(late)]
-    small_in = [over_tok(joined(small_mine, n), k) for n, k in enumerate(small) if k]
-    relayed = middle + early
-    relayed_mine = [over_layer(joined(middle_in + early_in, j), j) for j in layers if j]
+    second = merge_into([[(j, k) for k in near] for j in layers], [lengths])
+    early_in = [over_tok(array, k) for array, k in zip(first, early)]
+    early_in = [without_padding(array, k, tok ^ k) for array, k in zip(early_in, early)]
+    late_mine = first[len(early) :]
+    late_mine = [late_mine[0]] + [over_layer(late_mine[j], j) for j in layers if j]
+    near_mine = [second[0]] + [over_layer(second[j], j) for j in layers if j]
+    late_in = [over_tok(without_padding(joined(late_mine, n), k, tok), k) for n, k in enumerate(late)]
+    early_mine = [over_layer(joined(early_in, j), j) for j in layers if j]
+    near_in = [over_tok(joined(near_mine, n), k) for n, k in enumerate(near) if k]
     out = placed(
-        [(array[:1], [(0, k)]) for array, k in zip(middle_in + early_in, relayed)]
-        + [(array[:1], [(j, 0)]) for array, j in zip(small_mine, layers)]
-        + [(array, [(j, k) for j in layers]) for array, k in zip(small_in, small[1:])]
-        + [(array, [(j, k) for k in relayed]) for array, j in zip(relayed_mine, layers[1:])],
+        [(array[:1], [(0, k)]) for array, k in zip(early_in, early)]
+        + [(array[:1], [(j, 0)]) for array, j in zip(near_mine, layers)]
+        + [(array, [(j, k) for k in early]) for array, j in zip(early_mine, layers[1:])],
         groups, rows_dev,
     )
     return placed(
-        [(array, [(j, k) for j in layers]) for array, k in zip(late_in, late)],
+        [(array, [(j, k) for j in layers]) for array, k in zip(late_in + near_in, late + near[1:])],
         groups, rows_dev, before=out,
     )
 

time: 43.1 us -> 48 us (1.11)
  waiting for transfers between devices: 11.3 us -> 18.7 us
  Pallas kernels: 7.22 us -> 5.75 us
  starting transfers between devices: 23 us -> 21.9 us
    ppermute x7, waiting for transfers between devices: 8.39 us -> 12.9 us  [over_tok(): return lax.ppermute(array, 'tok', [(i, i ^ k) for i in range(tok_count)])]
    ppermute x9, waiting for transfers between devices: 2.91 us -> 5.84 us  [over_layer(): return lax.ppermute(array, 'layer', [(i, i ^ j) for i in range(groups)])]
    ppermute x7, starting transfers between devices: 15.8 us -> 13.8 us  [over_tok(): return lax.ppermute(array, 'tok', [(i, i ^ k) for i in range(tok_count)])]
    pallas_call x3 -> x2, Pallas kernels: 5.39 us -> 3.92 us  [merged(): pl.pallas_call(functools.partial(merge_kernel, plan=plan, groups=groups,...]
    ppermute x9, starting transfers between devices: 7.23 us -> 8.12 us  [over_layer(): return lax.ppermute(array, 'layer', [(i, i ^ j) for i in range(groups)])]
  transfers between devices with their start and end apart: 16 -> 16, of which waited for: 6 -> 6; matrix products, arithmetic and copies ran while one was open for 1% -> 1% of each run, Pallas kernels for 11% -> 6%
where the time goes in v2:
time: 48 us; the launch traced here: 47.8 us
  starting transfers between devices  21.9 us (46%)
  waiting for transfers between devices  18.7 us (39%)
  Pallas kernels  5.75 us (12%)
  between operations  0.91 us (2%)
    ppermute x7, starting transfers between devices, over_tok(): return lax.ppermute(array, 'tok', [(i, i ^ k) for i in range(tok_count)])  13.8 us
    ppermute x7, waiting for transfers between devices, over_tok(): return lax.ppermute(array, 'tok', [(i, i ^ k) for i in range(tok_count)])  12.9 us
    ppermute x9, starting transfers between devices, over_layer(): return lax.ppermute(array, 'layer', [(i, i ^ j) for i in range(groups)])  8.12 us
    ppermute x9, waiting for transfers between devices, over_layer(): return lax.ppermute(array, 'layer', [(i, i ^ j) for i in range(groups)])  5.84 us
    pallas_call x2, Pallas kernels, merged(): pl.pallas_call(functools.partial(merge_kernel, plan=plan, groups=groups,...  3.92 us
    pallas_call x2, Pallas kernels, placed(): pl.pallas_call(functools.partial(place_kernel, plan=plan, rounds=rounds,...  1.83 us
  transfers between devices with their start and end apart: 16, of which 6 were waited for; matrix products, arithmetic and copies ran while one was open for 1% of the time, Pallas kernels for 6%

profile of v2, /device:TPU:0, one launch (start us, length us, event | category | flops | bytes accessed | tf_op | source)
XLA Modules:
  0.0 47.8 jit_solution(1517454351834818434)
XLA Ops:
  0.7 2.0 %shard_map.38 = (bf16[4,1,2,2,2,16,128]{6,5,4,3,2,1,0:T(8,128)(2,1)S(1)}, bf16[4,1,2,2,2,16,128]{6,5,4,3,2,1,0:T(8,128)(2,1)S(1)}, bf16[4,1,2,2,2,16,128]{6,5,4,...) custom-call(s32[1]{0:T(128)} %copy.6.refs_0_, s32[1,128]{1,0:T(1,128)} %bitcast.10, bf16[2,2,128,1024]{3,2,1,0:T(8,128)(2,1)} %bitcast.8), custom_call_target="tpu_custom_call" | custom-call | tf_op jit(solution)/shard_map/pallas_call | solution.py:102
  2.6 0.6 %collective-permute-start.5 = (bf16[4,1,2,2,2,16,128]{6,5,4,3,2,1,0:T(8,128)(2,1)S(1)}, bf16[4,1,2,2,2,16,128]{6,5,4,3,2,1,0:T(8,128)(2,1)S(1)}, u32[]{:S(2)}, u32[]{:S(2)}) collective-permute-start(bf16[4,1,2,2,2,16,128]{6,5,4,3,2,1,0:T(8,128)(2,1)S(1)} %get-tuple-element.34), channel_id=1, source_target_pairs={{0,8},{8,0},{16,24},{24,16},{1,9},{9,1},{17,25},{25,17},{2,10},{10... | collective-permute-start | bytes 393224 | tf_op jit(solution)/shard_map/ppermute | solution.py:182
  3.2 2.6 %collective-permute-start.6 = (bf16[4,1,2,2,2,16,128]{6,5,4,3,2,1,0:T(8,128)(2,1)S(1)}, bf16[4,1,2,2,2,16,128]{6,5,4,3,2,1,0:T(8,128)(2,1)S(1)}, u32[]{:S(2)}, u32[]{:S(2)}) collective-permute-start(bf16[4,1,2,2,2,16,128]{6,5,4,3,2,1,0:T(8,128)(2,1)S(1)} %get-tuple-element.35), channel_id=1, source_target_pairs={{0,16},{8,24},{16,0},{24,8},{1,17},{9,25},{17,1},{25,9},{2,18},{10... | collective-permute-start | bytes 393224 | tf_op jit(solution)/shard_map/ppermute | solution.py:182
  5.7 0.0 collective-permute-start.7
  5.8 2.0 %shard_map.37 = (bf16[4,1,2,2,2,16,128]{6,5,4,3,2,1,0:T(8,128)(2,1)S(1)}, bf16[4,1,2,2,2,16,128]{6,5,4,3,2,1,0:T(8,128)(2,1)S(1)}, bf16[2,1,2,2,2,16,128]{6,5,4,...) custom-call(s32[1,128]{1,0:T(1,128)} %bitcast.11, ...), custom_call_target="tpu_custom_call" | custom-call | tf_op jit(solution)/shard_map/pallas_call | solution.py:102
  7.7 0.2 collective-permute-start
  8.0 1.9 %collective-permute-start.1 = (bf16[2,1,2,2,2,16,128]{6,5,4,3,2,1,0:T(8,128)(2,1)S(1)}, bf16[2,1,2,2,2,16,128]{6,5,4,3,2,1,0:T(8,128)(2,1)S(1)}, u32[]{:S(2)}, u32[]{:S(2)}) collective-permute-start(bf16[2,1,2,2,2,16,128]{6,5,4,3,2,1,0:T(8,128)(2,1)S(1)} %get-tuple-element.31), channel_id=1, source_target_pairs={{0,16},{8,24},{16,0},{24,8},{1,17},{9,25},{17,1},{25,9},{2,18},{10... | collective-permute-start | bytes 196616 | tf_op jit(solution)/shard_map/ppermute | solution.py:182
  10.0 0.0 collective-permute-done
  10.0 0.8 %collective-permute-start.2 = (bf16[2,1,2,2,2,16,128]{6,5,4,3,2,1,0:T(8,128)(2,1)S(1)}, bf16[2,1,2,2,2,16,128]{6,5,4,3,2,1,0:T(8,128)(2,1)S(1)}, u32[]{:S(2)}, u32[]{:S(2)}) collective-permute-start(bf16[2,1,2,2,2,16,128]{6,5,4,3,2,1,0:T(8,128)(2,1)S(1)} %get-tuple-element.32), channel_id=1, source_target_pairs={{0,24},{8,16},{16,8},{24,0},{1,25},{9,17},{17,9},{25,1},{2,26},{10... | collective-permute-start | bytes 196616 | tf_op jit(solution)/shard_map/ppermute | solution.py:182
  10.8 3.5 %collective-permute-done.1 = bf16[2,1,2,2,2,16,128]{6,5,4,3,2,1,0:T(8,128)(2,1)S(1)} collective-permute-done((bf16[2,1,2,2,2,16,128]{6,5,4,3,2,1,0:T(8,128)(2,1)S(1)}, bf16[2,1,2,2,2,16,128]{6,5,4,3,2,1,0:T(8,128)(2,1)S(1)}, u32[]{:S(2)}, u32[]{:S(2)}) %collective-permute-start.1) | collective-permute-done | bytes 65568 | tf_op jit(solution)/shard_map/ppermute | solution.py:182
  14.3 3.1 %collective-permute-start.11 = (bf16[4,1,2,2,2,16,128]{6,5,4,3,2,1,0:T(8,128)(2,1)S(1)}, bf16[4,1,2,2,2,16,128]{6,5,4,3,2,1,0:T(8,128)(2,1)S(1)}, u32[]{:S(2)}, u32[]{:S(2)}) collective-permute-start(bf16[4,1,2,2,2,16,128]{6,5,4,3,2,1,0:T(8,128)(2,1)S(1)} %get-tuple-element.37), channel_id=1, source_target_pairs={{0,4},{1,5},{2,6},{3,7},{4,0},{5,1},{6,2},{7,3},{8,12},{9,13},{10,... | collective-permute-start | bytes 393224 | tf_op jit(solution)/shard_map/ppermute | solution.py:185
  17.4 1.4 %collective-permute-start.12 = (bf16[4,1,2,2,2,16,128]{6,5,4,3,2,1,0:T(8,128)(2,1)S(1)}, bf16[4,1,2,2,2,16,128]{6,5,4,3,2,1,0:T(8,128)(2,1)S(1)}, u32[]{:S(2)}, u32[]{:S(2)}) collective-permute-start(bf16[4,1,2,2,2,16,128]{6,5,4,3,2,1,0:T(8,128)(2,1)S(1)} %get-tuple-element.38), channel_id=1, source_target_pairs={{0,5},{1,4},{2,7},{3,6},{4,1},{5,0},{6,3},{7,2},{8,13},{9,12},{10,... | collective-permute-start | bytes 393224 | tf_op jit(solution)/shard_map/ppermute | solution.py:185
  18.8 0.1 maximum_select_fusion.1
  18.9 0.1 maximum_select_fusion
  19.0 7.9 %collective-permute-done.11 = bf16[4,1,2,2,2,16,128]{6,5,4,3,2,1,0:T(8,128)(2,1)S(1)} collective-permute-done((bf16[4,1,2,2,2,16,128]{6,5,4,3,2,1,0:T(8,128)(2,1)S(1)}, bf16[4,1,2,2,2,16,128]{6,5,4,3,2,1,0:T(8,128)(2,1)S(1)}, u32[]{:S(2)}, u32[]{:S(2)}) %collective-permute-start.11) | collective-permute-done | bytes 131104 | tf_op jit(solution)/shard_map/ppermute | solution.py:185
  26.9 2.9 %collective-permute-start.3 = (bf16[4,1,2,2,2,16,128]{6,5,4,3,2,1,0:T(8,128)(2,1)S(1)}, bf16[4,1,2,2,2,16,128]{6,5,4,3,2,1,0:T(8,128)(2,1)S(1)}, u32[]{:S(2)}, u32[]{:S(2)}) collective-permute-start(bf16[4,1,2,2,2,16,128]{6,5,4,3,2,1,0:T(8,128)(2,1)S(1)} %maximum_select_fusion), channel_id=1, source_target_pairs={{0,6},{1,7},{2,4},{3,5},{4,2},{5,3},{6,0},{7,1},{8,14},{9,15},{10,... | collective-permute-start | bytes 393224 | tf_op jit(solution)/shard_map/ppermute | solution.py:185
  29.8 0.1 broadcast_select_fusion.1
  29.9 3.6 %collective-permute-start.4 = (bf16[4,1,2,2,2,16,128]{6,5,4,3,2,1,0:T(8,128)(2,1)S(1)}, bf16[4,1,2,2,2,16,128]{6,5,4,3,2,1,0:T(8,128)(2,1)S(1)}, u32[]{:S(2)}, u32[]{:S(2)}) collective-permute-start(bf16[4,1,2,2,2,16,128]{6,5,4,3,2,1,0:T(8,128)(2,1)S(1)} %maximum_select_fusion.1), channel_id=1, source_target_pairs={{0,7},{1,6},{2,5},{3,4},{4,3},{5,2},{6,1},{7,0},{8,15},{9,14},{10,... | collective-permute-start | bytes 393224 | tf_op jit(solution)/shard_map/ppermute | solution.py:185
  33.5 0.1 broadcast_select_fusion
  33.6 0.0 collective-permute-done.5
  33.6 0.1 collective-permute-start.13
  33.8 1.6 %collective-permute-start.14 = (bf16[2,1,2,2,2,16,128]{6,5,4,3,2,1,0:T(8,128)(2,1)S(1)}, bf16[2,1,2,2,2,16,128]{6,5,4,3,2,1,0:T(8,128)(2,1)S(1)}, u32[]{:S(2)}, u32[]{:S(2)}) collective-permute-start(bf16[2,1,2,2,2,16,128]{6,5,4,3,2,1,0:T(8,128)(2,1)S(1)} %pad_maximum_fusion.4), channel_id=1, source_target_pairs={{0,16},{8,24},{16,0},{24,8},{1,17},{9,25},{17,1},{25,9},{2,18},{10... | collective-permute-start | bytes 196616 | tf_op jit(solution)/shard_map/ppermute | solution.py:182
  35.4 0.4 collective-permute-start.15
  35.9 1.2 %collective-permute-start.8 = (bf16[4,1,2,2,2,16,128]{6,5,4,3,2,1,0:T(8,128)(2,1)S(1)}, bf16[4,1,2,2,2,16,128]{6,5,4,3,2,1,0:T(8,128)(2,1)S(1)}, u32[]{:S(2)}, u32[]{:S(2)}) collective-permute-start(bf16[4,1,2,2,2,16,128]{6,5,4,3,2,1,0:T(8,128)(2,1)S(1)} %pad_maximum_fusion), channel_id=1, source_target_pairs={{0,1},{1,0},{2,3},{3,2},{4,5},{5,4},{6,7},{7,6},{8,9},{9,8},{10,11... | collective-permute-start | bytes 393224 | tf_op jit(solution)/shard_map/ppermute | solution.py:185
  37.1 1.2 %collective-permute-done.14.rest_7_ = bf16[2,1,2,2,2,16,128]{6,5,4,3,2,1,0:T(8,128)(2,1)S(1)} collective-permute-done((bf16[2,1,2,2,2,16,128]{6,5,4,3,2,1,0:T(8,128)(2,1)S(1)}, bf16[2,1,2,2,2,16,128]{6,5,4,3,2,1,0:T(8,128)(2,1)S(1)}, u32[]{:S(2)}, u32[]{:S(2)}) %collective-permute-start.14) | collective-permute-done | bytes 65568 | tf_op jit(solution)/shard_map/ppermute | solution.py:182
  38.3 0.0 collective-permute-start.9
  38.3 1.1 %collective-permute-done.15.rest_8_ = bf16[2,1,2,2,2,16,128]{6,5,4,3,2,1,0:T(8,128)(2,1)S(1)} collective-permute-done((bf16[2,1,2,2,2,16,128]{6,5,4,3,2,1,0:T(8,128)(2,1)S(1)}, bf16[2,1,2,2,2,16,128]{6,5,4,3,2,1,0:T(8,128)(2,1)S(1)}, u32[]{:S(2)}, u32[]{:S(2)}) %collective-permute-start.15) | collective-permute-done | bytes 65568 | tf_op jit(solution)/shard_map/ppermute | solution.py:182
  39.4 1.5 %collective-permute-start.10 = (bf16[4,1,2,2,2,16,128]{6,5,4,3,2,1,0:T(8,128)(2,1)S(1)}, bf16[4,1,2,2,2,16,128]{6,5,4,3,2,1,0:T(8,128)(2,1)S(1)}, u32[]{:S(2)}, u32[]{:S(2)}) collective-permute-start(bf16[4,1,2,2,2,16,128]{6,5,4,3,2,1,0:T(8,128)(2,1)S(1)} %pad_maximum_fusion.2), channel_id=1, source_target_pairs={{0,3},{1,2},{2,1},{3,0},{4,7},{5,6},{6,5},{7,4},{8,11},{9,10},{10,... | collective-permute-start | bytes 393224 | tf_op jit(solution)/shard_map/ppermute | solution.py:185
  41.0 0.8 %shard_map.39.rest_5_ = bf16[2,8,2,128,128]{4,3,2,1,0:T(8,128)(2,1)} custom-call(bf16[1,1,2,2,2,16,128]{6,5,4,3,2,1,0:T(8,128)(2,1)S(1)} %get-tuple-element.42.rest_0_, bf16[1,1,2,2,2,16,128]{6,5,4,3,2,1,0:T(8,128)(2,1)S(1)} %get-tuple-element.46.rest_1_, bf16[1,1,2,2,2,16,128]{6,5,4,3,2,1,0:T(8,128)(2,1)S(1)} %get-tuple-element.59.rest_2_, ...), custom_call_target="tpu_custom_call" | custom-call | tf_op jit(solution)/shard_map/pallas_call | solution.py:156
  41.8 1.7 %collective-permute-done.9.rest_3_ = bf16[4,1,2,2,2,16,128]{6,5,4,3,2,1,0:T(8,128)(2,1)S(1)} collective-permute-done((bf16[4,1,2,2,2,16,128]{6,5,4,3,2,1,0:T(8,128)(2,1)S(1)}, bf16[4,1,2,2,2,16,128]{6,5,4,3,2,1,0:T(8,128)(2,1)S(1)}, u32[]{:S(2)}, u32[]{:S(2)}) %collective-permute-start.9) | collective-permute-done | bytes 131104 | tf_op jit(solution)/shard_map/ppermute | solution.py:185
  43.6 3.2 %collective-permute-done.10.rest_4_ = bf16[4,1,2,2,2,16,128]{6,5,4,3,2,1,0:T(8,128)(2,1)S(1)} collective-permute-done((bf16[4,1,2,2,2,16,128]{6,5,4,3,2,1,0:T(8,128)(2,1)S(1)}, bf16[4,1,2,2,2,16,128]{6,5,4,3,2,1,0:T(8,128)(2,1)S(1)}, u32[]{:S(2)}, u32[]{:S(2)}) %collective-permute-start.10) | collective-permute-done | bytes 131104 | tf_op jit(solution)/shard_map/ppermute | solution.py:185
  46.8 1.0 %shard_map.40 = bf16[2,8,2,128,128]{4,3,2,1,0:T(8,128)(2,1)} custom-call(bf16[4,1,2,2,2,16,128]{6,5,4,3,2,1,0:T(8,128)(2,1)S(1)} %collective-permute-done.3.rest_0_, bf16[4,1,2,2,2,16,128]{6,5,4,3,2,1,0:T(8,128)(2,1)S(1)} %collective-permute-done.4.rest_1_, ...), custom_call_target="tpu_custom_call", output_to_operand_aliasing={{}: (5, {})} | custom-call | tf_op jit(solution)/shard_map/pallas_call | solution.py:156
  (28 shorter events, 0.2 us)
Async XLA Ops:
  2.6 31.0 %collective-permute-start.5 = (bf16[4,1,2,2,2,16,128]{6,5,4,3,2,1,0:T(8,128)(2,1)S(1)}, bf16[4,1,2,2,2,16,128]{6,5,4,3,2,1,0:T(8,128)(2,1)S(1)}, u32[]{:S(2)}, u32[]{:S(2)}) collective-permute-start(bf16[4,1,2,2,2,16,128]{6,5,4,3,2,1,0:T(8,128)(2,1)S(1)} %get-tuple-element.34), channel_id=1, source_target_pairs={{0,8},{8,0},{16,24},{24,16},{1,9},{9,1},{17,25},{25,17},{2,10},{10... | collective-permute-start | bytes 393224 | tf_op jit(solution)/shard_map/ppermute | solution.py:182
  3.2 30.6 %collective-permute-start.6 = (bf16[4,1,2,2,2,16,128]{6,5,4,3,2,1,0:T(8,128)(2,1)S(1)}, bf16[4,1,2,2,2,16,128]{6,5,4,3,2,1,0:T(8,128)(2,1)S(1)}, u32[]{:S(2)}, u32[]{:S(2)}) collective-permute-start(bf16[4,1,2,2,2,16,128]{6,5,4,3,2,1,0:T(8,128)(2,1)S(1)} %get-tuple-element.35), channel_id=1, source_target_pairs={{0,16},{8,24},{16,0},{24,8},{1,17},{9,25},{17,1},{25,9},{2,18},{10... | collective-permute-start | bytes 393224 | tf_op jit(solution)/shard_map/ppermute | solution.py:182
  5.7 29.6 %collective-permute-start.7 = (bf16[4,1,2,2,2,16,128]{6,5,4,3,2,1,0:T(8,128)(2,1)S(1)}, bf16[4,1,2,2,2,16,128]{6,5,4,3,2,1,0:T(8,128)(2,1)S(1)}, u32[]{:S(2)}, u32[]{:S(2)}) collective-permute-start(bf16[4,1,2,2,2,16,128]{6,5,4,3,2,1,0:T(8,128)(2,1)S(1)} %get-tuple-element.36), channel_id=1, source_target_pairs={{0,24},{8,16},{16,8},{24,0},{1,25},{9,17},{17,9},{25,1},{2,26},{10... | collective-permute-start | bytes 393224 | tf_op jit(solution)/shard_map/ppermute | solution.py:182
  7.7 2.3 %collective-permute-start = (bf16[2,1,2,2,2,16,128]{6,5,4,3,2,1,0:T(8,128)(2,1)S(1)}, bf16[2,1,2,2,2,16,128]{6,5,4,3,2,1,0:T(8,128)(2,1)S(1)}, u32[]{:S(2)}, u32[]{:S(2)}) collective-permute-start(bf16[2,1,2,2,2,16,128]{6,5,4,3,2,1,0:T(8,128)(2,1)S(1)} %get-tuple-element.30), channel_id=1, source_target_pairs={{0,8},{8,0},{16,24},{24,16},{1,9},{9,1},{17,25},{25,17},{2,10},{10... | collective-permute-start | bytes 196616 | tf_op jit(solution)/shard_map/ppermute | solution.py:182
  8.0 6.3 %collective-permute-start.1 = (bf16[2,1,2,2,2,16,128]{6,5,4,3,2,1,0:T(8,128)(2,1)S(1)}, bf16[2,1,2,2,2,16,128]{6,5,4,3,2,1,0:T(8,128)(2,1)S(1)}, u32[]{:S(2)}, u32[]{:S(2)}) collective-permute-start(bf16[2,1,2,2,2,16,128]{6,5,4,3,2,1,0:T(8,128)(2,1)S(1)} %get-tuple-element.31), channel_id=1, source_target_pairs={{0,16},{8,24},{16,0},{24,8},{1,17},{9,25},{17,1},{25,9},{2,18},{10... | collective-permute-start | bytes 196616 | tf_op jit(solution)/shard_map/ppermute | solution.py:182
  10.0 7.4 %collective-permute-start.2 = (bf16[2,1,2,2,2,16,128]{6,5,4,3,2,1,0:T(8,128)(2,1)S(1)}, bf16[2,1,2,2,2,16,128]{6,5,4,3,2,1,0:T(8,128)(2,1)S(1)}, u32[]{:S(2)}, u32[]{:S(2)}) collective-permute-start(bf16[2,1,2,2,2,16,128]{6,5,4,3,2,1,0:T(8,128)(2,1)S(1)} %get-tuple-element.32), channel_id=1, source_target_pairs={{0,24},{8,16},{16,8},{24,0},{1,25},{9,17},{17,9},{25,1},{2,26},{10... | collective-permute-start | bytes 196616 | tf_op jit(solution)/shard_map/ppermute | solution.py:182
  14.3 12.6 %collective-permute-start.11 = (bf16[4,1,2,2,2,16,128]{6,5,4,3,2,1,0:T(8,128)(2,1)S(1)}, bf16[4,1,2,2,2,16,128]{6,5,4,3,2,1,0:T(8,128)(2,1)S(1)}, u32[]{:S(2)}, u32[]{:S(2)}) collective-permute-start(bf16[4,1,2,2,2,16,128]{6,5,4,3,2,1,0:T(8,128)(2,1)S(1)} %get-tuple-element.37), channel_id=1, source_target_pairs={{0,4},{1,5},{2,6},{3,7},{4,0},{5,1},{6,2},{7,3},{8,12},{9,13},{10,... | collective-permute-start | bytes 393224 | tf_op jit(solution)/shard_map/ppermute | solution.py:185
  17.4 12.5 %collective-permute-start.12 = (bf16[4,1,2,2,2,16,128]{6,5,4,3,2,1,0:T(8,128)(2,1)S(1)}, bf16[4,1,2,2,2,16,128]{6,5,4,3,2,1,0:T(8,128)(2,1)S(1)}, u32[]{:S(2)}, u32[]{:S(2)}) collective-permute-start(bf16[4,1,2,2,2,16,128]{6,5,4,3,2,1,0:T(8,128)(2,1)S(1)} %get-tuple-element.38), channel_id=1, source_target_pairs={{0,5},{1,4},{2,7},{3,6},{4,1},{5,0},{6,3},{7,2},{8,13},{9,12},{10,... | collective-permute-start | bytes 393224 | tf_op jit(solution)/shard_map/ppermute | solution.py:185
  26.9 14.9 %collective-permute-start.3 = (bf16[4,1,2,2,2,16,128]{6,5,4,3,2,1,0:T(8,128)(2,1)S(1)}, bf16[4,1,2,2,2,16,128]{6,5,4,3,2,1,0:T(8,128)(2,1)S(1)}, u32[]{:S(2)}, u32[]{:S(2)}) collective-permute-start(bf16[4,1,2,2,2,16,128]{6,5,4,3,2,1,0:T(8,128)(2,1)S(1)} %maximum_select_fusion), channel_id=1, source_target_pairs={{0,6},{1,7},{2,4},{3,5},{4,2},{5,3},{6,0},{7,1},{8,14},{9,15},{10,... | collective-permute-start | bytes 393224 | tf_op jit(solution)/shard_map/ppermute | solution.py:185
  29.9 11.9 %collective-permute-start.4 = (bf16[4,1,2,2,2,16,128]{6,5,4,3,2,1,0:T(8,128)(2,1)S(1)}, bf16[4,1,2,2,2,16,128]{6,5,4,3,2,1,0:T(8,128)(2,1)S(1)}, u32[]{:S(2)}, u32[]{:S(2)}) collective-permute-start(bf16[4,1,2,2,2,16,128]{6,5,4,3,2,1,0:T(8,128)(2,1)S(1)} %maximum_select_fusion.1), channel_id=1, source_target_pairs={{0,7},{1,6},{2,5},{3,4},{4,3},{5,2},{6,1},{7,0},{8,15},{9,14},{10,... | collective-permute-start | bytes 393224 | tf_op jit(solution)/shard_map/ppermute | solution.py:185
  33.6 2.2 %collective-permute-start.13 = (bf16[2,1,2,2,2,16,128]{6,5,4,3,2,1,0:T(8,128)(2,1)S(1)}, bf16[2,1,2,2,2,16,128]{6,5,4,3,2,1,0:T(8,128)(2,1)S(1)}, u32[]{:S(2)}, u32[]{:S(2)}) collective-permute-start(bf16[2,1,2,2,2,16,128]{6,5,4,3,2,1,0:T(8,128)(2,1)S(1)} %pad_maximum_fusion.3), channel_id=1, source_target_pairs={{0,8},{8,0},{16,24},{24,16},{1,9},{9,1},{17,25},{25,17},{2,10},{10... | collective-permute-start | bytes 196616 | tf_op jit(solution)/shard_map/ppermute | solution.py:182
  33.8 4.6 %collective-permute-start.14 = (bf16[2,1,2,2,2,16,128]{6,5,4,3,2,1,0:T(8,128)(2,1)S(1)}, bf16[2,1,2,2,2,16,128]{6,5,4,3,2,1,0:T(8,128)(2,1)S(1)}, u32[]{:S(2)}, u32[]{:S(2)}) collective-permute-start(bf16[2,1,2,2,2,16,128]{6,5,4,3,2,1,0:T(8,128)(2,1)S(1)} %pad_maximum_fusion.4), channel_id=1, source_target_pairs={{0,16},{8,24},{16,0},{24,8},{1,17},{9,25},{17,1},{25,9},{2,18},{10... | collective-permute-start | bytes 196616 | tf_op jit(solution)/shard_map/ppermute | solution.py:182
  35.4 4.1 %collective-permute-start.15 = (bf16[2,1,2,2,2,16,128]{6,5,4,3,2,1,0:T(8,128)(2,1)S(1)}, bf16[2,1,2,2,2,16,128]{6,5,4,3,2,1,0:T(8,128)(2,1)S(1)}, u32[]{:S(2)}, u32[]{:S(2)}) collective-permute-start(bf16[2,1,2,2,2,16,128]{6,5,4,3,2,1,0:T(8,128)(2,1)S(1)} %pad_maximum_fusion.5), channel_id=1, source_target_pairs={{0,24},{8,16},{16,8},{24,0},{1,25},{9,17},{17,9},{25,1},{2,26},{10... | collective-permute-start | bytes 196616 | tf_op jit(solution)/shard_map/ppermute | solution.py:182
  35.9 5.9 %collective-permute-start.8 = (bf16[4,1,2,2,2,16,128]{6,5,4,3,2,1,0:T(8,128)(2,1)S(1)}, bf16[4,1,2,2,2,16,128]{6,5,4,3,2,1,0:T(8,128)(2,1)S(1)}, u32[]{:S(2)}, u32[]{:S(2)}) collective-permute-start(bf16[4,1,2,2,2,16,128]{6,5,4,3,2,1,0:T(8,128)(2,1)S(1)} %pad_maximum_fusion), channel_id=1, source_target_pairs={{0,1},{1,0},{2,3},{3,2},{4,5},{5,4},{6,7},{7,6},{8,9},{9,8},{10,11... | collective-permute-start | bytes 393224 | tf_op jit(solution)/shard_map/ppermute | solution.py:185
  38.3 5.2 %collective-permute-start.9 = (bf16[4,1,2,2,2,16,128]{6,5,4,3,2,1,0:T(8,128)(2,1)S(1)}, bf16[4,1,2,2,2,16,128]{6,5,4,3,2,1,0:T(8,128)(2,1)S(1)}, u32[]{:S(2)}, u32[]{:S(2)}) collective-permute-start(bf16[4,1,2,2,2,16,128]{6,5,4,3,2,1,0:T(8,128)(2,1)S(1)} %pad_maximum_fusion.1), channel_id=1, source_target_pairs={{0,2},{1,3},{2,0},{3,1},{4,6},{5,7},{6,4},{7,5},{8,10},{9,11},{10,... | collective-permute-start | bytes 393224 | tf_op jit(solution)/shard_map/ppermute | solution.py:185
  39.4 7.3 %collective-permute-start.10 = (bf16[4,1,2,2,2,16,128]{6,5,4,3,2,1,0:T(8,128)(2,1)S(1)}, bf16[4,1,2,2,2,16,128]{6,5,4,3,2,1,0:T(8,128)(2,1)S(1)}, u32[]{:S(2)}, u32[]{:S(2)}) collective-permute-start(bf16[4,1,2,2,2,16,128]{6,5,4,3,2,1,0:T(8,128)(2,1)S(1)} %pad_maximum_fusion.2), channel_id=1, source_target_pairs={{0,3},{1,2},{2,1},{3,0},{4,7},{5,6},{6,5},{7,4},{8,11},{9,10},{10,... | collective-permute-start | bytes 393224 | tf_op jit(solution)/shard_map/ppermute | solution.py:185

commit v3 on v2

v3 whole, which is shorter than its diff:
```python
import functools

import jax
import jax.numpy as jnp
from jax import lax
from jax.experimental import pallas as pl
from jax.experimental.pallas import tpu as pltpu
from jax.sharding import PartitionSpec as P


KVH = 8
HD = 128
PAGE = 16


epsilon = 1e-06

VMEM_GRANT = 16 * 2**20


def merge(lower, upper, retained):
    lower_square = jnp.mean(lower * lower, axis=-1, keepdims=True) + epsilon
    upper_square = jnp.mean(upper * upper, axis=-1, keepdims=True) + epsilon
    lower_inverse = lax.rsqrt(lower_square)
    upper_inverse = lax.rsqrt(upper_square)
    summed = lower * lower_inverse + upper * upper_inverse
    summed_inverse = lax.rsqrt(jnp.mean(summed * summed, axis=-1, keepdims=True) + epsilon)
    direction = summed * summed_inverse
    lower_out = jnp.where(retained, lower, (lower_square * lower_inverse) * direction)
    upper_out = jnp.where(retained, upper, (upper_square * upper_inverse) * direction)
    return lower_out.astype(jnp.bfloat16), upper_out.astype(jnp.bfloat16)


def merge_kernel(keep_ref, values_ref, *rest, plan, always, lower, upper, groups, tok_count, rounds):
    loaded, mask, columns, sems, mask_sem = rest[-5:]
    outs = rest[-5 - len(plan) : -5]
    layer, tok = lax.axis_index("layer"), lax.axis_index("tok")
    rows_dev = values_ref.shape[2]
    head_group = KVH // groups
    width = head_group * HD
    where = {}
    for o, entry in enumerate(plan):
        for n, piece in enumerate(entry):
            where[piece] = (o, n)
    slots = {k: n for n, k in enumerate(always + lower + upper)}

    def copies(k):
        n = slots[k]
        for r in range(rounds):
            source = pl.ds(pl.multiple_of((r * tok_count + (tok ^ k)) * PAGE, PAGE), PAGE)
            yield pltpu.make_async_copy(values_ref.at[:, :, source, :], loaded.at[n, r], sems.at[n, r])

    mask_copy = pltpu.make_async_copy(keep_ref, mask, mask_sem)

    def load(offsets):
        for k in offsets:
            for copy in copies(k):
                copy.start()

    def turn_mask():
        mask_copy.wait()
        for block in range(0, rows_dev, HD):
            keep = (mask[:, block : block + HD] > 0).astype(jnp.float32)
            columns[block : block + HD, :] = jnp.broadcast_to(keep, (HD, HD)).T

    def work(offsets):
        for k in offsets:
            for copy in copies(k):
                copy.wait()
            n = slots[k]
            for r in range(rounds):
                start = pl.multiple_of((r * tok_count + (tok ^ k)) * PAGE, PAGE)
                retained = columns[pl.ds(start, PAGE), :] > 0.0
                for j in range(groups):
                    o, slot = where[(j, k)]
                    for c in range(2):
                        for member in range(head_group):
                            lane = pl.multiple_of((layer ^ j) * width + member * HD, HD)
                            both = merge(
                                loaded[n, r, 0, c, :, pl.ds(lane, HD)].astype(jnp.float32),
                                loaded[n, r, 1, c, :, pl.ds(lane, HD)].astype(jnp.float32),
                                retained,
                            )
                            for side in range(2):
                                outs[o][slot, r, member, side, c] = both[side]

    if always:
        mask_copy.start()
        load(always)
        if lower:
            pl.when(tok < tok_count // 2)(lambda: load(lower))
        turn_mask()
        work(always)
        if lower:
            pl.when(tok < tok_count // 2)(lambda: work(lower))
    if upper:

        @pl.when(tok >= tok_count // 2)
        def _():
            mask_copy.start()
            load(upper)
            turn_mask()
            work(upper)


def merged(values, keep, plan, groups, tok_count, always=(), lower=(), upper=(), before=()):
    rows_dev = values.shape[2]
    rounds = rows_dev // (PAGE * tok_count)
    head_group = KVH // groups
    count = len(always) + len(lower) + len(upper)
    return pl.pallas_call(
        functools.partial(
            merge_kernel, plan=plan, always=tuple(always), lower=tuple(lower), upper=tuple(upper),
            groups=groups, tok_count=tok_count, rounds=rounds,
        ),
        in_specs=[pl.BlockSpec(memory_space=pltpu.HBM)] * 2 + [pl.BlockSpec(memory_space=pltpu.VMEM) for _ in before],
        out_specs=[pl.BlockSpec(memory_space=pltpu.VMEM) for _ in plan],
        out_shape=[
            jax.ShapeDtypeStruct((len(entry), rounds, head_group, 2, 2, PAGE, HD), jnp.bfloat16)
            for entry in plan
        ],
        scratch_shapes=[
            pltpu.VMEM((count, rounds, 2, 2, PAGE, values.shape[3]), jnp.bfloat16),
            pltpu.VMEM((1, rows_dev), jnp.int32),
            pltpu.VMEM((rows_dev, HD), jnp.float32),
            pltpu.SemaphoreType.DMA((count, rounds)),
            pltpu.SemaphoreType.DMA(()),
        ],
        input_output_aliases={2 + n: n for n in range(len(before))},
        compiler_params=pltpu.CompilerParams(vmem_limit_bytes=VMEM_GRANT),
    )(*[pltpu.with_memory_space_constraint(array, pltpu.HBM) for array in (keep, values)], *before)


def place_kernel(*rest, plan, rounds, chained):
    pieces = rest[: len(plan)]
    out_ref, sems = rest[len(plan) + chained :]
    layer, tok = lax.axis_index("layer"), lax.axis_index("tok")

    def copies():
        n = 0
        for piece_ref, entry in zip(pieces, plan):
            for slot, offset in enumerate(entry):
                if offset is None:
                    continue
                j, k = offset
                for r in range(rounds):
                    pair = pl.ds((layer ^ j) * 2, 2)
                    rows = pl.ds(pl.multiple_of(((tok ^ k) * rounds + r) * PAGE, PAGE), PAGE)
                    yield pltpu.make_async_copy(
                        piece_ref.at[slot, r], out_ref.at[:, pair, :, rows, :], sems.at[n]
                    )
                    n += 1

    for copy in copies():
        copy.start()
    for copy in copies():
        copy.wait()


def placed(pieces, groups, rows_dev, before=None):
    arrays, plan = [array for array, _ in pieces], [entry for _, entry in pieces]
    rounds, head_group = arrays[0].shape[1], arrays[0].shape[2]
    count = sum(len(entry) for entry in plan) * rounds
    chained = before is not None
    return pl.pallas_call(
        functools.partial(place_kernel, plan=plan, rounds=rounds, chained=int(chained)),
        in_specs=[pl.BlockSpec(memory_space=pltpu.VMEM) for _ in arrays]
        + [pl.BlockSpec(memory_space=pltpu.HBM)] * chained,
        out_specs=pl.BlockSpec(memory_space=pltpu.HBM),
        out_shape=jax.ShapeDtypeStruct((head_group, 2 * groups, 2, rows_dev, HD), jnp.bfloat16),
        scratch_shapes=[pltpu.SemaphoreType.DMA((count,))],
        input_output_aliases={len(arrays): 0} if chained else {},
        compiler_params=pltpu.CompilerParams(vmem_limit_bytes=VMEM_GRANT),
    )(*arrays, *([before] if chained else []))


def offsets_of(groups, tok_count):
    half, quarter = tok_count // 2, tok_count // 4
    small = list(range(quarter))
    middle = list(range(quarter, half))
    early = list(range(half, half + quarter))
    late = list(range(half + quarter, tok_count))
    return list(range(groups - 1, 0, -1)), small, middle, early, late


def one_sequence(values, keep, lengths, groups, tok_count):
    rows_dev = values.shape[2]
    _, small, middle, early, late = offsets_of(groups, tok_count)
    layers = range(groups)

    def over_layer(array, j):
        return lax.ppermute(array, "layer", [(i, i ^ j) for i in range(groups)])

    def over_tok(array, k):
        return lax.ppermute(array, "tok", [(i, i ^ k) for i in range(tok_count)])

    def joined(arrays, n):
        return jnp.concatenate([array[n : n + 1] for array in arrays])

    def without_padding(array, k, source):
        rounds = array.shape[1]
        first = source * rows_dev + (source ^ k) * PAGE
        shape = (1, rounds, 1, 1, 1, PAGE, HD)
        position = first + lax.broadcasted_iota(jnp.int32, shape, 5)
        position += lax.broadcasted_iota(jnp.int32, shape, 1) * (PAGE * tok_count)
        return jnp.where(position < lengths[0], array, jnp.zeros_like(array))

    tok = lax.axis_index("tok")
    first = merged(
        values, keep, [[(j, k) for j in layers] for k in early] + [[(j, k) for k in late] for j in layers],
        groups, tok_count, always=early + late,
    )
    lengths, first = lax.optimization_barrier((lengths, first))
    second = merged(
        values, keep, [[(j, k) for k in middle] for j in layers] + [[(j, k) for j in layers] for k in small],
        groups, tok_count, always=middle + small,
    )
    early_in = [over_tok(array, k) for array, k in zip(first, early)]
    early_in = [without_padding(array, k, tok ^ k) for array, k in zip(early_in, early)]

    def at_home(arrays):
        return [arrays[0]] + [over_layer(arrays[j], j) for j in layers if j]

    late_mine = at_home(first[len(early) :])
    middle_mine = at_home(second[:groups])
    small_in = [over_tok(array, k) if k else array for array, k in zip(second[groups:], small)]
    small_in = [without_padding(array, k, tok ^ k) for array, k in zip(small_in, small)]
    small_mine = [over_layer(joined(small_in, j), j) for j in layers if j]

    def ready(arrays, n, k):
        return without_padding(joined(arrays, n), k, tok)

    late_in = [over_tok(ready(late_mine, n, k), k) for n, k in enumerate(late)]
    middle_in = [over_tok(ready(middle_mine, n, k), k) for n, k in enumerate(middle)]
    early_mine = [over_layer(joined(early_in, j), j) for j in layers if j]
    out = placed(
        [(array[:1], [(0, k)]) for array, k in zip(early_in + small_in, early + small)]
        + [(array, [(j, k) for k in small]) for array, j in zip(small_mine, layers[1:])],
        groups, rows_dev,
    )
    return placed(
        [(array, [(j, k) for j in layers]) for array, k in zip(late_in + middle_in, late + middle)]
        + [(array, [(j, k) for k in early]) for array, j in zip(early_mine, layers[1:])],
        groups, rows_dev, before=out,
    )


def shards(kv_cache, keep_mask, lengths):
    groups = lax.axis_size("layer")
    tok_count = lax.axis_size("tok")
    seq_count = kv_cache.shape[3]
    return jnp.stack(
        [
            one_sequence(kv_cache[0, :, :, s], keep_mask[0, s : s + 1], lengths[s : s + 1], groups, tok_count)
            for s in range(seq_count)
        ]
    )


def solution(mesh):
    in_specs = (P("layer", None, None, None, "tok", None), P("layer", None, "tok"), P())
    out_specs = P(None, "layer", None, None, "tok", None)
    return jax.shard_map(shards, mesh=mesh, in_specs=in_specs, out_specs=out_specs, check_vma=False)
```

time: 48 us -> 43.7 us (0.910)
  the two profiles are of different devices: /device:TPU:0 before, /device:TPU:25 now
where the time goes in v3:
time: 43.7 us; the launch traced here: 43.5 us
  waiting for transfers between devices  19.8 us (45%)
  starting transfers between devices  16.2 us (37%)
  Pallas kernels  5.75 us (13%)
  between operations  0.98 us (2%)
  other arithmetic  0.8 us (2%)
    ppermute x7, waiting for transfers between devices, over_tok(): return lax.ppermute(array, 'tok', [(i, i ^ k) for i in range(tok_count)])  14.2 us
    ppermute x12, starting transfers between devices, over_layer(): return lax.ppermute(array, 'layer', [(i, i ^ j) for i in range(groups)])  10.5 us
    ppermute x7, starting transfers between devices, over_tok(): return lax.ppermute(array, 'tok', [(i, i ^ k) for i in range(tok_count)])  5.64 us
    ppermute x12, waiting for transfers between devices, over_layer(): return lax.ppermute(array, 'layer', [(i, i ^ j) for i in range(groups)])  5.54 us
    pallas_call x2, Pallas kernels, merged(): pl.pallas_call(functools.partial(merge_kernel, plan=plan, always=tuple(al...  3.92 us
    pallas_call x2, Pallas kernels, placed(): pl.pallas_call(functools.partial(place_kernel, plan=plan, rounds=rounds,...  1.83 us
  transfers between devices with their start and end apart: 19, of which 6 were waited for; matrix products, arithmetic and copies ran while one was open for 2% of the time, Pallas kernels for 6%

profile of v3, /device:TPU:25, one launch (start us, length us, event | category | flops | bytes accessed | tf_op | source)
XLA Modules:
  0.0 43.5 jit_solution(3370566370547654197)
XLA Ops:
  0.0 2.0 %shard_map.38 = (bf16[2,1,2,2,2,16,128]{6,5,4,3,2,1,0:T(8,128)(2,1)S(1)}, bf16[2,1,2,2,2,16,128]{6,5,4,3,2,1,0:T(8,128)(2,1)S(1)}, bf16[2,1,2,2,2,16,128]{6,5,4,...) custom-call(s32[1,128]{1,0:T(1,128)} %bitcast.14, ...), custom_call_target="tpu_custom_call" | custom-call | tf_op jit(solution)/shard_map/pallas_call | solution.py:111
  2.0 0.7 %collective-permute-start.5 = (bf16[2,1,2,2,2,16,128]{6,5,4,3,2,1,0:T(8,128)(2,1)S(1)}, bf16[2,1,2,2,2,16,128]{6,5,4,3,2,1,0:T(8,128)(2,1)S(1)}, u32[]{:S(2)}, u32[]{:S(2)}) collective-permute-start(bf16[2,1,2,2,2,16,128]{6,5,4,3,2,1,0:T(8,128)(2,1)S(1)} %get-tuple-element.36), channel_id=1, source_target_pairs={{0,8},{8,0},{16,24},{24,16},{1,9},{9,1},{17,25},{25,17},{2,10},{10... | collective-permute-start | bytes 196616 | tf_op jit(solution)/shard_map/ppermute | solution.py:192
  2.7 1.2 %collective-permute-start.6 = (bf16[2,1,2,2,2,16,128]{6,5,4,3,2,1,0:T(8,128)(2,1)S(1)}, bf16[2,1,2,2,2,16,128]{6,5,4,3,2,1,0:T(8,128)(2,1)S(1)}, u32[]{:S(2)}, u32[]{:S(2)}) collective-permute-start(bf16[2,1,2,2,2,16,128]{6,5,4,3,2,1,0:T(8,128)(2,1)S(1)} %get-tuple-element.37), channel_id=1, source_target_pairs={{0,16},{8,24},{16,0},{24,8},{1,17},{9,25},{17,1},{25,9},{2,18},{10... | collective-permute-start | bytes 196616 | tf_op jit(solution)/shard_map/ppermute | solution.py:192
  3.9 0.5 %collective-permute-start.7 = (bf16[2,1,2,2,2,16,128]{6,5,4,3,2,1,0:T(8,128)(2,1)S(1)}, bf16[2,1,2,2,2,16,128]{6,5,4,3,2,1,0:T(8,128)(2,1)S(1)}, u32[]{:S(2)}, u32[]{:S(2)}) collective-permute-start(bf16[2,1,2,2,2,16,128]{6,5,4,3,2,1,0:T(8,128)(2,1)S(1)} %get-tuple-element.38), channel_id=1, source_target_pairs={{0,24},{8,16},{16,8},{24,0},{1,25},{9,17},{17,9},{25,1},{2,26},{10... | collective-permute-start | bytes 196616 | tf_op jit(solution)/shard_map/ppermute | solution.py:192
  4.4 1.2 %collective-permute-start.15 = (bf16[4,1,2,2,2,16,128]{6,5,4,3,2,1,0:T(8,128)(2,1)S(1)}, bf16[4,1,2,2,2,16,128]{6,5,4,3,2,1,0:T(8,128)(2,1)S(1)}, u32[]{:S(2)}, u32[]{:S(2)}) collective-permute-start(bf16[4,1,2,2,2,16,128]{6,5,4,3,2,1,0:T(8,128)(2,1)S(1)} %get-tuple-element.42), channel_id=1, source_target_pairs={{0,1},{1,0},{2,3},{3,2},{4,5},{5,4},{6,7},{7,6},{8,9},{9,8},{10,11... | collective-permute-start | bytes 393224 | tf_op jit(solution)/shard_map/ppermute | solution.py:195
  5.7 2.0 %shard_map.37 = (bf16[4,1,2,2,2,16,128]{6,5,4,3,2,1,0:T(8,128)(2,1)S(1)}, bf16[4,1,2,2,2,16,128]{6,5,4,3,2,1,0:T(8,128)(2,1)S(1)}, bf16[2,1,2,2,2,16,128]{6,5,4,...) custom-call(s32[1,128]{1,0:T(1,128)} %bitcast.15, ...), custom_call_target="tpu_custom_call" | custom-call | tf_op jit(solution)/shard_map/pallas_call | solution.py:111
  7.6 0.5 %collective-permute-start = (bf16[2,1,2,2,2,16,128]{6,5,4,3,2,1,0:T(8,128)(2,1)S(1)}, bf16[2,1,2,2,2,16,128]{6,5,4,3,2,1,0:T(8,128)(2,1)S(1)}, u32[]{:S(2)}, u32[]{:S(2)}) collective-permute-start(bf16[2,1,2,2,2,16,128]{6,5,4,3,2,1,0:T(8,128)(2,1)S(1)} %get-tuple-element.32), channel_id=1, source_target_pairs={{0,8},{8,0},{16,24},{24,16},{1,9},{9,1},{17,25},{25,17},{2,10},{10... | collective-permute-start | bytes 196616 | tf_op jit(solution)/shard_map/ppermute | solution.py:192
  8.8 0.1 broadcast_select_fusion.1
  9.1 1.3 %collective-permute-start.1 = (bf16[2,1,2,2,2,16,128]{6,5,4,3,2,1,0:T(8,128)(2,1)S(1)}, bf16[2,1,2,2,2,16,128]{6,5,4,3,2,1,0:T(8,128)(2,1)S(1)}, u32[]{:S(2)}, u32[]{:S(2)}) collective-permute-start(bf16[2,1,2,2,2,16,128]{6,5,4,3,2,1,0:T(8,128)(2,1)S(1)} %get-tuple-element.33), channel_id=1, source_target_pairs={{0,16},{8,24},{16,0},{24,8},{1,17},{9,25},{17,1},{25,9},{2,18},{10... | collective-permute-start | bytes 196616 | tf_op jit(solution)/shard_map/ppermute | solution.py:192
  10.4 0.6 %collective-permute-start.2 = (bf16[2,1,2,2,2,16,128]{6,5,4,3,2,1,0:T(8,128)(2,1)S(1)}, bf16[2,1,2,2,2,16,128]{6,5,4,3,2,1,0:T(8,128)(2,1)S(1)}, u32[]{:S(2)}, u32[]{:S(2)}) collective-permute-start(bf16[2,1,2,2,2,16,128]{6,5,4,3,2,1,0:T(8,128)(2,1)S(1)} %get-tuple-element.34), channel_id=1, source_target_pairs={{0,24},{8,16},{16,8},{24,0},{1,25},{9,17},{17,9},{25,1},{2,26},{10... | collective-permute-start | bytes 196616 | tf_op jit(solution)/shard_map/ppermute | solution.py:192
  10.9 0.1 collective-permute-start.10
  11.1 0.1 maximum_select_fusion.3
  11.1 0.1 maximum_select_fusion.2
  11.2 2.3 %collective-permute-start.11 = (bf16[4,1,2,2,2,16,128]{6,5,4,3,2,1,0:T(8,128)(2,1)S(1)}, bf16[4,1,2,2,2,16,128]{6,5,4,3,2,1,0:T(8,128)(2,1)S(1)}, u32[]{:S(2)}, u32[]{:S(2)}) collective-permute-start(bf16[4,1,2,2,2,16,128]{6,5,4,3,2,1,0:T(8,128)(2,1)S(1)} %get-tuple-element.40), channel_id=1, source_target_pairs={{0,5},{1,4},{2,7},{3,6},{4,1},{5,0},{6,3},{7,2},{8,13},{9,12},{10,... | collective-permute-start | bytes 393224 | tf_op jit(solution)/shard_map/ppermute | solution.py:195
  13.6 0.2 collective-permute-start.8
  13.8 0.7 %collective-permute-done.2 = bf16[2,1,2,2,2,16,128]{6,5,4,3,2,1,0:T(8,128)(2,1)S(1)} collective-permute-done((bf16[2,1,2,2,2,16,128]{6,5,4,3,2,1,0:T(8,128)(2,1)S(1)}, bf16[2,1,2,2,2,16,128]{6,5,4,3,2,1,0:T(8,128)(2,1)S(1)}, u32[]{:S(2)}, u32[]{:S(2)}) %collective-permute-start.2) | collective-permute-done | bytes 65568 | tf_op jit(solution)/shard_map/ppermute | solution.py:192
  14.5 1.7 %collective-permute-start.9 = (bf16[4,1,2,2,2,16,128]{6,5,4,3,2,1,0:T(8,128)(2,1)S(1)}, bf16[4,1,2,2,2,16,128]{6,5,4,3,2,1,0:T(8,128)(2,1)S(1)}, u32[]{:S(2)}, u32[]{:S(2)}) collective-permute-start(bf16[4,1,2,2,2,16,128]{6,5,4,3,2,1,0:T(8,128)(2,1)S(1)} %maximum_select_fusion.3), channel_id=1, source_target_pairs={{0,3},{1,2},{2,1},{3,0},{4,7},{5,6},{6,5},{7,4},{8,11},{9,10},{10,... | collective-permute-start | bytes 393224 | tf_op jit(solution)/shard_map/ppermute | solution.py:195
  16.1 0.1 maximum_select_fusion.1
  16.2 0.1 maximum_select_fusion
  16.4 0.1 broadcast_select_fusion
  16.5 6.4 %collective-permute-done.10 = bf16[4,1,2,2,2,16,128]{6,5,4,3,2,1,0:T(8,128)(2,1)S(1)} collective-permute-done((bf16[4,1,2,2,2,16,128]{6,5,4,3,2,1,0:T(8,128)(2,1)S(1)}, bf16[4,1,2,2,2,16,128]{6,5,4,3,2,1,0:T(8,128)(2,1)S(1)}, u32[]{:S(2)}, u32[]{:S(2)}) %collective-permute-start.10) | collective-permute-done | bytes 131104 | tf_op jit(solution)/shard_map/ppermute | solution.py:195
  23.0 3.2 %collective-permute-done.11 = bf16[4,1,2,2,2,16,128]{6,5,4,3,2,1,0:T(8,128)(2,1)S(1)} collective-permute-done((bf16[4,1,2,2,2,16,128]{6,5,4,3,2,1,0:T(8,128)(2,1)S(1)}, bf16[4,1,2,2,2,16,128]{6,5,4,3,2,1,0:T(8,128)(2,1)S(1)}, u32[]{:S(2)}, u32[]{:S(2)}) %collective-permute-start.11) | collective-permute-done | bytes 131104 | tf_op jit(solution)/shard_map/ppermute | solution.py:195
  26.2 0.6 %collective-permute-start.16 = (bf16[2,1,2,2,2,16,128]{6,5,4,3,2,1,0:T(8,128)(2,1)S(1)}, bf16[2,1,2,2,2,16,128]{6,5,4,3,2,1,0:T(8,128)(2,1)S(1)}, u32[]{:S(2)}, u32[]{:S(2)}) collective-permute-start(bf16[2,1,2,2,2,16,128]{6,5,4,3,2,1,0:T(8,128)(2,1)S(1)} %pad_maximum_fusion.3), channel_id=1, source_target_pairs={{0,8},{8,0},{16,24},{24,16},{1,9},{9,1},{17,25},{25,17},{2,10},{10... | collective-permute-start | bytes 196616 | tf_op jit(solution)/shard_map/ppermute | solution.py:192
  27.0 1.3 %collective-permute-start.17 = (bf16[2,1,2,2,2,16,128]{6,5,4,3,2,1,0:T(8,128)(2,1)S(1)}, bf16[2,1,2,2,2,16,128]{6,5,4,3,2,1,0:T(8,128)(2,1)S(1)}, u32[]{:S(2)}, u32[]{:S(2)}) collective-permute-start(bf16[2,1,2,2,2,16,128]{6,5,4,3,2,1,0:T(8,128)(2,1)S(1)} %pad_maximum_fusion.4), channel_id=1, source_target_pairs={{0,16},{8,24},{16,0},{24,8},{1,17},{9,25},{17,1},{25,9},{2,18},{10... | collective-permute-start | bytes 196616 | tf_op jit(solution)/shard_map/ppermute | solution.py:192
  28.2 4.6 %collective-permute-done.9.rest_3_ = bf16[4,1,2,2,2,16,128]{6,5,4,3,2,1,0:T(8,128)(2,1)S(1)} collective-permute-done((bf16[4,1,2,2,2,16,128]{6,5,4,3,2,1,0:T(8,128)(2,1)S(1)}, bf16[4,1,2,2,2,16,128]{6,5,4,3,2,1,0:T(8,128)(2,1)S(1)}, u32[]{:S(2)}, u32[]{:S(2)}) %collective-permute-start.9) | collective-permute-done | bytes 131104 | tf_op jit(solution)/shard_map/ppermute | solution.py:195
  32.9 2.7 %collective-permute-start.18 = (bf16[2,1,2,2,2,16,128]{6,5,4,3,2,1,0:T(8,128)(2,1)S(1)}, bf16[2,1,2,2,2,16,128]{6,5,4,3,2,1,0:T(8,128)(2,1)S(1)}, u32[]{:S(2)}, u32[]{:S(2)}) collective-permute-start(bf16[2,1,2,2,2,16,128]{6,5,4,3,2,1,0:T(8,128)(2,1)S(1)} %pad_maximum_fusion.5), channel_id=1, source_target_pairs={{0,24},{8,16},{16,8},{24,0},{1,25},{9,17},{17,9},{25,1},{2,26},{10... | collective-permute-start | bytes 196616 | tf_op jit(solution)/shard_map/ppermute | solution.py:192
  35.7 0.3 collective-permute-start.13
  36.0 2.4 %collective-permute-done.18.rest_6_ = bf16[2,1,2,2,2,16,128]{6,5,4,3,2,1,0:T(8,128)(2,1)S(1)} collective-permute-done((bf16[2,1,2,2,2,16,128]{6,5,4,3,2,1,0:T(8,128)(2,1)S(1)}, bf16[2,1,2,2,2,16,128]{6,5,4,3,2,1,0:T(8,128)(2,1)S(1)}, u32[]{:S(2)}, u32[]{:S(2)}) %collective-permute-start.18) | collective-permute-done | bytes 65568 | tf_op jit(solution)/shard_map/ppermute | solution.py:192
  38.4 0.8 %collective-permute-start.14 = (bf16[2,1,2,2,2,16,128]{6,5,4,3,2,1,0:T(8,128)(2,1)S(1)}, bf16[2,1,2,2,2,16,128]{6,5,4,3,2,1,0:T(8,128)(2,1)S(1)}, u32[]{:S(2)}, u32[]{:S(2)}) collective-permute-start(bf16[2,1,2,2,2,16,128]{6,5,4,3,2,1,0:T(8,128)(2,1)S(1)} %pad_maximum_fusion.2), channel_id=1, source_target_pairs={{0,24},{8,16},{16,8},{24,0},{1,25},{9,17},{17,9},{25,1},{2,26},{10... | collective-permute-start | bytes 196616 | tf_op jit(solution)/shard_map/ppermute | solution.py:192
  39.2 0.8 %shard_map.39.rest_7_ = bf16[2,8,2,128,128]{4,3,2,1,0:T(8,128)(2,1)} custom-call(bf16[1,1,2,2,2,16,128]{6,5,4,3,2,1,0:T(8,128)(2,1)S(1)} %get-tuple-element.55.rest_0_, bf16[1,1,2,2,2,16,128]{6,5,4,3,2,1,0:T(8,128)(2,1)S(1)} %get-tuple-element.51.rest_1_, bf16[1,1,2,2,2,16,128]{6,5,4,3,2,1,0:T(8,128)(2,1)S(1)} %get-tuple-element.46.rest_2_, ...), custom_call_target="tpu_custom_call" | custom-call | tf_op jit(solution)/shard_map/pallas_call | solution.py:165
  40.1 2.4 %collective-permute-done.14.rest_6_ = bf16[2,1,2,2,2,16,128]{6,5,4,3,2,1,0:T(8,128)(2,1)S(1)} collective-permute-done((bf16[2,1,2,2,2,16,128]{6,5,4,3,2,1,0:T(8,128)(2,1)S(1)}, bf16[2,1,2,2,2,16,128]{6,5,4,3,2,1,0:T(8,128)(2,1)S(1)}, u32[]{:S(2)}, u32[]{:S(2)}) %collective-permute-start.14) | collective-permute-done | bytes 65568 | tf_op jit(solution)/shard_map/ppermute | solution.py:192
  42.5 1.0 %shard_map.40 = bf16[2,8,2,128,128]{4,3,2,1,0:T(8,128)(2,1)} custom-call(bf16[4,1,2,2,2,16,128]{6,5,4,3,2,1,0:T(8,128)(2,1)S(1)} %collective-permute-done.3.rest_0_, bf16[4,1,2,2,2,16,128]{6,5,4,3,2,1,0:T(8,128)(2,1)S(1)} %collective-permute-done.4.rest_1_, ...), custom_call_target="tpu_custom_call", output_to_operand_aliasing={{}: (7, {})} | custom-call | tf_op jit(solution)/shard_map/pallas_call | solution.py:165
  (44 shorter events, 0.6 us)
Async XLA Ops:
  2.0 7.1 %collective-permute-start.5 = (bf16[2,1,2,2,2,16,128]{6,5,4,3,2,1,0:T(8,128)(2,1)S(1)}, bf16[2,1,2,2,2,16,128]{6,5,4,3,2,1,0:T(8,128)(2,1)S(1)}, u32[]{:S(2)}, u32[]{:S(2)}) collective-permute-start(bf16[2,1,2,2,2,16,128]{6,5,4,3,2,1,0:T(8,128)(2,1)S(1)} %get-tuple-element.36), channel_id=1, source_target_pairs={{0,8},{8,0},{16,24},{24,16},{1,9},{9,1},{17,25},{25,17},{2,10},{10... | collective-permute-start | bytes 196616 | tf_op jit(solution)/shard_map/ppermute | solution.py:192
  2.7 7.6 %collective-permute-start.6 = (bf16[2,1,2,2,2,16,128]{6,5,4,3,2,1,0:T(8,128)(2,1)S(1)}, bf16[2,1,2,2,2,16,128]{6,5,4,3,2,1,0:T(8,128)(2,1)S(1)}, u32[]{:S(2)}, u32[]{:S(2)}) collective-permute-start(bf16[2,1,2,2,2,16,128]{6,5,4,3,2,1,0:T(8,128)(2,1)S(1)} %get-tuple-element.37), channel_id=1, source_target_pairs={{0,16},{8,24},{16,0},{24,8},{1,17},{9,25},{17,1},{25,9},{2,18},{10... | collective-permute-start | bytes 196616 | tf_op jit(solution)/shard_map/ppermute | solution.py:192
  3.9 7.0 %collective-permute-start.7 = (bf16[2,1,2,2,2,16,128]{6,5,4,3,2,1,0:T(8,128)(2,1)S(1)}, bf16[2,1,2,2,2,16,128]{6,5,4,3,2,1,0:T(8,128)(2,1)S(1)}, u32[]{:S(2)}, u32[]{:S(2)}) collective-permute-start(bf16[2,1,2,2,2,16,128]{6,5,4,3,2,1,0:T(8,128)(2,1)S(1)} %get-tuple-element.38), channel_id=1, source_target_pairs={{0,24},{8,16},{16,8},{24,0},{1,25},{9,17},{17,9},{25,1},{2,26},{10... | collective-permute-start | bytes 196616 | tf_op jit(solution)/shard_map/ppermute | solution.py:192
  4.4 11.9 %collective-permute-start.15 = (bf16[4,1,2,2,2,16,128]{6,5,4,3,2,1,0:T(8,128)(2,1)S(1)}, bf16[4,1,2,2,2,16,128]{6,5,4,3,2,1,0:T(8,128)(2,1)S(1)}, u32[]{:S(2)}, u32[]{:S(2)}) collective-permute-start(bf16[4,1,2,2,2,16,128]{6,5,4,3,2,1,0:T(8,128)(2,1)S(1)} %get-tuple-element.42), channel_id=1, source_target_pairs={{0,1},{1,0},{2,3},{3,2},{4,5},{5,4},{6,7},{7,6},{8,9},{9,8},{10,11... | collective-permute-start | bytes 393224 | tf_op jit(solution)/shard_map/ppermute | solution.py:195
  7.6 3.6 %collective-permute-start = (bf16[2,1,2,2,2,16,128]{6,5,4,3,2,1,0:T(8,128)(2,1)S(1)}, bf16[2,1,2,2,2,16,128]{6,5,4,3,2,1,0:T(8,128)(2,1)S(1)}, u32[]{:S(2)}, u32[]{:S(2)}) collective-permute-start(bf16[2,1,2,2,2,16,128]{6,5,4,3,2,1,0:T(8,128)(2,1)S(1)} %get-tuple-element.32), channel_id=1, source_target_pairs={{0,8},{8,0},{16,24},{24,16},{1,9},{9,1},{17,25},{25,17},{2,10},{10... | collective-permute-start | bytes 196616 | tf_op jit(solution)/shard_map/ppermute | solution.py:192
  9.1 4.5 %collective-permute-start.1 = (bf16[2,1,2,2,2,16,128]{6,5,4,3,2,1,0:T(8,128)(2,1)S(1)}, bf16[2,1,2,2,2,16,128]{6,5,4,3,2,1,0:T(8,128)(2,1)S(1)}, u32[]{:S(2)}, u32[]{:S(2)}) collective-permute-start(bf16[2,1,2,2,2,16,128]{6,5,4,3,2,1,0:T(8,128)(2,1)S(1)} %get-tuple-element.33), channel_id=1, source_target_pairs={{0,16},{8,24},{16,0},{24,8},{1,17},{9,25},{17,1},{25,9},{2,18},{10... | collective-permute-start | bytes 196616 | tf_op jit(solution)/shard_map/ppermute | solution.py:192
  10.4 4.1 %collective-permute-start.2 = (bf16[2,1,2,2,2,16,128]{6,5,4,3,2,1,0:T(8,128)(2,1)S(1)}, bf16[2,1,2,2,2,16,128]{6,5,4,3,2,1,0:T(8,128)(2,1)S(1)}, u32[]{:S(2)}, u32[]{:S(2)}) collective-permute-start(bf16[2,1,2,2,2,16,128]{6,5,4,3,2,1,0:T(8,128)(2,1)S(1)} %get-tuple-element.34), channel_id=1, source_target_pairs={{0,24},{8,16},{16,8},{24,0},{1,25},{9,17},{17,9},{25,1},{2,26},{10... | collective-permute-start | bytes 196616 | tf_op jit(solution)/shard_map/ppermute | solution.py:192
  10.9 12.0 %collective-permute-start.10 = (bf16[4,1,2,2,2,16,128]{6,5,4,3,2,1,0:T(8,128)(2,1)S(1)}, bf16[4,1,2,2,2,16,128]{6,5,4,3,2,1,0:T(8,128)(2,1)S(1)}, u32[]{:S(2)}, u32[]{:S(2)}) collective-permute-start(bf16[4,1,2,2,2,16,128]{6,5,4,3,2,1,0:T(8,128)(2,1)S(1)} %get-tuple-element.39), channel_id=1, source_target_pairs={{0,4},{1,5},{2,6},{3,7},{4,0},{5,1},{6,2},{7,3},{8,12},{9,13},{10,... | collective-permute-start | bytes 393224 | tf_op jit(solution)/shard_map/ppermute | solution.py:195
  11.2 15.0 %collective-permute-start.11 = (bf16[4,1,2,2,2,16,128]{6,5,4,3,2,1,0:T(8,128)(2,1)S(1)}, bf16[4,1,2,2,2,16,128]{6,5,4,3,2,1,0:T(8,128)(2,1)S(1)}, u32[]{:S(2)}, u32[]{:S(2)}) collective-permute-start(bf16[4,1,2,2,2,16,128]{6,5,4,3,2,1,0:T(8,128)(2,1)S(1)} %get-tuple-element.40), channel_id=1, source_target_pairs={{0,5},{1,4},{2,7},{3,6},{4,1},{5,0},{6,3},{7,2},{8,13},{9,12},{10,... | collective-permute-start | bytes 393224 | tf_op jit(solution)/shard_map/ppermute | solution.py:195
  13.6 13.4 %collective-permute-start.8 = (bf16[4,1,2,2,2,16,128]{6,5,4,3,2,1,0:T(8,128)(2,1)S(1)}, bf16[4,1,2,2,2,16,128]{6,5,4,3,2,1,0:T(8,128)(2,1)S(1)}, u32[]{:S(2)}, u32[]{:S(2)}) collective-permute-start(bf16[4,1,2,2,2,16,128]{6,5,4,3,2,1,0:T(8,128)(2,1)S(1)} %maximum_select_fusion.2), channel_id=1, source_target_pairs={{0,2},{1,3},{2,0},{3,1},{4,6},{5,7},{6,4},{7,5},{8,10},{9,11},{10,... | collective-permute-start | bytes 393224 | tf_op jit(solution)/shard_map/ppermute | solution.py:195
  14.5 18.4 %collective-permute-start.9 = (bf16[4,1,2,2,2,16,128]{6,5,4,3,2,1,0:T(8,128)(2,1)S(1)}, bf16[4,1,2,2,2,16,128]{6,5,4,3,2,1,0:T(8,128)(2,1)S(1)}, u32[]{:S(2)}, u32[]{:S(2)}) collective-permute-start(bf16[4,1,2,2,2,16,128]{6,5,4,3,2,1,0:T(8,128)(2,1)S(1)} %maximum_select_fusion.3), channel_id=1, source_target_pairs={{0,3},{1,2},{2,1},{3,0},{4,7},{5,6},{6,5},{7,4},{8,11},{9,10},{10,... | collective-permute-start | bytes 393224 | tf_op jit(solution)/shard_map/ppermute | solution.py:195
  16.3 23.7 %collective-permute-start.3 = (bf16[4,1,2,2,2,16,128]{6,5,4,3,2,1,0:T(8,128)(2,1)S(1)}, bf16[4,1,2,2,2,16,128]{6,5,4,3,2,1,0:T(8,128)(2,1)S(1)}, u32[]{:S(2)}, u32[]{:S(2)}) collective-permute-start(bf16[4,1,2,2,2,16,128]{6,5,4,3,2,1,0:T(8,128)(2,1)S(1)} %maximum_select_fusion), channel_id=1, source_target_pairs={{0,6},{1,7},{2,4},{3,5},{4,2},{5,3},{6,0},{7,1},{8,14},{9,15},{10,... | collective-permute-start | bytes 393224 | tf_op jit(solution)/shard_map/ppermute | solution.py:195
  22.9 17.2 %collective-permute-start.4 = (bf16[4,1,2,2,2,16,128]{6,5,4,3,2,1,0:T(8,128)(2,1)S(1)}, bf16[4,1,2,2,2,16,128]{6,5,4,3,2,1,0:T(8,128)(2,1)S(1)}, u32[]{:S(2)}, u32[]{:S(2)}) collective-permute-start(bf16[4,1,2,2,2,16,128]{6,5,4,3,2,1,0:T(8,128)(2,1)S(1)} %maximum_select_fusion.1), channel_id=1, source_target_pairs={{0,7},{1,6},{2,5},{3,4},{4,3},{5,2},{6,1},{7,0},{8,15},{9,14},{10,... | collective-permute-start | bytes 393224 | tf_op jit(solution)/shard_map/ppermute | solution.py:195
  26.2 9.4 %collective-permute-start.16 = (bf16[2,1,2,2,2,16,128]{6,5,4,3,2,1,0:T(8,128)(2,1)S(1)}, bf16[2,1,2,2,2,16,128]{6,5,4,3,2,1,0:T(8,128)(2,1)S(1)}, u32[]{:S(2)}, u32[]{:S(2)}) collective-permute-start(bf16[2,1,2,2,2,16,128]{6,5,4,3,2,1,0:T(8,128)(2,1)S(1)} %pad_maximum_fusion.3), channel_id=1, source_target_pairs={{0,8},{8,0},{16,24},{24,16},{1,9},{9,1},{17,25},{25,17},{2,10},{10... | collective-permute-start | bytes 196616 | tf_op jit(solution)/shard_map/ppermute | solution.py:192
  27.0 8.7 %collective-permute-start.17 = (bf16[2,1,2,2,2,16,128]{6,5,4,3,2,1,0:T(8,128)(2,1)S(1)}, bf16[2,1,2,2,2,16,128]{6,5,4,3,2,1,0:T(8,128)(2,1)S(1)}, u32[]{:S(2)}, u32[]{:S(2)}) collective-permute-start(bf16[2,1,2,2,2,16,128]{6,5,4,3,2,1,0:T(8,128)(2,1)S(1)} %pad_maximum_fusion.4), channel_id=1, source_target_pairs={{0,16},{8,24},{16,0},{24,8},{1,17},{9,25},{17,1},{25,9},{2,18},{10... | collective-permute-start | bytes 196616 | tf_op jit(solution)/shard_map/ppermute | solution.py:192
  32.9 5.5 %collective-permute-start.18 = (bf16[2,1,2,2,2,16,128]{6,5,4,3,2,1,0:T(8,128)(2,1)S(1)}, bf16[2,1,2,2,2,16,128]{6,5,4,3,2,1,0:T(8,128)(2,1)S(1)}, u32[]{:S(2)}, u32[]{:S(2)}) collective-permute-start(bf16[2,1,2,2,2,16,128]{6,5,4,3,2,1,0:T(8,128)(2,1)S(1)} %pad_maximum_fusion.5), channel_id=1, source_target_pairs={{0,24},{8,16},{16,8},{24,0},{1,25},{9,17},{17,9},{25,1},{2,26},{10... | collective-permute-start | bytes 196616 | tf_op jit(solution)/shard_map/ppermute | solution.py:192
  35.6 4.5 %collective-permute-start.12 = (bf16[2,1,2,2,2,16,128]{6,5,4,3,2,1,0:T(8,128)(2,1)S(1)}, bf16[2,1,2,2,2,16,128]{6,5,4,3,2,1,0:T(8,128)(2,1)S(1)}, u32[]{:S(2)}, u32[]{:S(2)}) collective-permute-start(bf16[2,1,2,2,2,16,128]{6,5,4,3,2,1,0:T(8,128)(2,1)S(1)} %pad_maximum_fusion), channel_id=1, source_target_pairs={{0,8},{8,0},{16,24},{24,16},{1,9},{9,1},{17,25},{25,17},{2,10},{10... | collective-permute-start | bytes 196616 | tf_op jit(solution)/shard_map/ppermute | solution.py:192
  35.7 4.4 %collective-permute-start.13 = (bf16[2,1,2,2,2,16,128]{6,5,4,3,2,1,0:T(8,128)(2,1)S(1)}, bf16[2,1,2,2,2,16,128]{6,5,4,3,2,1,0:T(8,128)(2,1)S(1)}, u32[]{:S(2)}, u32[]{:S(2)}) collective-permute-start(bf16[2,1,2,2,2,16,128]{6,5,4,3,2,1,0:T(8,128)(2,1)S(1)} %pad_maximum_fusion.1), channel_id=1, source_target_pairs={{0,16},{8,24},{16,0},{24,8},{1,17},{9,25},{17,1},{25,9},{2,18},{10... | collective-permute-start | bytes 196616 | tf_op jit(solution)/shard_map/ppermute | solution.py:192
  38.4 4.1 %collective-permute-start.14 = (bf16[2,1,2,2,2,16,128]{6,5,4,3,2,1,0:T(8,128)(2,1)S(1)}, bf16[2,1,2,2,2,16,128]{6,5,4,3,2,1,0:T(8,128)(2,1)S(1)}, u32[]{:S(2)}, u32[]{:S(2)}) collective-permute-start(bf16[2,1,2,2,2,16,128]{6,5,4,3,2,1,0:T(8,128)(2,1)S(1)} %pad_maximum_fusion.2), channel_id=1, source_target_pairs={{0,24},{8,16},{16,8},{24,0},{1,25},{9,17},{17,9},{25,1},{2,26},{10... | collective-permute-start | bytes 196616 | tf_op jit(solution)/shard_map/ppermute | solution.py:192

commit v4 on v3

--- a/solution.py
+++ b/solution.py
@@ -18,22 +18,13 @@
 VMEM_GRANT = 16 * 2**20
 
 
-def merge(lower, upper, retained):
-    lower_square = jnp.mean(lower * lower, axis=-1, keepdims=True) + epsilon
-    upper_square = jnp.mean(upper * upper, axis=-1, keepdims=True) + epsilon
-    lower_inverse = lax.rsqrt(lower_square)
-    upper_inverse = lax.rsqrt(upper_square)
-    summed = lower * lower_inverse + upper * upper_inverse
-    summed_inverse = lax.rsqrt(jnp.mean(summed * summed, axis=-1, keepdims=True) + epsilon)
-    direction = summed * summed_inverse
-    lower_out = jnp.where(retained, lower, (lower_square * lower_inverse) * direction)
-    upper_out = jnp.where(retained, upper, (upper_square * upper_inverse) * direction)
-    return lower_out.astype(jnp.bfloat16), upper_out.astype(jnp.bfloat16)
+def mean_square(x):
+    return jnp.mean(x * x, axis=-1, keepdims=True) + epsilon
 
 
 def merge_kernel(keep_ref, values_ref, *rest, plan, always, lower, upper, groups, tok_count, rounds):
-    loaded, mask, columns, sems, mask_sem = rest[-5:]
-    outs = rest[-5 - len(plan) : -5]
+    loaded, mask, columns, squares, sems, mask_sem = rest[-6:]
+    outs = rest[-6 - len(plan) : -6]
     layer, tok = lax.axis_index("layer"), lax.axis_index("tok")
     rows_dev = values_ref.shape[2]
     head_group = KVH // groups
@@ -64,25 +55,59 @@
             columns[block : block + HD, :] = jnp.broadcast_to(keep, (HD, HD)).T
 
     def work(offsets):
+        def parts(k):
+            for r in range(rounds):
+                for j in range(groups):
+                    for c in range(2):
+                        for member in range(head_group):
+                            yield slots[k], r, j, c, member
+
+        def read(n, r, side, j, c, member):
+            lane = pl.multiple_of((layer ^ j) * width + member * HD, HD)
+            return loaded[n, r, side, c, :, pl.ds(lane, HD)].astype(jnp.float32)
+
+        def put(at, which, value):
+            squares[at + (which,)] = jnp.broadcast_to(value, (PAGE, HD))
+
+        def total(n, r, j, c, member):
+            at = (n, r, j, c, member)
+            lower = read(n, r, 0, j, c, member) * lax.rsqrt(squares[at + (0,)])
+            return lower + read(n, r, 1, j, c, member) * lax.rsqrt(squares[at + (1,)])
+
+        def singles(k):
+            pass
+            for at in parts(k):
+                n, r, j, c, member = at
+                for side in range(2):
+                    put(at, side, mean_square(read(n, r, side, j, c, member)))
+
+        def sums(k):
+            for at in parts(k):
+                put(at, 2, mean_square(total(*at)))
+
+        def results(k):
+            for at in parts(k):
+                n, r, j, c, member = at
+                start = pl.multiple_of((r * tok_count + (tok ^ k)) * PAGE, PAGE)
+                retained = columns[pl.ds(start, PAGE), :] > 0.0
+                direction = total(*at) * lax.rsqrt(squares[at + (2,)])
+                o, slot = where[(j, k)]
+                for side in range(2):
+                    square = squares[at + (side,)]
+                    scaled = (square * lax.rsqrt(square)) * direction
+                    chosen = jnp.where(retained, read(n, r, side, j, c, member), scaled)
+                    outs[o][slot, r, member, side, c] = chosen.astype(jnp.bfloat16)
+
         for k in offsets:
             for copy in copies(k):
                 copy.wait()
-            n = slots[k]
-            for r in range(rounds):
-                start = pl.multiple_of((r * tok_count + (tok ^ k)) * PAGE, PAGE)
-                retained = columns[pl.ds(start, PAGE), :] > 0.0
-                for j in range(groups):
-                    o, slot = where[(j, k)]
-                    for c in range(2):
-                        for member in range(head_group):
-                            lane = pl.multiple_of((layer ^ j) * width + member * HD, HD)
-                            both = merge(
-                                loaded[n, r, 0, c, :, pl.ds(lane, HD)].astype(jnp.float32),
-                                loaded[n, r, 1, c, :, pl.ds(lane, HD)].astype(jnp.float32),
-                                retained,
-                            )
-                            for side in range(2):
-                                outs[o][slot, r, member, side, c] = both[side]
+        for step in range(len(offsets) + 2):
+            if step < len(offsets):
+                singles(offsets[step])
+            if 0 <= step - 1 < len(offsets):
+                sums(offsets[step - 1])
+            if 0 <= step - 2:
+                results(offsets[step - 2])
 
     if always:
         mask_copy.start()
@@ -123,6 +148,7 @@
             pltpu.VMEM((count, rounds, 2, 2, PAGE, values.shape[3]), jnp.bfloat16),
             pltpu.VMEM((1, rows_dev), jnp.int32),
             pltpu.VMEM((rows_dev, HD), jnp.float32),
+            pltpu.VMEM((count, rounds, groups, 2, head_group, 3, PAGE, HD), jnp.float32),
             pltpu.SemaphoreType.DMA((count, rounds)),
             pltpu.SemaphoreType.DMA(()),
         ],

time: 43.7 us -> 43.4 us (level)
  no operation moved by 1% of the time
where the time goes in v4:
time: 43.4 us; the launch traced here: 43.3 us
  waiting for transfers between devices  19.8 us (46%)
  starting transfers between devices  16.2 us (37%)
  Pallas kernels  5.46 us (13%)
  between operations  0.98 us (2%)
  other arithmetic  0.8 us (2%)
    ppermute x7, waiting for transfers between devices, over_tok(): return lax.ppermute(array, 'tok', [(i, i ^ k) for i in range(tok_count)])  14.2 us
    ppermute x12, starting transfers between devices, over_layer(): return lax.ppermute(array, 'layer', [(i, i ^ j) for i in range(groups)])  10.5 us
    ppermute x7, starting transfers between devices, over_tok(): return lax.ppermute(array, 'tok', [(i, i ^ k) for i in range(tok_count)])  5.64 us
    ppermute x12, waiting for transfers between devices, over_layer(): return lax.ppermute(array, 'layer', [(i, i ^ j) for i in range(groups)])  5.54 us
    pallas_call x2, Pallas kernels, merged(): pl.pallas_call(functools.partial(merge_kernel, plan=plan, always=tuple(al...  3.63 us
    pallas_call x2, Pallas kernels, placed(): pl.pallas_call(functools.partial(place_kernel, plan=plan, rounds=rounds,...  1.83 us
  transfers between devices with their start and end apart: 19, of which 6 were waited for; matrix products, arithmetic and copies ran while one was open for 2% of the time, Pallas kernels for 6%

profile of v4, /device:TPU:25, one launch (start us, length us, event | category | flops | bytes accessed | tf_op | source)
XLA Modules:
  0.0 43.3 jit_solution(17792587578308953230)
XLA Ops:
  0.0 1.8 %shard_map.38 = (bf16[2,1,2,2,2,16,128]{6,5,4,3,2,1,0:T(8,128)(2,1)S(1)}, bf16[2,1,2,2,2,16,128]{6,5,4,3,2,1,0:T(8,128)(2,1)S(1)}, bf16[2,1,2,2,2,16,128]{6,5,4,...) custom-call(s32[1,128]{1,0:T(1,128)} %bitcast.14, ...), custom_call_target="tpu_custom_call" | custom-call | tf_op jit(solution)/shard_map/pallas_call | solution.py:136
  1.8 0.7 %collective-permute-start.5 = (bf16[2,1,2,2,2,16,128]{6,5,4,3,2,1,0:T(8,128)(2,1)S(1)}, bf16[2,1,2,2,2,16,128]{6,5,4,3,2,1,0:T(8,128)(2,1)S(1)}, u32[]{:S(2)}, u32[]{:S(2)}) collective-permute-start(bf16[2,1,2,2,2,16,128]{6,5,4,3,2,1,0:T(8,128)(2,1)S(1)} %get-tuple-element.36), channel_id=1, source_target_pairs={{0,8},{8,0},{16,24},{24,16},{1,9},{9,1},{17,25},{25,17},{2,10},{10... | collective-permute-start | bytes 196616 | tf_op jit(solution)/shard_map/ppermute | solution.py:218
  2.6 1.2 %collective-permute-start.6 = (bf16[2,1,2,2,2,16,128]{6,5,4,3,2,1,0:T(8,128)(2,1)S(1)}, bf16[2,1,2,2,2,16,128]{6,5,4,3,2,1,0:T(8,128)(2,1)S(1)}, u32[]{:S(2)}, u32[]{:S(2)}) collective-permute-start(bf16[2,1,2,2,2,16,128]{6,5,4,3,2,1,0:T(8,128)(2,1)S(1)} %get-tuple-element.37), channel_id=1, source_target_pairs={{0,16},{8,24},{16,0},{24,8},{1,17},{9,25},{17,1},{25,9},{2,18},{10... | collective-permute-start | bytes 196616 | tf_op jit(solution)/shard_map/ppermute | solution.py:218
  3.8 0.5 %collective-permute-start.7 = (bf16[2,1,2,2,2,16,128]{6,5,4,3,2,1,0:T(8,128)(2,1)S(1)}, bf16[2,1,2,2,2,16,128]{6,5,4,3,2,1,0:T(8,128)(2,1)S(1)}, u32[]{:S(2)}, u32[]{:S(2)}) collective-permute-start(bf16[2,1,2,2,2,16,128]{6,5,4,3,2,1,0:T(8,128)(2,1)S(1)} %get-tuple-element.38), channel_id=1, source_target_pairs={{0,24},{8,16},{16,8},{24,0},{1,25},{9,17},{17,9},{25,1},{2,26},{10... | collective-permute-start | bytes 196616 | tf_op jit(solution)/shard_map/ppermute | solution.py:218
  4.3 1.2 %collective-permute-start.15 = (bf16[4,1,2,2,2,16,128]{6,5,4,3,2,1,0:T(8,128)(2,1)S(1)}, bf16[4,1,2,2,2,16,128]{6,5,4,3,2,1,0:T(8,128)(2,1)S(1)}, u32[]{:S(2)}, u32[]{:S(2)}) collective-permute-start(bf16[4,1,2,2,2,16,128]{6,5,4,3,2,1,0:T(8,128)(2,1)S(1)} %get-tuple-element.42), channel_id=1, source_target_pairs={{0,1},{1,0},{2,3},{3,2},{4,5},{5,4},{6,7},{7,6},{8,9},{9,8},{10,11... | collective-permute-start | bytes 393224 | tf_op jit(solution)/shard_map/ppermute | solution.py:221
  5.5 1.8 %shard_map.37 = (bf16[4,1,2,2,2,16,128]{6,5,4,3,2,1,0:T(8,128)(2,1)S(1)}, bf16[4,1,2,2,2,16,128]{6,5,4,3,2,1,0:T(8,128)(2,1)S(1)}, bf16[2,1,2,2,2,16,128]{6,5,4,...) custom-call(s32[1,128]{1,0:T(1,128)} %bitcast.15, ...), custom_call_target="tpu_custom_call" | custom-call | tf_op jit(solution)/shard_map/pallas_call | solution.py:136
  7.3 0.5 %collective-permute-start = (bf16[2,1,2,2,2,16,128]{6,5,4,3,2,1,0:T(8,128)(2,1)S(1)}, bf16[2,1,2,2,2,16,128]{6,5,4,3,2,1,0:T(8,128)(2,1)S(1)}, u32[]{:S(2)}, u32[]{:S(2)}) collective-permute-start(bf16[2,1,2,2,2,16,128]{6,5,4,3,2,1,0:T(8,128)(2,1)S(1)} %get-tuple-element.32), channel_id=1, source_target_pairs={{0,8},{8,0},{16,24},{24,16},{1,9},{9,1},{17,25},{25,17},{2,10},{10... | collective-permute-start | bytes 196616 | tf_op jit(solution)/shard_map/ppermute | solution.py:218
  8.5 0.1 broadcast_select_fusion.1
  8.8 1.3 %collective-permute-start.1 = (bf16[2,1,2,2,2,16,128]{6,5,4,3,2,1,0:T(8,128)(2,1)S(1)}, bf16[2,1,2,2,2,16,128]{6,5,4,3,2,1,0:T(8,128)(2,1)S(1)}, u32[]{:S(2)}, u32[]{:S(2)}) collective-permute-start(bf16[2,1,2,2,2,16,128]{6,5,4,3,2,1,0:T(8,128)(2,1)S(1)} %get-tuple-element.33), channel_id=1, source_target_pairs={{0,16},{8,24},{16,0},{24,8},{1,17},{9,25},{17,1},{25,9},{2,18},{10... | collective-permute-start | bytes 196616 | tf_op jit(solution)/shard_map/ppermute | solution.py:218
  10.1 0.6 %collective-permute-start.2 = (bf16[2,1,2,2,2,16,128]{6,5,4,3,2,1,0:T(8,128)(2,1)S(1)}, bf16[2,1,2,2,2,16,128]{6,5,4,3,2,1,0:T(8,128)(2,1)S(1)}, u32[]{:S(2)}, u32[]{:S(2)}) collective-permute-start(bf16[2,1,2,2,2,16,128]{6,5,4,3,2,1,0:T(8,128)(2,1)S(1)} %get-tuple-element.34), channel_id=1, source_target_pairs={{0,24},{8,16},{16,8},{24,0},{1,25},{9,17},{17,9},{25,1},{2,26},{10... | collective-permute-start | bytes 196616 | tf_op jit(solution)/shard_map/ppermute | solution.py:218
  10.6 0.1 collective-permute-start.10
  10.8 0.1 maximum_select_fusion.3
  10.9 0.1 maximum_select_fusion.2
  11.0 2.3 %collective-permute-start.11 = (bf16[4,1,2,2,2,16,128]{6,5,4,3,2,1,0:T(8,128)(2,1)S(1)}, bf16[4,1,2,2,2,16,128]{6,5,4,3,2,1,0:T(8,128)(2,1)S(1)}, u32[]{:S(2)}, u32[]{:S(2)}) collective-permute-start(bf16[4,1,2,2,2,16,128]{6,5,4,3,2,1,0:T(8,128)(2,1)S(1)} %get-tuple-element.40), channel_id=1, source_target_pairs={{0,5},{1,4},{2,7},{3,6},{4,1},{5,0},{6,3},{7,2},{8,13},{9,12},{10,... | collective-permute-start | bytes 393224 | tf_op jit(solution)/shard_map/ppermute | solution.py:221
  13.3 0.2 collective-permute-start.8
  13.5 0.7 %collective-permute-done.2 = bf16[2,1,2,2,2,16,128]{6,5,4,3,2,1,0:T(8,128)(2,1)S(1)} collective-permute-done((bf16[2,1,2,2,2,16,128]{6,5,4,3,2,1,0:T(8,128)(2,1)S(1)}, bf16[2,1,2,2,2,16,128]{6,5,4,3,2,1,0:T(8,128)(2,1)S(1)}, u32[]{:S(2)}, u32[]{:S(2)}) %collective-permute-start.2) | collective-permute-done | bytes 65568 | tf_op jit(solution)/shard_map/ppermute | solution.py:218
  14.2 1.7 %collective-permute-start.9 = (bf16[4,1,2,2,2,16,128]{6,5,4,3,2,1,0:T(8,128)(2,1)S(1)}, bf16[4,1,2,2,2,16,128]{6,5,4,3,2,1,0:T(8,128)(2,1)S(1)}, u32[]{:S(2)}, u32[]{:S(2)}) collective-permute-start(bf16[4,1,2,2,2,16,128]{6,5,4,3,2,1,0:T(8,128)(2,1)S(1)} %maximum_select_fusion.3), channel_id=1, source_target_pairs={{0,3},{1,2},{2,1},{3,0},{4,7},{5,6},{6,5},{7,4},{8,11},{9,10},{10,... | collective-permute-start | bytes 393224 | tf_op jit(solution)/shard_map/ppermute | solution.py:221
  15.9 0.1 maximum_select_fusion.1
  15.9 0.1 maximum_select_fusion
  16.1 0.1 broadcast_select_fusion
  16.2 6.4 %collective-permute-done.10 = bf16[4,1,2,2,2,16,128]{6,5,4,3,2,1,0:T(8,128)(2,1)S(1)} collective-permute-done((bf16[4,1,2,2,2,16,128]{6,5,4,3,2,1,0:T(8,128)(2,1)S(1)}, bf16[4,1,2,2,2,16,128]{6,5,4,3,2,1,0:T(8,128)(2,1)S(1)}, u32[]{:S(2)}, u32[]{:S(2)}) %collective-permute-start.10) | collective-permute-done | bytes 131104 | tf_op jit(solution)/shard_map/ppermute | solution.py:221
  22.7 3.2 %collective-permute-done.11 = bf16[4,1,2,2,2,16,128]{6,5,4,3,2,1,0:T(8,128)(2,1)S(1)} collective-permute-done((bf16[4,1,2,2,2,16,128]{6,5,4,3,2,1,0:T(8,128)(2,1)S(1)}, bf16[4,1,2,2,2,16,128]{6,5,4,3,2,1,0:T(8,128)(2,1)S(1)}, u32[]{:S(2)}, u32[]{:S(2)}) %collective-permute-start.11) | collective-permute-done | bytes 131104 | tf_op jit(solution)/shard_map/ppermute | solution.py:221
  25.9 0.6 %collective-permute-start.16 = (bf16[2,1,2,2,2,16,128]{6,5,4,3,2,1,0:T(8,128)(2,1)S(1)}, bf16[2,1,2,2,2,16,128]{6,5,4,3,2,1,0:T(8,128)(2,1)S(1)}, u32[]{:S(2)}, u32[]{:S(2)}) collective-permute-start(bf16[2,1,2,2,2,16,128]{6,5,4,3,2,1,0:T(8,128)(2,1)S(1)} %pad_maximum_fusion.3), channel_id=1, source_target_pairs={{0,8},{8,0},{16,24},{24,16},{1,9},{9,1},{17,25},{25,17},{2,10},{10... | collective-permute-start | bytes 196616 | tf_op jit(solution)/shard_map/ppermute | solution.py:218
  26.7 1.3 %collective-permute-start.17 = (bf16[2,1,2,2,2,16,128]{6,5,4,3,2,1,0:T(8,128)(2,1)S(1)}, bf16[2,1,2,2,2,16,128]{6,5,4,3,2,1,0:T(8,128)(2,1)S(1)}, u32[]{:S(2)}, u32[]{:S(2)}) collective-permute-start(bf16[2,1,2,2,2,16,128]{6,5,4,3,2,1,0:T(8,128)(2,1)S(1)} %pad_maximum_fusion.4), channel_id=1, source_target_pairs={{0,16},{8,24},{16,0},{24,8},{1,17},{9,25},{17,1},{25,9},{2,18},{10... | collective-permute-start | bytes 196616 | tf_op jit(solution)/shard_map/ppermute | solution.py:218
  28.0 4.6 %collective-permute-done.9.rest_3_ = bf16[4,1,2,2,2,16,128]{6,5,4,3,2,1,0:T(8,128)(2,1)S(1)} collective-permute-done((bf16[4,1,2,2,2,16,128]{6,5,4,3,2,1,0:T(8,128)(2,1)S(1)}, bf16[4,1,2,2,2,16,128]{6,5,4,3,2,1,0:T(8,128)(2,1)S(1)}, u32[]{:S(2)}, u32[]{:S(2)}) %collective-permute-start.9) | collective-permute-done | bytes 131104 | tf_op jit(solution)/shard_map/ppermute | solution.py:221
  32.6 2.7 %collective-permute-start.18 = (bf16[2,1,2,2,2,16,128]{6,5,4,3,2,1,0:T(8,128)(2,1)S(1)}, bf16[2,1,2,2,2,16,128]{6,5,4,3,2,1,0:T(8,128)(2,1)S(1)}, u32[]{:S(2)}, u32[]{:S(2)}) collective-permute-start(bf16[2,1,2,2,2,16,128]{6,5,4,3,2,1,0:T(8,128)(2,1)S(1)} %pad_maximum_fusion.5), channel_id=1, source_target_pairs={{0,24},{8,16},{16,8},{24,0},{1,25},{9,17},{17,9},{25,1},{2,26},{10... | collective-permute-start | bytes 196616 | tf_op jit(solution)/shard_map/ppermute | solution.py:218
  35.4 0.3 collective-permute-start.13
  35.7 2.4 %collective-permute-done.18.rest_6_ = bf16[2,1,2,2,2,16,128]{6,5,4,3,2,1,0:T(8,128)(2,1)S(1)} collective-permute-done((bf16[2,1,2,2,2,16,128]{6,5,4,3,2,1,0:T(8,128)(2,1)S(1)}, bf16[2,1,2,2,2,16,128]{6,5,4,3,2,1,0:T(8,128)(2,1)S(1)}, u32[]{:S(2)}, u32[]{:S(2)}) %collective-permute-start.18) | collective-permute-done | bytes 65568 | tf_op jit(solution)/shard_map/ppermute | solution.py:218
  38.1 0.8 %collective-permute-start.14 = (bf16[2,1,2,2,2,16,128]{6,5,4,3,2,1,0:T(8,128)(2,1)S(1)}, bf16[2,1,2,2,2,16,128]{6,5,4,3,2,1,0:T(8,128)(2,1)S(1)}, u32[]{:S(2)}, u32[]{:S(2)}) collective-permute-start(bf16[2,1,2,2,2,16,128]{6,5,4,3,2,1,0:T(8,128)(2,1)S(1)} %pad_maximum_fusion.2), channel_id=1, source_target_pairs={{0,24},{8,16},{16,8},{24,0},{1,25},{9,17},{17,9},{25,1},{2,26},{10... | collective-permute-start | bytes 196616 | tf_op jit(solution)/shard_map/ppermute | solution.py:218
  39.0 0.8 %shard_map.39.rest_7_ = bf16[2,8,2,128,128]{4,3,2,1,0:T(8,128)(2,1)} custom-call(bf16[1,1,2,2,2,16,128]{6,5,4,3,2,1,0:T(8,128)(2,1)S(1)} %get-tuple-element.55.rest_0_, bf16[1,1,2,2,2,16,128]{6,5,4,3,2,1,0:T(8,128)(2,1)S(1)} %get-tuple-element.51.rest_1_, bf16[1,1,2,2,2,16,128]{6,5,4,3,2,1,0:T(8,128)(2,1)S(1)} %get-tuple-element.46.rest_2_, ...), custom_call_target="tpu_custom_call" | custom-call | tf_op jit(solution)/shard_map/pallas_call | solution.py:191
  39.8 2.4 %collective-permute-done.14.rest_6_ = bf16[2,1,2,2,2,16,128]{6,5,4,3,2,1,0:T(8,128)(2,1)S(1)} collective-permute-done((bf16[2,1,2,2,2,16,128]{6,5,4,3,2,1,0:T(8,128)(2,1)S(1)}, bf16[2,1,2,2,2,16,128]{6,5,4,3,2,1,0:T(8,128)(2,1)S(1)}, u32[]{:S(2)}, u32[]{:S(2)}) %collective-permute-start.14) | collective-permute-done | bytes 65568 | tf_op jit(solution)/shard_map/ppermute | solution.py:218
  42.2 1.0 %shard_map.40 = bf16[2,8,2,128,128]{4,3,2,1,0:T(8,128)(2,1)} custom-call(bf16[4,1,2,2,2,16,128]{6,5,4,3,2,1,0:T(8,128)(2,1)S(1)} %collective-permute-done.3.rest_0_, bf16[4,1,2,2,2,16,128]{6,5,4,3,2,1,0:T(8,128)(2,1)S(1)} %collective-permute-done.4.rest_1_, ...), custom_call_target="tpu_custom_call", output_to_operand_aliasing={{}: (7, {})} | custom-call | tf_op jit(solution)/shard_map/pallas_call | solution.py:191
  (44 shorter events, 0.6 us)
Async XLA Ops:
  1.8 7.0 %collective-permute-start.5 = (bf16[2,1,2,2,2,16,128]{6,5,4,3,2,1,0:T(8,128)(2,1)S(1)}, bf16[2,1,2,2,2,16,128]{6,5,4,3,2,1,0:T(8,128)(2,1)S(1)}, u32[]{:S(2)}, u32[]{:S(2)}) collective-permute-start(bf16[2,1,2,2,2,16,128]{6,5,4,3,2,1,0:T(8,128)(2,1)S(1)} %get-tuple-element.36), channel_id=1, source_target_pairs={{0,8},{8,0},{16,24},{24,16},{1,9},{9,1},{17,25},{25,17},{2,10},{10... | collective-permute-start | bytes 196616 | tf_op jit(solution)/shard_map/ppermute | solution.py:218
  2.6 7.5 %collective-permute-start.6 = (bf16[2,1,2,2,2,16,128]{6,5,4,3,2,1,0:T(8,128)(2,1)S(1)}, bf16[2,1,2,2,2,16,128]{6,5,4,3,2,1,0:T(8,128)(2,1)S(1)}, u32[]{:S(2)}, u32[]{:S(2)}) collective-permute-start(bf16[2,1,2,2,2,16,128]{6,5,4,3,2,1,0:T(8,128)(2,1)S(1)} %get-tuple-element.37), channel_id=1, source_target_pairs={{0,16},{8,24},{16,0},{24,8},{1,17},{9,25},{17,1},{25,9},{2,18},{10... | collective-permute-start | bytes 196616 | tf_op jit(solution)/shard_map/ppermute | solution.py:218
  3.8 6.9 %collective-permute-start.7 = (bf16[2,1,2,2,2,16,128]{6,5,4,3,2,1,0:T(8,128)(2,1)S(1)}, bf16[2,1,2,2,2,16,128]{6,5,4,3,2,1,0:T(8,128)(2,1)S(1)}, u32[]{:S(2)}, u32[]{:S(2)}) collective-permute-start(bf16[2,1,2,2,2,16,128]{6,5,4,3,2,1,0:T(8,128)(2,1)S(1)} %get-tuple-element.38), channel_id=1, source_target_pairs={{0,24},{8,16},{16,8},{24,0},{1,25},{9,17},{17,9},{25,1},{2,26},{10... | collective-permute-start | bytes 196616 | tf_op jit(solution)/shard_map/ppermute | solution.py:218
  4.3 11.8 %collective-permute-start.15 = (bf16[4,1,2,2,2,16,128]{6,5,4,3,2,1,0:T(8,128)(2,1)S(1)}, bf16[4,1,2,2,2,16,128]{6,5,4,3,2,1,0:T(8,128)(2,1)S(1)}, u32[]{:S(2)}, u32[]{:S(2)}) collective-permute-start(bf16[4,1,2,2,2,16,128]{6,5,4,3,2,1,0:T(8,128)(2,1)S(1)} %get-tuple-element.42), channel_id=1, source_target_pairs={{0,1},{1,0},{2,3},{3,2},{4,5},{5,4},{6,7},{7,6},{8,9},{9,8},{10,11... | collective-permute-start | bytes 393224 | tf_op jit(solution)/shard_map/ppermute | solution.py:221
  7.3 3.6 %collective-permute-start = (bf16[2,1,2,2,2,16,128]{6,5,4,3,2,1,0:T(8,128)(2,1)S(1)}, bf16[2,1,2,2,2,16,128]{6,5,4,3,2,1,0:T(8,128)(2,1)S(1)}, u32[]{:S(2)}, u32[]{:S(2)}) collective-permute-start(bf16[2,1,2,2,2,16,128]{6,5,4,3,2,1,0:T(8,128)(2,1)S(1)} %get-tuple-element.32), channel_id=1, source_target_pairs={{0,8},{8,0},{16,24},{24,16},{1,9},{9,1},{17,25},{25,17},{2,10},{10... | collective-permute-start | bytes 196616 | tf_op jit(solution)/shard_map/ppermute | solution.py:218
  8.8 4.5 %collective-permute-start.1 = (bf16[2,1,2,2,2,16,128]{6,5,4,3,2,1,0:T(8,128)(2,1)S(1)}, bf16[2,1,2,2,2,16,128]{6,5,4,3,2,1,0:T(8,128)(2,1)S(1)}, u32[]{:S(2)}, u32[]{:S(2)}) collective-permute-start(bf16[2,1,2,2,2,16,128]{6,5,4,3,2,1,0:T(8,128)(2,1)S(1)} %get-tuple-element.33), channel_id=1, source_target_pairs={{0,16},{8,24},{16,0},{24,8},{1,17},{9,25},{17,1},{25,9},{2,18},{10... | collective-permute-start | bytes 196616 | tf_op jit(solution)/shard_map/ppermute | solution.py:218
  10.1 4.1 %collective-permute-start.2 = (bf16[2,1,2,2,2,16,128]{6,5,4,3,2,1,0:T(8,128)(2,1)S(1)}, bf16[2,1,2,2,2,16,128]{6,5,4,3,2,1,0:T(8,128)(2,1)S(1)}, u32[]{:S(2)}, u32[]{:S(2)}) collective-permute-start(bf16[2,1,2,2,2,16,128]{6,5,4,3,2,1,0:T(8,128)(2,1)S(1)} %get-tuple-element.34), channel_id=1, source_target_pairs={{0,24},{8,16},{16,8},{24,0},{1,25},{9,17},{17,9},{25,1},{2,26},{10... | collective-permute-start | bytes 196616 | tf_op jit(solution)/shard_map/ppermute | solution.py:218
  10.6 12.0 %collective-permute-start.10 = (bf16[4,1,2,2,2,16,128]{6,5,4,3,2,1,0:T(8,128)(2,1)S(1)}, bf16[4,1,2,2,2,16,128]{6,5,4,3,2,1,0:T(8,128)(2,1)S(1)}, u32[]{:S(2)}, u32[]{:S(2)}) collective-permute-start(bf16[4,1,2,2,2,16,128]{6,5,4,3,2,1,0:T(8,128)(2,1)S(1)} %get-tuple-element.39), channel_id=1, source_target_pairs={{0,4},{1,5},{2,6},{3,7},{4,0},{5,1},{6,2},{7,3},{8,12},{9,13},{10,... | collective-permute-start | bytes 393224 | tf_op jit(solution)/shard_map/ppermute | solution.py:221
  11.0 15.0 %collective-permute-start.11 = (bf16[4,1,2,2,2,16,128]{6,5,4,3,2,1,0:T(8,128)(2,1)S(1)}, bf16[4,1,2,2,2,16,128]{6,5,4,3,2,1,0:T(8,128)(2,1)S(1)}, u32[]{:S(2)}, u32[]{:S(2)}) collective-permute-start(bf16[4,1,2,2,2,16,128]{6,5,4,3,2,1,0:T(8,128)(2,1)S(1)} %get-tuple-element.40), channel_id=1, source_target_pairs={{0,5},{1,4},{2,7},{3,6},{4,1},{5,0},{6,3},{7,2},{8,13},{9,12},{10,... | collective-permute-start | bytes 393224 | tf_op jit(solution)/shard_map/ppermute | solution.py:221
  13.3 13.4 %collective-permute-start.8 = (bf16[4,1,2,2,2,16,128]{6,5,4,3,2,1,0:T(8,128)(2,1)S(1)}, bf16[4,1,2,2,2,16,128]{6,5,4,3,2,1,0:T(8,128)(2,1)S(1)}, u32[]{:S(2)}, u32[]{:S(2)}) collective-permute-start(bf16[4,1,2,2,2,16,128]{6,5,4,3,2,1,0:T(8,128)(2,1)S(1)} %maximum_select_fusion.2), channel_id=1, source_target_pairs={{0,2},{1,3},{2,0},{3,1},{4,6},{5,7},{6,4},{7,5},{8,10},{9,11},{10,... | collective-permute-start | bytes 393224 | tf_op jit(solution)/shard_map/ppermute | solution.py:221
  14.2 18.4 %collective-permute-start.9 = (bf16[4,1,2,2,2,16,128]{6,5,4,3,2,1,0:T(8,128)(2,1)S(1)}, bf16[4,1,2,2,2,16,128]{6,5,4,3,2,1,0:T(8,128)(2,1)S(1)}, u32[]{:S(2)}, u32[]{:S(2)}) collective-permute-start(bf16[4,1,2,2,2,16,128]{6,5,4,3,2,1,0:T(8,128)(2,1)S(1)} %maximum_select_fusion.3), channel_id=1, source_target_pairs={{0,3},{1,2},{2,1},{3,0},{4,7},{5,6},{6,5},{7,4},{8,11},{9,10},{10,... | collective-permute-start | bytes 393224 | tf_op jit(solution)/shard_map/ppermute | solution.py:221
  16.0 23.7 %collective-permute-start.3 = (bf16[4,1,2,2,2,16,128]{6,5,4,3,2,1,0:T(8,128)(2,1)S(1)}, bf16[4,1,2,2,2,16,128]{6,5,4,3,2,1,0:T(8,128)(2,1)S(1)}, u32[]{:S(2)}, u32[]{:S(2)}) collective-permute-start(bf16[4,1,2,2,2,16,128]{6,5,4,3,2,1,0:T(8,128)(2,1)S(1)} %maximum_select_fusion), channel_id=1, source_target_pairs={{0,6},{1,7},{2,4},{3,5},{4,2},{5,3},{6,0},{7,1},{8,14},{9,15},{10,... | collective-permute-start | bytes 393224 | tf_op jit(solution)/shard_map/ppermute | solution.py:221
  22.6 17.2 %collective-permute-start.4 = (bf16[4,1,2,2,2,16,128]{6,5,4,3,2,1,0:T(8,128)(2,1)S(1)}, bf16[4,1,2,2,2,16,128]{6,5,4,3,2,1,0:T(8,128)(2,1)S(1)}, u32[]{:S(2)}, u32[]{:S(2)}) collective-permute-start(bf16[4,1,2,2,2,16,128]{6,5,4,3,2,1,0:T(8,128)(2,1)S(1)} %maximum_select_fusion.1), channel_id=1, source_target_pairs={{0,7},{1,6},{2,5},{3,4},{4,3},{5,2},{6,1},{7,0},{8,15},{9,14},{10,... | collective-permute-start | bytes 393224 | tf_op jit(solution)/shard_map/ppermute | solution.py:221
  25.9 9.4 %collective-permute-start.16 = (bf16[2,1,2,2,2,16,128]{6,5,4,3,2,1,0:T(8,128)(2,1)S(1)}, bf16[2,1,2,2,2,16,128]{6,5,4,3,2,1,0:T(8,128)(2,1)S(1)}, u32[]{:S(2)}, u32[]{:S(2)}) collective-permute-start(bf16[2,1,2,2,2,16,128]{6,5,4,3,2,1,0:T(8,128)(2,1)S(1)} %pad_maximum_fusion.3), channel_id=1, source_target_pairs={{0,8},{8,0},{16,24},{24,16},{1,9},{9,1},{17,25},{25,17},{2,10},{10... | collective-permute-start | bytes 196616 | tf_op jit(solution)/shard_map/ppermute | solution.py:218
  26.7 8.7 %collective-permute-start.17 = (bf16[2,1,2,2,2,16,128]{6,5,4,3,2,1,0:T(8,128)(2,1)S(1)}, bf16[2,1,2,2,2,16,128]{6,5,4,3,2,1,0:T(8,128)(2,1)S(1)}, u32[]{:S(2)}, u32[]{:S(2)}) collective-permute-start(bf16[2,1,2,2,2,16,128]{6,5,4,3,2,1,0:T(8,128)(2,1)S(1)} %pad_maximum_fusion.4), channel_id=1, source_target_pairs={{0,16},{8,24},{16,0},{24,8},{1,17},{9,25},{17,1},{25,9},{2,18},{10... | collective-permute-start | bytes 196616 | tf_op jit(solution)/shard_map/ppermute | solution.py:218
  32.6 5.5 %collective-permute-start.18 = (bf16[2,1,2,2,2,16,128]{6,5,4,3,2,1,0:T(8,128)(2,1)S(1)}, bf16[2,1,2,2,2,16,128]{6,5,4,3,2,1,0:T(8,128)(2,1)S(1)}, u32[]{:S(2)}, u32[]{:S(2)}) collective-permute-start(bf16[2,1,2,2,2,16,128]{6,5,4,3,2,1,0:T(8,128)(2,1)S(1)} %pad_maximum_fusion.5), channel_id=1, source_target_pairs={{0,24},{8,16},{16,8},{24,0},{1,25},{9,17},{17,9},{25,1},{2,26},{10... | collective-permute-start | bytes 196616 | tf_op jit(solution)/shard_map/ppermute | solution.py:218
  35.3 4.5 %collective-permute-start.12 = (bf16[2,1,2,2,2,16,128]{6,5,4,3,2,1,0:T(8,128)(2,1)S(1)}, bf16[2,1,2,2,2,16,128]{6,5,4,3,2,1,0:T(8,128)(2,1)S(1)}, u32[]{:S(2)}, u32[]{:S(2)}) collective-permute-start(bf16[2,1,2,2,2,16,128]{6,5,4,3,2,1,0:T(8,128)(2,1)S(1)} %pad_maximum_fusion), channel_id=1, source_target_pairs={{0,8},{8,0},{16,24},{24,16},{1,9},{9,1},{17,25},{25,17},{2,10},{10... | collective-permute-start | bytes 196616 | tf_op jit(solution)/shard_map/ppermute | solution.py:218
  35.4 4.4 %collective-permute-start.13 = (bf16[2,1,2,2,2,16,128]{6,5,4,3,2,1,0:T(8,128)(2,1)S(1)}, bf16[2,1,2,2,2,16,128]{6,5,4,3,2,1,0:T(8,128)(2,1)S(1)}, u32[]{:S(2)}, u32[]{:S(2)}) collective-permute-start(bf16[2,1,2,2,2,16,128]{6,5,4,3,2,1,0:T(8,128)(2,1)S(1)} %pad_maximum_fusion.1), channel_id=1, source_target_pairs={{0,16},{8,24},{16,0},{24,8},{1,17},{9,25},{17,1},{25,9},{2,18},{10... | collective-permute-start | bytes 196616 | tf_op jit(solution)/shard_map/ppermute | solution.py:218
  38.1 4.1 %collective-permute-start.14 = (bf16[2,1,2,2,2,16,128]{6,5,4,3,2,1,0:T(8,128)(2,1)S(1)}, bf16[2,1,2,2,2,16,128]{6,5,4,3,2,1,0:T(8,128)(2,1)S(1)}, u32[]{:S(2)}, u32[]{:S(2)}) collective-permute-start(bf16[2,1,2,2,2,16,128]{6,5,4,3,2,1,0:T(8,128)(2,1)S(1)} %pad_maximum_fusion.2), channel_id=1, source_target_pairs={{0,24},{8,16},{16,8},{24,0},{1,25},{9,17},{17,9},{25,1},{2,26},{10... | collective-permute-start | bytes 196616 | tf_op jit(solution)/shard_map/ppermute | solution.py:218

commit v5 on v4

--- a/solution.py
+++ b/solution.py
@@ -253,11 +253,10 @@
     small_in = [without_padding(array, k, tok ^ k) for array, k in zip(small_in, small)]
     small_mine = [over_layer(joined(small_in, j), j) for j in layers if j]
 
-    def ready(arrays, n, k):
-        return without_padding(joined(arrays, n), k, tok)
-
-    late_in = [over_tok(ready(late_mine, n, k), k) for n, k in enumerate(late)]
-    middle_in = [over_tok(ready(middle_mine, n, k), k) for n, k in enumerate(middle)]
+    late_in = [over_tok(joined(late_mine, n), k) for n, k in enumerate(late)]
+    late_in = [without_padding(array, k, tok ^ k) for array, k in zip(late_in, late)]
+    middle_out = [without_padding(joined(middle_mine, n), k, tok) for n, k in enumerate(middle)]
+    middle_in = [over_tok(array, k) for array, k in zip(middle_out, middle)]
     early_mine = [over_layer(joined(early_in, j), j) for j in layers if j]
     out = placed(
         [(array[:1], [(0, k)]) for array, k in zip(early_in + small_in, early + small)]

time: 43.4 us -> 45.3 us (1.044)
  the two profiles are of different devices: /device:TPU:25 before, /device:TPU:0 now
where the time goes in v5:
time: 45.3 us; the launch traced here: 44.6 us
  starting transfers between devices  22.8 us (50%)
  waiting for transfers between devices  14.5 us (32%)
  Pallas kernels  5.48 us (12%)
  between operations  0.98 us (2%)
  other arithmetic  0.82 us (2%)
    ppermute x7, starting transfers between devices, over_tok(): return lax.ppermute(array, 'tok', [(i, i ^ k) for i in range(tok_count)])  13.6 us
    ppermute x7, waiting for transfers between devices, over_tok(): return lax.ppermute(array, 'tok', [(i, i ^ k) for i in range(tok_count)])  12 us
    ppermute x12, starting transfers between devices, over_layer(): return lax.ppermute(array, 'layer', [(i, i ^ j) for i in range(groups)])  9.1 us
    pallas_call x2, Pallas kernels, merged(): pl.pallas_call(functools.partial(merge_kernel, plan=plan, always=tuple(al...  3.63 us
    ppermute x12, waiting for transfers between devices, over_layer(): return lax.ppermute(array, 'layer', [(i, i ^ j) for i in range(groups)])  2.46 us
    pallas_call x2, Pallas kernels, placed(): pl.pallas_call(functools.partial(place_kernel, plan=plan, rounds=rounds,...  1.84 us
  transfers between devices with their start and end apart: 19, of which 6 were waited for; matrix products, arithmetic and copies ran while one was open for 2% of the time, Pallas kernels for 6%

profile of v5, /device:TPU:0, one launch (start us, length us, event | category | flops | bytes accessed | tf_op | source)
XLA Modules:
  0.0 44.6 jit_solution(18278993907720961426)
XLA Ops:
  0.0 1.8 %shard_map.38 = (bf16[2,1,2,2,2,16,128]{6,5,4,3,2,1,0:T(8,128)(2,1)S(1)}, bf16[2,1,2,2,2,16,128]{6,5,4,3,2,1,0:T(8,128)(2,1)S(1)}, bf16[2,1,2,2,2,16,128]{6,5,4,...) custom-call(s32[1,128]{1,0:T(1,128)} %bitcast.13, ...), custom_call_target="tpu_custom_call" | custom-call | tf_op jit(solution)/shard_map/pallas_call | solution.py:136
  1.8 0.6 %collective-permute-start.5 = (bf16[2,1,2,2,2,16,128]{6,5,4,3,2,1,0:T(8,128)(2,1)S(1)}, bf16[2,1,2,2,2,16,128]{6,5,4,3,2,1,0:T(8,128)(2,1)S(1)}, u32[]{:S(2)}, u32[]{:S(2)}) collective-permute-start(bf16[2,1,2,2,2,16,128]{6,5,4,3,2,1,0:T(8,128)(2,1)S(1)} %get-tuple-element.36), channel_id=1, source_target_pairs={{0,8},{8,0},{16,24},{24,16},{1,9},{9,1},{17,25},{25,17},{2,10},{10... | collective-permute-start | bytes 196616 | tf_op jit(solution)/shard_map/ppermute | solution.py:218
  2.4 2.6 %collective-permute-start.6 = (bf16[2,1,2,2,2,16,128]{6,5,4,3,2,1,0:T(8,128)(2,1)S(1)}, bf16[2,1,2,2,2,16,128]{6,5,4,3,2,1,0:T(8,128)(2,1)S(1)}, u32[]{:S(2)}, u32[]{:S(2)}) collective-permute-start(bf16[2,1,2,2,2,16,128]{6,5,4,3,2,1,0:T(8,128)(2,1)S(1)} %get-tuple-element.37), channel_id=1, source_target_pairs={{0,16},{8,24},{16,0},{24,8},{1,17},{9,25},{17,1},{25,9},{2,18},{10... | collective-permute-start | bytes 196616 | tf_op jit(solution)/shard_map/ppermute | solution.py:218
  5.0 1.8 %collective-permute-start.15 = (bf16[4,1,2,2,2,16,128]{6,5,4,3,2,1,0:T(8,128)(2,1)S(1)}, bf16[4,1,2,2,2,16,128]{6,5,4,3,2,1,0:T(8,128)(2,1)S(1)}, u32[]{:S(2)}, u32[]{:S(2)}) collective-permute-start(bf16[4,1,2,2,2,16,128]{6,5,4,3,2,1,0:T(8,128)(2,1)S(1)} %get-tuple-element.42), channel_id=1, source_target_pairs={{0,1},{1,0},{2,3},{3,2},{4,5},{5,4},{6,7},{7,6},{8,9},{9,8},{10,11... | collective-permute-start | bytes 393224 | tf_op jit(solution)/shard_map/ppermute | solution.py:221
  6.7 1.8 %shard_map.37 = (bf16[4,1,2,2,2,16,128]{6,5,4,3,2,1,0:T(8,128)(2,1)S(1)}, bf16[4,1,2,2,2,16,128]{6,5,4,3,2,1,0:T(8,128)(2,1)S(1)}, bf16[2,1,2,2,2,16,128]{6,5,4,...) custom-call(s32[1,128]{1,0:T(1,128)} %bitcast.14, ...), custom_call_target="tpu_custom_call" | custom-call | tf_op jit(solution)/shard_map/pallas_call | solution.py:136
  8.6 0.1 collective-permute-start
  9.4 0.1 broadcast_select_fusion.1
  9.6 1.6 %collective-permute-start.1 = (bf16[2,1,2,2,2,16,128]{6,5,4,3,2,1,0:T(8,128)(2,1)S(1)}, bf16[2,1,2,2,2,16,128]{6,5,4,3,2,1,0:T(8,128)(2,1)S(1)}, u32[]{:S(2)}, u32[]{:S(2)}) collective-permute-start(bf16[2,1,2,2,2,16,128]{6,5,4,3,2,1,0:T(8,128)(2,1)S(1)} %get-tuple-element.33), channel_id=1, source_target_pairs={{0,16},{8,24},{16,0},{24,8},{1,17},{9,25},{17,1},{25,9},{2,18},{10... | collective-permute-start | bytes 196616 | tf_op jit(solution)/shard_map/ppermute | solution.py:218
  11.2 0.4 collective-permute-start.2
  11.6 2.7 %collective-permute-start.10 = (bf16[4,1,2,2,2,16,128]{6,5,4,3,2,1,0:T(8,128)(2,1)S(1)}, bf16[4,1,2,2,2,16,128]{6,5,4,3,2,1,0:T(8,128)(2,1)S(1)}, u32[]{:S(2)}, u32[]{:S(2)}) collective-permute-start(bf16[4,1,2,2,2,16,128]{6,5,4,3,2,1,0:T(8,128)(2,1)S(1)} %get-tuple-element.39), channel_id=1, source_target_pairs={{0,4},{1,5},{2,6},{3,7},{4,0},{5,1},{6,2},{7,3},{8,12},{9,13},{10,... | collective-permute-start | bytes 393224 | tf_op jit(solution)/shard_map/ppermute | solution.py:221
  14.2 0.1 maximum_select_fusion
  14.3 0.1 collective-permute-start.11
  14.5 1.9 %collective-permute-start.8 = (bf16[4,1,2,2,2,16,128]{6,5,4,3,2,1,0:T(8,128)(2,1)S(1)}, bf16[4,1,2,2,2,16,128]{6,5,4,3,2,1,0:T(8,128)(2,1)S(1)}, u32[]{:S(2)}, u32[]{:S(2)}) collective-permute-start(bf16[4,1,2,2,2,16,128]{6,5,4,3,2,1,0:T(8,128)(2,1)S(1)} %maximum_select_fusion), channel_id=1, source_target_pairs={{0,2},{1,3},{2,0},{3,1},{4,6},{5,7},{6,4},{7,5},{8,10},{9,11},{10,... | collective-permute-start | bytes 393224 | tf_op jit(solution)/shard_map/ppermute | solution.py:221
  16.4 2.6 %collective-permute-start.3 = (bf16[4,1,2,2,2,16,128]{6,5,4,3,2,1,0:T(8,128)(2,1)S(1)}, bf16[4,1,2,2,2,16,128]{6,5,4,3,2,1,0:T(8,128)(2,1)S(1)}, u32[]{:S(2)}, u32[]{:S(2)}) collective-permute-start(bf16[4,1,2,2,2,16,128]{6,5,4,3,2,1,0:T(8,128)(2,1)S(1)} %pad_maximum_fusion), channel_id=1, source_target_pairs={{0,6},{1,7},{2,4},{3,5},{4,2},{5,3},{6,0},{7,1},{8,14},{9,15},{10,... | collective-permute-start | bytes 393224 | tf_op jit(solution)/shard_map/ppermute | solution.py:221
  19.0 0.1 maximum_select_fusion.1
  19.2 2.3 %collective-permute-start.4 = (bf16[4,1,2,2,2,16,128]{6,5,4,3,2,1,0:T(8,128)(2,1)S(1)}, bf16[4,1,2,2,2,16,128]{6,5,4,3,2,1,0:T(8,128)(2,1)S(1)}, u32[]{:S(2)}, u32[]{:S(2)}) collective-permute-start(bf16[4,1,2,2,2,16,128]{6,5,4,3,2,1,0:T(8,128)(2,1)S(1)} %pad_maximum_fusion.1), channel_id=1, source_target_pairs={{0,7},{1,6},{2,5},{3,4},{4,3},{5,2},{6,1},{7,0},{8,15},{9,14},{10,... | collective-permute-start | bytes 393224 | tf_op jit(solution)/shard_map/ppermute | solution.py:221
  21.6 3.0 %collective-permute-done.10 = bf16[4,1,2,2,2,16,128]{6,5,4,3,2,1,0:T(8,128)(2,1)S(1)} collective-permute-done((bf16[4,1,2,2,2,16,128]{6,5,4,3,2,1,0:T(8,128)(2,1)S(1)}, bf16[4,1,2,2,2,16,128]{6,5,4,3,2,1,0:T(8,128)(2,1)S(1)}, u32[]{:S(2)}, u32[]{:S(2)}) %collective-permute-start.10) | collective-permute-done | bytes 131104 | tf_op jit(solution)/shard_map/ppermute | solution.py:221
  24.5 0.1 broadcast_select_fusion.3
  24.7 8.0 %collective-permute-done.11 = bf16[4,1,2,2,2,16,128]{6,5,4,3,2,1,0:T(8,128)(2,1)S(1)} collective-permute-done((bf16[4,1,2,2,2,16,128]{6,5,4,3,2,1,0:T(8,128)(2,1)S(1)}, bf16[4,1,2,2,2,16,128]{6,5,4,3,2,1,0:T(8,128)(2,1)S(1)}, u32[]{:S(2)}, u32[]{:S(2)}) %collective-permute-start.11) | collective-permute-done | bytes 131104 | tf_op jit(solution)/shard_map/ppermute | solution.py:221
  32.7 1.7 %collective-permute-start.17 = (bf16[2,1,2,2,2,16,128]{6,5,4,3,2,1,0:T(8,128)(2,1)S(1)}, bf16[2,1,2,2,2,16,128]{6,5,4,3,2,1,0:T(8,128)(2,1)S(1)}, u32[]{:S(2)}, u32[]{:S(2)}) collective-permute-start(bf16[2,1,2,2,2,16,128]{6,5,4,3,2,1,0:T(8,128)(2,1)S(1)} %pad_maximum_fusion.6), channel_id=1, source_target_pairs={{0,16},{8,24},{16,0},{24,8},{1,17},{9,25},{17,1},{25,9},{2,18},{10... | collective-permute-start | bytes 196616 | tf_op jit(solution)/shard_map/ppermute | solution.py:218
  34.7 0.1 broadcast_select_fusion.5.rest_0_
  34.8 2.3 %collective-permute-start.9 = (bf16[4,1,2,2,2,16,128]{6,5,4,3,2,1,0:T(8,128)(2,1)S(1)}, bf16[4,1,2,2,2,16,128]{6,5,4,3,2,1,0:T(8,128)(2,1)S(1)}, u32[]{:S(2)}, u32[]{:S(2)}) collective-permute-start(bf16[4,1,2,2,2,16,128]{6,5,4,3,2,1,0:T(8,128)(2,1)S(1)} %maximum_select_fusion.1), channel_id=1, source_target_pairs={{0,3},{1,2},{2,1},{3,0},{4,7},{5,6},{6,5},{7,4},{8,11},{9,10},{10,... | collective-permute-start | bytes 393224 | tf_op jit(solution)/shard_map/ppermute | solution.py:221
  37.1 0.7 %collective-permute-start.12 = (bf16[2,1,2,2,2,16,128]{6,5,4,3,2,1,0:T(8,128)(2,1)S(1)}, bf16[2,1,2,2,2,16,128]{6,5,4,3,2,1,0:T(8,128)(2,1)S(1)}, u32[]{:S(2)}, u32[]{:S(2)}) collective-permute-start(bf16[2,1,2,2,2,16,128]{6,5,4,3,2,1,0:T(8,128)(2,1)S(1)} %pad_maximum_fusion.2), channel_id=1, source_target_pairs={{0,8},{8,0},{16,24},{24,16},{1,9},{9,1},{17,25},{25,17},{2,10},{10... | collective-permute-start | bytes 196616 | tf_op jit(solution)/shard_map/ppermute | solution.py:218
  37.8 0.6 %collective-permute-done.18.rest_6_ = bf16[2,1,2,2,2,16,128]{6,5,4,3,2,1,0:T(8,128)(2,1)S(1)} collective-permute-done((bf16[2,1,2,2,2,16,128]{6,5,4,3,2,1,0:T(8,128)(2,1)S(1)}, bf16[2,1,2,2,2,16,128]{6,5,4,3,2,1,0:T(8,128)(2,1)S(1)}, u32[]{:S(2)}, u32[]{:S(2)}) %collective-permute-start.18) | collective-permute-done | bytes 65568 | tf_op jit(solution)/shard_map/ppermute | solution.py:218
  38.4 1.0 %collective-permute-start.13 = (bf16[2,1,2,2,2,16,128]{6,5,4,3,2,1,0:T(8,128)(2,1)S(1)}, bf16[2,1,2,2,2,16,128]{6,5,4,3,2,1,0:T(8,128)(2,1)S(1)}, u32[]{:S(2)}, u32[]{:S(2)}) collective-permute-start(bf16[2,1,2,2,2,16,128]{6,5,4,3,2,1,0:T(8,128)(2,1)S(1)} %pad_maximum_fusion.3), channel_id=1, source_target_pairs={{0,16},{8,24},{16,0},{24,8},{1,17},{9,25},{17,1},{25,9},{2,18},{10... | collective-permute-start | bytes 196616 | tf_op jit(solution)/shard_map/ppermute | solution.py:218
  39.4 0.4 collective-permute-start.14
  39.8 0.1 broadcast_select_fusion.4.rest_1_
  39.9 0.8 %shard_map.39.rest_7_ = bf16[2,8,2,128,128]{4,3,2,1,0:T(8,128)(2,1)} custom-call(bf16[1,1,2,2,2,16,128]{6,5,4,3,2,1,0:T(8,128)(2,1)S(1)} %get-tuple-element.55.rest_0_, bf16[1,1,2,2,2,16,128]{6,5,4,3,2,1,0:T(8,128)(2,1)S(1)} %get-tuple-element.51.rest_1_, bf16[1,1,2,2,2,16,128]{6,5,4,3,2,1,0:T(8,128)(2,1)S(1)} %get-tuple-element.46.rest_2_, ...), custom_call_target="tpu_custom_call" | custom-call | tf_op jit(solution)/shard_map/pallas_call | solution.py:191
  40.7 1.0 %collective-permute-done.9.rest_3_ = bf16[4,1,2,2,2,16,128]{6,5,4,3,2,1,0:T(8,128)(2,1)S(1)} collective-permute-done((bf16[4,1,2,2,2,16,128]{6,5,4,3,2,1,0:T(8,128)(2,1)S(1)}, bf16[4,1,2,2,2,16,128]{6,5,4,3,2,1,0:T(8,128)(2,1)S(1)}, u32[]{:S(2)}, u32[]{:S(2)}) %collective-permute-start.9) | collective-permute-done | bytes 131104 | tf_op jit(solution)/shard_map/ppermute | solution.py:221
  41.7 1.2 %collective-permute-done.13.rest_5_ = bf16[2,1,2,2,2,16,128]{6,5,4,3,2,1,0:T(8,128)(2,1)S(1)} collective-permute-done((bf16[2,1,2,2,2,16,128]{6,5,4,3,2,1,0:T(8,128)(2,1)S(1)}, bf16[2,1,2,2,2,16,128]{6,5,4,3,2,1,0:T(8,128)(2,1)S(1)}, u32[]{:S(2)}, u32[]{:S(2)}) %collective-permute-start.13) | collective-permute-done | bytes 65568 | tf_op jit(solution)/shard_map/ppermute | solution.py:218
  42.9 0.7 %collective-permute-done.14.rest_6_ = bf16[2,1,2,2,2,16,128]{6,5,4,3,2,1,0:T(8,128)(2,1)S(1)} collective-permute-done((bf16[2,1,2,2,2,16,128]{6,5,4,3,2,1,0:T(8,128)(2,1)S(1)}, bf16[2,1,2,2,2,16,128]{6,5,4,3,2,1,0:T(8,128)(2,1)S(1)}, u32[]{:S(2)}, u32[]{:S(2)}) %collective-permute-start.14) | collective-permute-done | bytes 65568 | tf_op jit(solution)/shard_map/ppermute | solution.py:218
  43.6 1.0 %shard_map.40 = bf16[2,8,2,128,128]{4,3,2,1,0:T(8,128)(2,1)} custom-call(bf16[4,1,2,2,2,16,128]{6,5,4,3,2,1,0:T(8,128)(2,1)S(1)} %broadcast_select_fusion.5.rest_0_, bf16[4,1,2,2,2,16,128]{6,5,4,3,2,1,0:T(8,128)(2,1)S(1)} %broadcast_select_fusion.4.rest_1_, ...), custom_call_target="tpu_custom_call", output_to_operand_aliasing={{}: (7, {})} | custom-call | tf_op jit(solution)/shard_map/pallas_call | solution.py:191
  (45 shorter events, 0.6 us)
Async XLA Ops:
  1.8 7.8 %collective-permute-start.5 = (bf16[2,1,2,2,2,16,128]{6,5,4,3,2,1,0:T(8,128)(2,1)S(1)}, bf16[2,1,2,2,2,16,128]{6,5,4,3,2,1,0:T(8,128)(2,1)S(1)}, u32[]{:S(2)}, u32[]{:S(2)}) collective-permute-start(bf16[2,1,2,2,2,16,128]{6,5,4,3,2,1,0:T(8,128)(2,1)S(1)} %get-tuple-element.36), channel_id=1, source_target_pairs={{0,8},{8,0},{16,24},{24,16},{1,9},{9,1},{17,25},{25,17},{2,10},{10... | collective-permute-start | bytes 196616 | tf_op jit(solution)/shard_map/ppermute | solution.py:218
  2.4 8.8 %collective-permute-start.6 = (bf16[2,1,2,2,2,16,128]{6,5,4,3,2,1,0:T(8,128)(2,1)S(1)}, bf16[2,1,2,2,2,16,128]{6,5,4,3,2,1,0:T(8,128)(2,1)S(1)}, u32[]{:S(2)}, u32[]{:S(2)}) collective-permute-start(bf16[2,1,2,2,2,16,128]{6,5,4,3,2,1,0:T(8,128)(2,1)S(1)} %get-tuple-element.37), channel_id=1, source_target_pairs={{0,16},{8,24},{16,0},{24,8},{1,17},{9,25},{17,1},{25,9},{2,18},{10... | collective-permute-start | bytes 196616 | tf_op jit(solution)/shard_map/ppermute | solution.py:218
  4.9 6.6 %collective-permute-start.7 = (bf16[2,1,2,2,2,16,128]{6,5,4,3,2,1,0:T(8,128)(2,1)S(1)}, bf16[2,1,2,2,2,16,128]{6,5,4,3,2,1,0:T(8,128)(2,1)S(1)}, u32[]{:S(2)}, u32[]{:S(2)}) collective-permute-start(bf16[2,1,2,2,2,16,128]{6,5,4,3,2,1,0:T(8,128)(2,1)S(1)} %get-tuple-element.38), channel_id=1, source_target_pairs={{0,24},{8,16},{16,8},{24,0},{1,25},{9,17},{17,9},{25,1},{2,26},{10... | collective-permute-start | bytes 196616 | tf_op jit(solution)/shard_map/ppermute | solution.py:218
  5.0 14.2 %collective-permute-start.15 = (bf16[4,1,2,2,2,16,128]{6,5,4,3,2,1,0:T(8,128)(2,1)S(1)}, bf16[4,1,2,2,2,16,128]{6,5,4,3,2,1,0:T(8,128)(2,1)S(1)}, u32[]{:S(2)}, u32[]{:S(2)}) collective-permute-start(bf16[4,1,2,2,2,16,128]{6,5,4,3,2,1,0:T(8,128)(2,1)S(1)} %get-tuple-element.42), channel_id=1, source_target_pairs={{0,1},{1,0},{2,3},{3,2},{4,5},{5,4},{6,7},{7,6},{8,9},{9,8},{10,11... | collective-permute-start | bytes 393224 | tf_op jit(solution)/shard_map/ppermute | solution.py:221
  8.6 5.8 %collective-permute-start = (bf16[2,1,2,2,2,16,128]{6,5,4,3,2,1,0:T(8,128)(2,1)S(1)}, bf16[2,1,2,2,2,16,128]{6,5,4,3,2,1,0:T(8,128)(2,1)S(1)}, u32[]{:S(2)}, u32[]{:S(2)}) collective-permute-start(bf16[2,1,2,2,2,16,128]{6,5,4,3,2,1,0:T(8,128)(2,1)S(1)} %get-tuple-element.32), channel_id=1, source_target_pairs={{0,8},{8,0},{16,24},{24,16},{1,9},{9,1},{17,25},{25,17},{2,10},{10... | collective-permute-start | bytes 196616 | tf_op jit(solution)/shard_map/ppermute | solution.py:218
  9.6 4.8 %collective-permute-start.1 = (bf16[2,1,2,2,2,16,128]{6,5,4,3,2,1,0:T(8,128)(2,1)S(1)}, bf16[2,1,2,2,2,16,128]{6,5,4,3,2,1,0:T(8,128)(2,1)S(1)}, u32[]{:S(2)}, u32[]{:S(2)}) collective-permute-start(bf16[2,1,2,2,2,16,128]{6,5,4,3,2,1,0:T(8,128)(2,1)S(1)} %get-tuple-element.33), channel_id=1, source_target_pairs={{0,16},{8,24},{16,0},{24,8},{1,17},{9,25},{17,1},{25,9},{2,18},{10... | collective-permute-start | bytes 196616 | tf_op jit(solution)/shard_map/ppermute | solution.py:218
  11.2 5.1 %collective-permute-start.2 = (bf16[2,1,2,2,2,16,128]{6,5,4,3,2,1,0:T(8,128)(2,1)S(1)}, bf16[2,1,2,2,2,16,128]{6,5,4,3,2,1,0:T(8,128)(2,1)S(1)}, u32[]{:S(2)}, u32[]{:S(2)}) collective-permute-start(bf16[2,1,2,2,2,16,128]{6,5,4,3,2,1,0:T(8,128)(2,1)S(1)} %get-tuple-element.34), channel_id=1, source_target_pairs={{0,24},{8,16},{16,8},{24,0},{1,25},{9,17},{17,9},{25,1},{2,26},{10... | collective-permute-start | bytes 196616 | tf_op jit(solution)/shard_map/ppermute | solution.py:218
  11.6 13.0 %collective-permute-start.10 = (bf16[4,1,2,2,2,16,128]{6,5,4,3,2,1,0:T(8,128)(2,1)S(1)}, bf16[4,1,2,2,2,16,128]{6,5,4,3,2,1,0:T(8,128)(2,1)S(1)}, u32[]{:S(2)}, u32[]{:S(2)}) collective-permute-start(bf16[4,1,2,2,2,16,128]{6,5,4,3,2,1,0:T(8,128)(2,1)S(1)} %get-tuple-element.39), channel_id=1, source_target_pairs={{0,4},{1,5},{2,6},{3,7},{4,0},{5,1},{6,2},{7,3},{8,12},{9,13},{10,... | collective-permute-start | bytes 393224 | tf_op jit(solution)/shard_map/ppermute | solution.py:221
  14.3 18.3 %collective-permute-start.11 = (bf16[4,1,2,2,2,16,128]{6,5,4,3,2,1,0:T(8,128)(2,1)S(1)}, bf16[4,1,2,2,2,16,128]{6,5,4,3,2,1,0:T(8,128)(2,1)S(1)}, u32[]{:S(2)}, u32[]{:S(2)}) collective-permute-start(bf16[4,1,2,2,2,16,128]{6,5,4,3,2,1,0:T(8,128)(2,1)S(1)} %get-tuple-element.40), channel_id=1, source_target_pairs={{0,5},{1,4},{2,7},{3,6},{4,1},{5,0},{6,3},{7,2},{8,13},{9,12},{10,... | collective-permute-start | bytes 393224 | tf_op jit(solution)/shard_map/ppermute | solution.py:221
  14.5 26.2 %collective-permute-start.8 = (bf16[4,1,2,2,2,16,128]{6,5,4,3,2,1,0:T(8,128)(2,1)S(1)}, bf16[4,1,2,2,2,16,128]{6,5,4,3,2,1,0:T(8,128)(2,1)S(1)}, u32[]{:S(2)}, u32[]{:S(2)}) collective-permute-start(bf16[4,1,2,2,2,16,128]{6,5,4,3,2,1,0:T(8,128)(2,1)S(1)} %maximum_select_fusion), channel_id=1, source_target_pairs={{0,2},{1,3},{2,0},{3,1},{4,6},{5,7},{6,4},{7,5},{8,10},{9,11},{10,... | collective-permute-start | bytes 393224 | tf_op jit(solution)/shard_map/ppermute | solution.py:221
  16.4 18.2 %collective-permute-start.3 = (bf16[4,1,2,2,2,16,128]{6,5,4,3,2,1,0:T(8,128)(2,1)S(1)}, bf16[4,1,2,2,2,16,128]{6,5,4,3,2,1,0:T(8,128)(2,1)S(1)}, u32[]{:S(2)}, u32[]{:S(2)}) collective-permute-start(bf16[4,1,2,2,2,16,128]{6,5,4,3,2,1,0:T(8,128)(2,1)S(1)} %pad_maximum_fusion), channel_id=1, source_target_pairs={{0,6},{1,7},{2,4},{3,5},{4,2},{5,3},{6,0},{7,1},{8,14},{9,15},{10,... | collective-permute-start | bytes 393224 | tf_op jit(solution)/shard_map/ppermute | solution.py:221
  19.2 20.2 %collective-permute-start.4 = (bf16[4,1,2,2,2,16,128]{6,5,4,3,2,1,0:T(8,128)(2,1)S(1)}, bf16[4,1,2,2,2,16,128]{6,5,4,3,2,1,0:T(8,128)(2,1)S(1)}, u32[]{:S(2)}, u32[]{:S(2)}) collective-permute-start(bf16[4,1,2,2,2,16,128]{6,5,4,3,2,1,0:T(8,128)(2,1)S(1)} %pad_maximum_fusion.1), channel_id=1, source_target_pairs={{0,7},{1,6},{2,5},{3,4},{4,3},{5,2},{6,1},{7,0},{8,15},{9,14},{10,... | collective-permute-start | bytes 393224 | tf_op jit(solution)/shard_map/ppermute | solution.py:221
  24.5 10.2 %collective-permute-start.16 = (bf16[2,1,2,2,2,16,128]{6,5,4,3,2,1,0:T(8,128)(2,1)S(1)}, bf16[2,1,2,2,2,16,128]{6,5,4,3,2,1,0:T(8,128)(2,1)S(1)}, u32[]{:S(2)}, u32[]{:S(2)}) collective-permute-start(bf16[2,1,2,2,2,16,128]{6,5,4,3,2,1,0:T(8,128)(2,1)S(1)} %pad_maximum_fusion.5), channel_id=1, source_target_pairs={{0,8},{8,0},{16,24},{24,16},{1,9},{9,1},{17,25},{25,17},{2,10},{10... | collective-permute-start | bytes 196616 | tf_op jit(solution)/shard_map/ppermute | solution.py:218
  32.7 4.4 %collective-permute-start.17 = (bf16[2,1,2,2,2,16,128]{6,5,4,3,2,1,0:T(8,128)(2,1)S(1)}, bf16[2,1,2,2,2,16,128]{6,5,4,3,2,1,0:T(8,128)(2,1)S(1)}, u32[]{:S(2)}, u32[]{:S(2)}) collective-permute-start(bf16[2,1,2,2,2,16,128]{6,5,4,3,2,1,0:T(8,128)(2,1)S(1)} %pad_maximum_fusion.6), channel_id=1, source_target_pairs={{0,16},{8,24},{16,0},{24,8},{1,17},{9,25},{17,1},{25,9},{2,18},{10... | collective-permute-start | bytes 196616 | tf_op jit(solution)/shard_map/ppermute | solution.py:218
  34.6 3.8 %collective-permute-start.18 = (bf16[2,1,2,2,2,16,128]{6,5,4,3,2,1,0:T(8,128)(2,1)S(1)}, bf16[2,1,2,2,2,16,128]{6,5,4,3,2,1,0:T(8,128)(2,1)S(1)}, u32[]{:S(2)}, u32[]{:S(2)}) collective-permute-start(bf16[2,1,2,2,2,16,128]{6,5,4,3,2,1,0:T(8,128)(2,1)S(1)} %pad_maximum_fusion.7), channel_id=1, source_target_pairs={{0,24},{8,16},{16,8},{24,0},{1,25},{9,17},{17,9},{25,1},{2,26},{10... | collective-permute-start | bytes 196616 | tf_op jit(solution)/shard_map/ppermute | solution.py:218
  34.8 7.0 %collective-permute-start.9 = (bf16[4,1,2,2,2,16,128]{6,5,4,3,2,1,0:T(8,128)(2,1)S(1)}, bf16[4,1,2,2,2,16,128]{6,5,4,3,2,1,0:T(8,128)(2,1)S(1)}, u32[]{:S(2)}, u32[]{:S(2)}) collective-permute-start(bf16[4,1,2,2,2,16,128]{6,5,4,3,2,1,0:T(8,128)(2,1)S(1)} %maximum_select_fusion.1), channel_id=1, source_target_pairs={{0,3},{1,2},{2,1},{3,0},{4,7},{5,6},{6,5},{7,4},{8,11},{9,10},{10,... | collective-permute-start | bytes 393224 | tf_op jit(solution)/shard_map/ppermute | solution.py:221
  37.1 4.6 %collective-permute-start.12 = (bf16[2,1,2,2,2,16,128]{6,5,4,3,2,1,0:T(8,128)(2,1)S(1)}, bf16[2,1,2,2,2,16,128]{6,5,4,3,2,1,0:T(8,128)(2,1)S(1)}, u32[]{:S(2)}, u32[]{:S(2)}) collective-permute-start(bf16[2,1,2,2,2,16,128]{6,5,4,3,2,1,0:T(8,128)(2,1)S(1)} %pad_maximum_fusion.2), channel_id=1, source_target_pairs={{0,8},{8,0},{16,24},{24,16},{1,9},{9,1},{17,25},{25,17},{2,10},{10... | collective-permute-start | bytes 196616 | tf_op jit(solution)/shard_map/ppermute | solution.py:218
  38.4 4.5 %collective-permute-start.13 = (bf16[2,1,2,2,2,16,128]{6,5,4,3,2,1,0:T(8,128)(2,1)S(1)}, bf16[2,1,2,2,2,16,128]{6,5,4,3,2,1,0:T(8,128)(2,1)S(1)}, u32[]{:S(2)}, u32[]{:S(2)}) collective-permute-start(bf16[2,1,2,2,2,16,128]{6,5,4,3,2,1,0:T(8,128)(2,1)S(1)} %pad_maximum_fusion.3), channel_id=1, source_target_pairs={{0,16},{8,24},{16,0},{24,8},{1,17},{9,25},{17,1},{25,9},{2,18},{10... | collective-permute-start | bytes 196616 | tf_op jit(solution)/shard_map/ppermute | solution.py:218
  39.4 4.2 %collective-permute-start.14 = (bf16[2,1,2,2,2,16,128]{6,5,4,3,2,1,0:T(8,128)(2,1)S(1)}, bf16[2,1,2,2,2,16,128]{6,5,4,3,2,1,0:T(8,128)(2,1)S(1)}, u32[]{:S(2)}, u32[]{:S(2)}) collective-permute-start(bf16[2,1,2,2,2,16,128]{6,5,4,3,2,1,0:T(8,128)(2,1)S(1)} %pad_maximum_fusion.4), channel_id=1, source_target_pairs={{0,24},{8,16},{16,8},{24,0},{1,25},{9,17},{17,9},{25,1},{2,26},{10... | collective-permute-start | bytes 196616 | tf_op jit(solution)/shard_map/ppermute | solution.py:218
